TPU v7x, 128 devices: a whole 4x4x4 slice. The times are simulated.
128 devices in a mesh: bx: 4 (over z_hi, core), by: 8 (over z_lo, x), bz: 4 (over y).
Axes of the slice: x: 4, y: 4, z: 4 (z_hi: 2, z_lo: 2; z = z_hi * 2 + z_lo), core: 2. Of those that a mesh axis runs over, the one named last changes fastest.
Arguments:
- estimate: float32 [64, 128, 512], P('bx', 'by', 'bz'), may hold values from 0.2 to 5
- observed: float32 [8, 64, 128, 512], P(None, 'bx', 'by', 'bz'), may hold values from 0.3 to 180, as said below
- coverage: int32 [8, 4, 8, 4], P(None, 'bx', 'by', 'bz'), may hold values from 0 to 1, as said below
- psf_taps: float32 [8, 3, 17], replicated, may hold values from 0.05 to 1
Outputs:
- refined: float32 [64, 128, 512], P('bx', 'by', 'bz')
Inputs may be any that keep to these rules, and one draw needn't show every extreme that they name: `coverage`: each block is covered by 2 to 8 views; in every draw some block is covered by all 8. `observed`: positive.
All inputs are finite; a program needn't handle non-finite values.
Results may differ from a plain program's by a relative error of at most 0.0001.
Values sent between devices are 32-bit elements; how exact they have to be, the bound alone decides.
No kernel may reach another device: no remote copies, remote signals or barrier semaphores. Data moves between devices by JAX's collectives and lax.ppermute only.
A program may use at most 64 MiB of HBM per device.

v0:
```python
import jax
import jax.numpy as jnp
from jax import lax
from jax.experimental import pallas as pl
from jax.experimental.pallas import tpu as pltpu
from jax.sharding import PartitionSpec as P

ALL = ("bx", "by", "bz")
F32, BF16 = jnp.float32, jnp.bfloat16
V, R, K = 8, 8, 17
CX, CY, CZ = 16, 16, 128
EX, EY = CX + 2 * R, CY + 2 * R
ROWS = EX * EY
LANES = 128


def pairs(count, first):
    both = []
    for i in range(first, count - 1, 2):
        both += [(i, i + 1), (i + 1, i)]
    return both


def swap(one, two, axis):
    count = lax.axis_size(axis)
    return lax.ppermute(one, axis, pairs(count, 0)), lax.ppermute(two, axis, pairs(count, 1))


def kernel_call(body, out_shape, scratch=(), in_smem=0, flops=0, n_in=0):
    vmem = pl.BlockSpec(memory_space=pltpu.VMEM)
    smem = pl.BlockSpec(memory_space=pltpu.SMEM)
    return pl.pallas_call(
        body,
        out_shape=out_shape,
        in_specs=[smem] * in_smem + [vmem] * (n_in - in_smem),
        out_specs=jax.tree.map(lambda _: vmem, out_shape),
        scratch_shapes=list(scratch),
        compiler_params=pltpu.CompilerParams(vmem_limit_bytes=48 * 1024 * 1024),
        cost_estimate=pl.CostEstimate(flops=flops, bytes_accessed=1024, transcendentals=0),
    )


def shape(*dims, dtype=F32):
    return jax.ShapeDtypeStruct(dims, dtype)


def x_pack(flag, est, w, op1, op2):
    odd = flag[0] == 1
    for a in range(R):
        low, high = est[a], est[CX - R + a]
        op1[a * CY : (a + 1) * CY, :] = jnp.where(odd, low, high)
        op2[a * CY : (a + 1) * CY, :] = jnp.where(odd, high, low)
    op1[R * CY :, :] = w[...]
    op2[R * CY :, :] = w[...]


def y_pack(flag, est, w, x1, x2, field, ws, op1, op2):
    odd_x, odd_y = flag[0] == 1, flag[1] == 1
    one, two = x1[...], x2[...]
    below, above = jnp.where(odd_x, one, two), jnp.where(odd_x, two, one)
    cells = R * CY
    field[:R] = below[:cells].reshape(R, CY, LANES)
    field[R : R + CX] = est[...]
    field[R + CX :] = above[:cells].reshape(R, CY, LANES)
    ws[:V] = below[cells:]
    ws[V : 2 * V] = w[...]
    ws[2 * V :] = above[cells:]
    for i in range(EX):
        low, high = field[i, :R], field[i, CY - R :]
        op1[i * R : (i + 1) * R, :] = jnp.where(odd_y, low, high)
        op2[i * R : (i + 1) * R, :] = jnp.where(odd_y, high, low)
    op1[EX * R :, :] = ws[...]
    op2[EX * R :, :] = ws[...]


def z_pack(flag, fx, wx, y1, y2, field, ws, op1, op2):
    odd_y, odd_z = flag[1] == 1, flag[2] == 1
    one, two = y1[...], y2[...]
    below, above = jnp.where(odd_y, one, two), jnp.where(odd_y, two, one)
    cells = EX * R
    field[:, :R] = below[:cells].reshape(EX, R, LANES)
    field[:, R : R + CY] = fx[...]
    field[:, R + CY :] = above[:cells].reshape(EX, R, LANES)
    ws[: 3 * V] = below[cells:]
    ws[3 * V : 6 * V] = wx[...]
    ws[6 * V :] = above[cells:]
    turned = jnp.transpose(field[...].reshape(ROWS, LANES))
    low, high = turned[:R], turned[CZ - R :]
    op1[:, :ROWS] = jnp.where(odd_z, low, high)
    op2[:, :ROWS] = jnp.where(odd_z, high, low)
    for b in range(9):
        part = ws[b * V : (b + 1) * V]
        op1[:, ROWS + b * LANES : ROWS + (b + 1) * LANES] = part
        op2[:, ROWS + b * LANES : ROWS + (b + 1) * LANES] = part


def total_of(x):
    return jnp.sum(jnp.sum(x, axis=0, keepdims=True), axis=1, keepdims=True)


def split(x):
    high = x.astype(BF16)
    return high, (x - high.astype(F32)).astype(BF16)


def main_kernel(
    flag, taps, field, w9, z1, z2, observed, wz1, wz2, tz1, tz2,
    part, op1, op2, sums,
    ab, eb, hs, tx, rp, uy, ub, edge, edges, ws,
):
    odd_z = flag[2] == 1
    one, two = z1[...], z2[...]
    below, above = jnp.where(odd_z, one, two), jnp.where(odd_z, two, one)
    for b in range(9):
        ws[b * V : (b + 1) * V] = below[:, ROWS + b * LANES : ROWS + (b + 1) * LANES]
        ws[(18 + b) * V : (19 + b) * V] = above[:, ROWS + b * LANES : ROWS + (b + 1) * LANES]
    ws[9 * V : 18 * V] = w9[...]

    edges[:R] = below[:, :ROWS]
    edges[R:] = above[:, :ROWS]
    e = edges[...]
    e_high = e.astype(BF16).astype(F32)
    e_low = e - e_high
    stacked = jnp.concatenate([e_high, e_low, e_high, jnp.zeros((LANES - 6 * R, ROWS), F32)], axis=0)
    eb[...] = jnp.transpose(stacked).astype(BF16)

    for c in range(4):
        rows = slice(c * 256, (c + 1) * 256)
        high, low = split(field[c * 8 : (c + 1) * 8].reshape(256, LANES))
        ab[rows, :LANES] = high
        ab[rows, LANES:] = low
    for c in range(4):
        rows = slice(c * 256, (c + 1) * 256)
        first = ab[rows, :]
        second = jnp.concatenate([ab[rows, :LANES], eb[rows, :]], axis=1)
        for n in range(4):
            cols = slice(n * 256, (n + 1) * 256)
            got = jnp.dot(first, wz1[:, cols], preferred_element_type=F32)
            got += jnp.dot(second, wz2[:, cols], preferred_element_type=F32)
            hs[2 * n, c * 8 : (c + 1) * 8] = got[:, :LANES].reshape(8, EY, LANES)
            hs[2 * n + 1, c * 8 : (c + 1) * 8] = got[:, LANES:].reshape(8, EY, LANES)

    rp[...] = jnp.zeros_like(rp)
    part[...] = jnp.zeros_like(part)
    edge[...] = jnp.zeros_like(edge)
    lane = lax.broadcasted_iota(jnp.int32, (8, LANES), 1)

    def view_step(v, seen):
        t = [[taps[(v * 3 + d) * K + k] for k in range(K)] for d in range(2)]
        for y in range(EY // 8):
            rows = slice(y * 8, (y + 1) * 8)
            for a in range(CX):
                acc = t[0][0] * hs[v, a, rows]
                for k in range(1, K):
                    acc += t[0][k] * hs[v, a + k, rows]
                tx[a, rows] = acc
        own = ws[pl.ds(13 * V + v, 1), :]
        for a in range(CX):
            for b in range(CY // 8):
                acc = t[1][0] * tx[a, b * 8 : b * 8 + 8]
                for k in range(1, K):
                    acc += t[1][k] * tx[a, b * 8 + k : b * 8 + k + 8]
                seen_here = observed[v, a, b * 8 : b * 8 + 8]
                seen = seen + own * seen_here
                rp[a, 16 + b * 8 : 24 + b * 8] = seen_here / acc
        for a in range(CX):
            for m in range(EY // 8):
                acc = None
                for k in range(K):
                    start = 16 + 8 * m - k
                    if start + 8 <= 16 or start >= 32:
                        continue
                    term = t[1][k] * rp[a, start : start + 8]
                    acc = term if acc is None else acc + term
                uy[a, m * 8 : m * 8 + 8] = acc
        for y in range(EY // 16):
            rows = slice(y * 16, (y + 1) * 16)
            for i in range(EX):
                acc = None
                for a in range(max(0, i - K + 1), min(CX, i + 1)):
                    term = t[0][i - a] * uy[a, rows]
                    acc = term if acc is None else acc + term
                high, low = split(acc)
                ub[i * EY + y * 16 : i * EY + (y + 1) * 16, :LANES] = high
                ub[i * EY + y * 16 : i * EY + (y + 1) * 16, LANES:] = low
        for c in range(4):
            rows = slice(c * 256, (c + 1) * 256)
            got = jnp.dot(ub[rows, :], tz1[v], preferred_element_type=F32)
            got += jnp.dot(ub[rows, :LANES], tz2[v], preferred_element_type=F32)
            bx = (0, 1, 1, 2)[c]
            for j in range(3):
                ys = ((0, 8), (8, 24), (24, 32))[j]
                here = slice(ys[0], ys[1])
                at = j * 3 + bx
                w_mid = ws[pl.ds((9 + at) * V + v, 1), :]
                w_edge = jnp.where(
                    lane < R, ws[pl.ds(at * V + v, 1), :], ws[pl.ds((18 + at) * V + v, 1), :]
                )[:1]
                for i in range(8):
                    r0 = i * EY
                    part[c * 8 + i, here] += w_mid * got[r0 + ys[0] : r0 + ys[1], :LANES]
                    edge[c * 256 + r0 + ys[0] : c * 256 + r0 + ys[1], :] += (
                        w_edge * got[r0 + ys[0] : r0 + ys[1], LANES:]
                    )
        return seen

    seen = lax.fori_loop(0, V, view_step, jnp.zeros((8, LANES), F32))

    turned = jnp.transpose(edge[...])
    low, high = turned[:R], turned[R : 2 * R]
    op1[...] = jnp.where(odd_z, low, high)
    op2[...] = jnp.where(odd_z, high, low)

    def count_of(block):
        return jnp.maximum(
            jnp.sum(ws[block * V : (block + 1) * V], axis=0, keepdims=True), 1.0
        )

    total = jnp.zeros((8, LANES), F32)
    place = lax.broadcasted_iota(jnp.int32, (8, ROWS), 1)
    in_y = place % EY
    y_band = jnp.where(in_y < R, 0, jnp.where(in_y < R + CY, 1, 2))
    low_sum = edges[:R] * low
    high_sum = edges[R:] * high
    for bx in range(3):
        xs = ((0, 8), (8, 24), (24, 32))[bx]
        for j in range(3):
            ys = ((0, 8), (8, 24), (24, 32))[j]
            at = j * 3 + bx
            block = field[xs[0] : xs[1], ys[0] : ys[1]] * part[xs[0] : xs[1], ys[0] : ys[1]]
            block = block.reshape((-1, 8, LANES))
            total += jnp.sum(block, axis=0) / count_of(9 + at)
            lanes = slice(xs[0] * EY, xs[1] * EY)
            picked = y_band[:, lanes] == j
            for side, first in ((low_sum, 0), (high_sum, 18)):
                cut = jnp.where(picked, side[:, lanes], 0.0)
                folded = cut[:, :LANES]
                for q in range(1, cut.shape[1] // LANES):
                    folded = folded + cut[:, q * LANES : (q + 1) * LANES]
                total += folded / count_of(first + at)
    target = seen / count_of(13)
    both = jnp.where(lane < 64, total_of(target), total_of(total))
    for p in range(sums.shape[0]):
        sums[p] = both


def z_add(flag, part, r1, r2, mid, op1, op2):
    odd_y, odd_z = flag[1] == 1, flag[2] == 1
    one, two = r1[...], r2[...]
    below, above = jnp.where(odd_z, one, two), jnp.where(odd_z, two, one)
    stacked = jnp.concatenate([below, jnp.zeros((CZ - 2 * R, ROWS), F32), above], axis=0)
    added = jnp.transpose(stacked).reshape(EX, EY, LANES)
    for i in range(EX):
        plane = part[i] + added[i]
        mid[i] = plane[R : R + CY]
        low, high = plane[:R], plane[R + CY :]
        op1[i * R : (i + 1) * R, :] = jnp.where(odd_y, low, high)
        op2[i * R : (i + 1) * R, :] = jnp.where(odd_y, high, low)


def y_add(flag, part, r1, r2, mid, op1, op2):
    odd_x, odd_y = flag[0] == 1, flag[1] == 1
    for i in range(EX):
        one, two = r1[i * R : (i + 1) * R], r2[i * R : (i + 1) * R]
        first = part[i, :R] + jnp.where(odd_y, one, two)
        second = part[i, R:] + jnp.where(odd_y, two, one)
        if i < R:
            at = i
            rows = slice(at * CY, at * CY + R), slice(at * CY + R, (at + 1) * CY)
            op2[rows[0], :] = first
            op2[rows[1], :] = second
        elif i < R + CX:
            mid[i - R, :R] = first
            mid[i - R, R:] = second
        else:
            at = i - R - CX
            rows = slice(at * CY, at * CY + R), slice(at * CY + R, (at + 1) * CY)
            for row, new in zip(rows, (first, second)):
                low = op2[row, :]
                op1[row, :] = jnp.where(odd_x, low, new)
                op2[row, :] = jnp.where(odd_x, new, low)


def x_add(flag, part, r1, r2, est, count, sums, out):
    odd_x = flag[0] == 1
    gathered = jnp.sum(sums[...], axis=0)[:1]
    lane = lax.broadcasted_iota(jnp.int32, (1, LANES), 1)
    target = jnp.sum(jnp.where(lane == 0, gathered, 0.0), axis=1, keepdims=True)
    total = jnp.sum(jnp.where(lane == 64, gathered, 0.0), axis=1, keepdims=True)
    scale = target / total
    counts = jnp.sum(count[...], axis=0, keepdims=True)
    for a in range(CX):
        rows = slice((a % R) * CY, (a % R + 1) * CY)
        one, two = r1[rows, :], r2[rows, :]
        got = jnp.where(odd_x, one, two) if a < R else jnp.where(odd_x, two, one)
        out[a] = est[a] * ((part[a] + got) / counts) * scale


def z_bands(taps):
    near = jnp.arange(CZ + 2 * R)
    offset = near[:, None] - jnp.arange(CZ)[None, :]
    picked = offset[None, :, :, None] == jnp.arange(K)
    band = jnp.sum(jnp.where(picked, taps[:, None, None, :], 0.0), axis=3)
    high = lax.reduce_precision(band, 8, 7)
    low = band - high
    pad = jnp.zeros((V, LANES - 6 * R, CZ), F32)

    def faces(x):
        return jnp.concatenate([x[:, :R], x[:, R + CZ :]], axis=1)

    def middle(x):
        return x[:, R : R + CZ]

    wz1 = jnp.concatenate([middle(high), middle(high)], axis=1)
    wz2 = jnp.concatenate([middle(low), faces(high), faces(high), faces(low), pad], axis=1)

    def flat(x):
        return jnp.transpose(x, (1, 0, 2)).reshape(2 * LANES, V * CZ).astype(BF16)

    pad2 = jnp.zeros((V, LANES - 2 * R, CZ), F32)

    def turned(x):
        return jnp.transpose(jnp.concatenate([middle(x), faces(x), pad2], axis=1), (0, 2, 1))

    tz1 = jnp.concatenate([turned(high), turned(high)], axis=1).astype(BF16)
    tz2 = turned(low).astype(BF16)
    return flat(wz1), flat(wz2), tz1, tz2


def on_device(estimate, observed, coverage, psf_taps):
    taps = psf_taps / jnp.sum(psf_taps, axis=2, keepdims=True)
    flag = jnp.stack([lax.axis_index(axis) % 2 for axis in ALL]).astype(jnp.int32)
    w = jnp.broadcast_to(coverage.reshape(V, 1).astype(F32), (V, LANES))
    peers = lax.axis_size(ALL)

    op = shape((R * CY) + V, LANES)
    x1, x2 = kernel_call(x_pack, (op, op), n_in=3, in_smem=1)(flag, estimate, w)
    x1, x2 = swap(x1, x2, "bx")
    bands = z_bands(taps[:, 2])
    op = shape(EX * R + 3 * V, LANES)
    fx, wx, y1, y2 = kernel_call(
        y_pack, (shape(EX, CY, LANES), shape(3 * V, LANES), op, op), n_in=5, in_smem=1
    )(flag, estimate, w, x1, x2)
    y1, y2 = swap(y1, y2, "by")
    op = shape(R, ROWS + 9 * LANES)
    field, w9, z1, z2 = kernel_call(
        z_pack, (shape(EX, EY, LANES), shape(9 * V, LANES), op, op), n_in=5, in_smem=1
    )(flag, fx, wx, y1, y2)
    z1, z2 = swap(z1, z2, "bz")

    face = shape(R, ROWS)
    part, z1, z2, sums = kernel_call(
        main_kernel,
        (shape(EX, EY, LANES), face, face, shape(peers, 8, LANES)),
        scratch=(
            pltpu.VMEM((ROWS, 2 * LANES), BF16),
            pltpu.VMEM((ROWS, LANES), BF16),
            pltpu.VMEM((V, EX, EY, LANES), F32),
            pltpu.VMEM((CX, EY, LANES), F32),
            pltpu.VMEM((CX, 48, LANES), F32),
            pltpu.VMEM((CX, EY, LANES), F32),
            pltpu.VMEM((ROWS, 2 * LANES), BF16),
            pltpu.VMEM((ROWS, LANES), F32),
            pltpu.VMEM((2 * R, ROWS), F32),
            pltpu.VMEM((27 * V, LANES), F32),
        ),
        n_in=11,
        in_smem=2,
        flops=2 * 10**9,
    )(flag, taps.reshape(-1), field, w9, z1, z2, observed, *bands)

    sums = lax.all_to_all(sums, ALL, 0, 0)
    z1, z2 = swap(z1, z2, "bz")
    op = shape(EX * R, LANES)
    part, y1, y2 = kernel_call(z_add, (shape(EX, CY, LANES), op, op), n_in=4, in_smem=1)(
        flag, part, z1, z2
    )
    y1, y2 = swap(y1, y2, "by")
    op = shape(R * CY, LANES)
    part, x1, x2 = kernel_call(y_add, (shape(CX, CY, LANES), op, op), n_in=4, in_smem=1)(
        flag, part, y1, y2
    )
    x1, x2 = swap(x1, x2, "bx")
    return kernel_call(x_add, shape(CX, CY, LANES), n_in=7, in_smem=1)(
        flag, part, x1, x2, estimate, w, sums
    )


def solution(mesh):
    spec = P("bx", "by", "bz")
    views_spec = P(None, "bx", "by", "bz")
    return jax.shard_map(
        on_device,
        mesh=mesh,
        in_specs=(spec, views_spec, views_spec, P()),
        out_specs=spec,
        check_vma=False,
    )
```

profile of v0, /device:TPU:41, one launch (start us, length us, event | category | flops | bytes accessed | tf_op | source)
XLA Modules:
  0.0 86.3 jit_solution(8529446931248892040)
XLA Ops:
  0.0 0.7 convert_bitcast_fusion
  0.7 0.1 pad_add_fusion.flag
  0.7 0.1 broadcast_in_dim.40.w.count
  0.8 0.0 copy-start
  0.8 0.9 %copy-done = f32[16,16,128]{2,1,0:T(8,128)S(1)} copy-done((f32[16,16,128]{2,1,0:T(8,128)S(1)}, f32[16,16,128]{2,1,0:T(8,128)}, u32[]{:S(2)}) %copy-start) | copy-done | bytes 131096
  1.7 0.6 shard_map.46
  2.3 0.8 collective-permute-start
  3.0 4.5 %collective-permute-start.1 = (f32[136,128]{1,0:T(8,128)S(1)}, f32[136,128]{1,0:T(8,128)S(1)}, u32[]{:S(2)}, u32[]{:S(2)}) collective-permute-start(f32[136,128]{1,0:T(8,128)S(1)} %get-tuple-element.26), channel_id=1, source_target_pairs={{32,64},{64,32},{33,65},{65,33},{34,66},{66,34},{35,67},{67,35},{3... | collective-permute-start | bytes 208904 | tf_op jit(solution)/shard_map/ppermute | solution.py:26
  7.5 0.8 reduce_sum.18
  8.3 0.8 broadcast_divide_fusion
  9.1 0.2 iota_compare_fusion
  9.3 1.6 %select_reduce_fusion = f32[8,144,128]{2,1,0:T(8,128)S(1)} fusion(f32[8,17]{1,0:T(8,128)S(1)} %slice_bitcast_fusion, pred[144,128,17]{1,0,2:T(8,128)(4,1)S(1)} %iota_compare_fusion), kind=kLoop, calls=%fused_computation | loop fusion | flops 4866048 | bytes 903712 | tf_op jit(solution)/shard_map/reduce_sum | solution.py:303
  10.9 0.3 copy.11
  11.2 0.2 reduce-precision_subtract_fusion
  11.4 0.1 slice.56
  11.6 0.1 slice.68
  11.7 0.3 fusion.2
  12.0 0.1 pad.9.clone
  12.1 0.1 pad.3.clone
  12.1 0.1 reshape.38.taps
  12.2 0.2 maximum_bitcast_fusion.tz2
  12.5 3.5 %concatenate.21 = bf16[8,256,128]{1,2,0:T(8,128)(2,1)S(1)} concatenate(bf16[8,128,128]{1,2,0:T(8,128)(2,1)S(1)} %slice.56, bf16[8,8,128]{1,2,0:T(8,128)(2,1)S(1)} %get-tuple-element.49, bf16[8,8,128]{1,2,0:T(8,128)(2,1)S(1)} %get-tuple-element.51, bf16[8,8,128]{1,2,0:T(8,128)(2,1)S(1)} %get-tuple-element.49, bf16[8,8,128]{1,2,0:T(8,128)(2,1)S(1)} %get-tuple-element.51, ...), dimensions={1} | concatenate | bytes 1048576 | tf_op jit(solution)/shard_map/concatenate | solution.py:315
  16.0 0.2 copy.14.wz2
  16.2 0.0 copy-start.1
  16.3 0.2 copy.13.wz1
  16.5 0.0 collective-permute-done.x1
  16.5 0.0 collective-permute-done.1.x2
  16.5 0.6 copy-done.1
  17.2 0.6 shard_map.47
  17.7 1.3 %collective-permute-start.2 = (f32[280,128]{1,0:T(8,128)S(1)}, f32[280,128]{1,0:T(8,128)S(1)}, u32[]{:S(2)}, u32[]{:S(2)}) collective-permute-start(f32[280,128]{1,0:T(8,128)S(1)} %get-tuple-element.29), channel_id=1, source_target_pairs={{0,4},{4,0},{8,12},{12,8},{16,20},{20,16},{24,28},{28,24},{1,5},{5... | collective-permute-start | bytes 430088 | tf_op jit(solution)/shard_map/ppermute | solution.py:26
  19.0 4.2 %collective-permute-start.3 = (f32[280,128]{1,0:T(8,128)S(1)}, f32[280,128]{1,0:T(8,128)S(1)}, u32[]{:S(2)}, u32[]{:S(2)}) collective-permute-start(f32[280,128]{1,0:T(8,128)S(1)} %get-tuple-element.30), channel_id=1, source_target_pairs={{4,8},{8,4},{12,16},{16,12},{20,24},{24,20},{5,9},{9,5},{13,17},{1... | collective-permute-start | bytes 430088 | tf_op jit(solution)/shard_map/ppermute | solution.py:26
  23.2 0.2 fusion
  23.4 0.0 collective-permute-done.2.y1
  23.4 3.6 %collective-permute-done.3.y2 = f32[280,128]{1,0:T(8,128)S(1)} collective-permute-done((f32[280,128]{1,0:T(8,128)S(1)}, f32[280,128]{1,0:T(8,128)S(1)}, u32[]{:S(2)}, u32[]{:S(2)}) %collective-permute-start.3) | collective-permute-done | bytes 143392 | tf_op jit(solution)/shard_map/ppermute | solution.py:26
  27.0 0.0 copy-start.2
  27.0 0.7 shard_map.48
  27.7 0.2 collective-permute-start.4
  28.0 4.0 %collective-permute-start.5 = (f32[8,2176]{1,0:T(8,128)S(1)}, f32[8,2176]{1,0:T(8,128)S(1)}, u32[]{:S(2)}, u32[]{:S(2)}) collective-permute-start(f32[8,2176]{1,0:T(8,128)S(1)} %get-tuple-element.34), channel_id=1, source_target_pairs={{1,2},{2,1},{5,6},{6,5},{9,10},{10,9},{13,14},{14,13},{17,18},{18,... | collective-permute-start | bytes 208904 | tf_op jit(solution)/shard_map/ppermute | solution.py:26
  32.0 0.1 pad_maximum_fusion.tz1
  32.1 0.0 collective-permute-done.4.z1
  32.1 1.6 %collective-permute-done.5.z2 = f32[8,2176]{1,0:T(8,128)S(1)} collective-permute-done((f32[8,2176]{1,0:T(8,128)S(1)}, f32[8,2176]{1,0:T(8,128)S(1)}, u32[]{:S(2)}, u32[]{:S(2)}) %collective-permute-start.5) | collective-permute-done | bytes 69664 | tf_op jit(solution)/shard_map/ppermute | solution.py:26
  33.7 0.0 copy-done.2
  33.7 14.2 %shard_map.49 = (f32[32,32,128]{2,1,0:T(8,128)S(1)}, f32[8,1024]{1,0:T(8,128)S(1)}, f32[8,1024]{1,0:T(8,128)S(1)}, f32[128,8,128]{2,1,0:T(8,128)}) custom-call(s32[3]{0:T(128)S(1)} %pad_add_fusion.flag, f32[408]{0:T(512)S(1)} %reshape.38.taps, f32[32,32,128]{2,1,0:T(8,128)S(1)} %get-tuple-element.31.field, f32[72,128]{1,0:T(8,128)S(1)} %get-tuple-element.32.w9, ...), custom_call_target="tpu_custom_call" | custom-call | flops 2000000000 | bytes 1024 | tf_op jit(solution)/shard_map/pallas_call | solution.py:352
  47.9 9.2 %all-to-all-start = ((f32[128,8,128]{2,1,0:T(8,128)}), f32[128,8,128]{2,1,0:T(8,128)S(1)}, u32[]{:S(2)}, u32[]{:S(2)}) async-start(f32[128,8,128]{2,1,0:T(8,128)} %get-tuple-element.44), calls=%async_computation | async-start | bytes 1048576 | tf_op jit(solution)/shard_map/all_to_all | solution.py:372
  57.1 0.3 collective-permute-start.6
  57.4 3.9 %collective-permute-start.7 = (f32[8,1024]{1,0:T(8,128)S(1)}, f32[8,1024]{1,0:T(8,128)S(1)}, u32[]{:S(2)}, u32[]{:S(2)}) collective-permute-start(f32[8,1024]{1,0:T(8,128)S(1)} %get-tuple-element.37), channel_id=1, source_target_pairs={{1,2},{2,1},{5,6},{6,5},{9,10},{10,9},{13,14},{14,13},{17,18},{18,... | collective-permute-start | bytes 98312 | tf_op jit(solution)/shard_map/ppermute | solution.py:26
  61.3 0.0 collective-permute-done.6.r1
  61.3 3.5 %collective-permute-done.7.r2 = f32[8,1024]{1,0:T(8,128)S(1)} collective-permute-done((f32[8,1024]{1,0:T(8,128)S(1)}, f32[8,1024]{1,0:T(8,128)S(1)}, u32[]{:S(2)}, u32[]{:S(2)}) %collective-permute-start.7) | collective-permute-done | bytes 32800 | tf_op jit(solution)/shard_map/ppermute | solution.py:26
  64.8 0.7 shard_map.50
  65.5 1.8 %collective-permute-start.8 = (f32[256,128]{1,0:T(8,128)S(1)}, f32[256,128]{1,0:T(8,128)S(1)}, u32[]{:S(2)}, u32[]{:S(2)}) collective-permute-start(f32[256,128]{1,0:T(8,128)S(1)} %get-tuple-element.39), channel_id=1, source_target_pairs={{0,4},{4,0},{8,12},{12,8},{16,20},{20,16},{24,28},{28,24},{1,5},{5... | collective-permute-start | bytes 393224 | tf_op jit(solution)/shard_map/ppermute | solution.py:26
  67.3 3.5 %collective-permute-start.9 = (f32[256,128]{1,0:T(8,128)S(1)}, f32[256,128]{1,0:T(8,128)S(1)}, u32[]{:S(2)}, u32[]{:S(2)}) collective-permute-start(f32[256,128]{1,0:T(8,128)S(1)} %get-tuple-element.40), channel_id=1, source_target_pairs={{4,8},{8,4},{12,16},{16,12},{20,24},{24,20},{5,9},{9,5},{13,17},{1... | collective-permute-start | bytes 393224 | tf_op jit(solution)/shard_map/ppermute | solution.py:26
  70.8 0.0 collective-permute-done.8.r1
  70.8 4.8 %collective-permute-done.9.r2 = f32[256,128]{1,0:T(8,128)S(1)} collective-permute-done((f32[256,128]{1,0:T(8,128)S(1)}, f32[256,128]{1,0:T(8,128)S(1)}, u32[]{:S(2)}, u32[]{:S(2)}) %collective-permute-start.9) | collective-permute-done | bytes 131104 | tf_op jit(solution)/shard_map/ppermute | solution.py:26
  75.6 0.6 shard_map.51
  76.1 1.7 %collective-permute-start.10 = (f32[128,128]{1,0:T(8,128)S(1)}, f32[128,128]{1,0:T(8,128)S(1)}, u32[]{:S(2)}, u32[]{:S(2)}) collective-permute-start(f32[128,128]{1,0:T(8,128)S(1)} %get-tuple-element.42), channel_id=1, source_target_pairs={{0,32},{32,0},{64,96},{96,64},{1,33},{33,1},{65,97},{97,65},{2,34}... | collective-permute-start | bytes 196616 | tf_op jit(solution)/shard_map/ppermute | solution.py:26
  77.8 4.2 %collective-permute-start.11 = (f32[128,128]{1,0:T(8,128)S(1)}, f32[128,128]{1,0:T(8,128)S(1)}, u32[]{:S(2)}, u32[]{:S(2)}) collective-permute-start(f32[128,128]{1,0:T(8,128)S(1)} %get-tuple-element.43), channel_id=1, source_target_pairs={{32,64},{64,32},{33,65},{65,33},{34,66},{66,34},{35,67},{67,35},{3... | collective-permute-start | bytes 196616 | tf_op jit(solution)/shard_map/ppermute | solution.py:26
  82.0 0.0 collective-permute-done.10.r1
  82.0 2.9 %collective-permute-done.11.r2 = f32[128,128]{1,0:T(8,128)S(1)} collective-permute-done((f32[128,128]{1,0:T(8,128)S(1)}, f32[128,128]{1,0:T(8,128)S(1)}, u32[]{:S(2)}, u32[]{:S(2)}) %collective-permute-start.11) | collective-permute-done | bytes 65568 | tf_op jit(solution)/shard_map/ppermute | solution.py:26
  84.9 0.0 all-to-all-done.sums
  84.9 1.4 %shard_map.52 = f32[16,16,128]{2,1,0:T(8,128)} custom-call(s32[3]{0:T(128)S(1)} %pad_add_fusion.flag, f32[16,16,128]{2,1,0:T(8,128)S(1)} %get-tuple-element.41.part, f32[128,128]{1,0:T(8,128)S(1)} %collective-permute-done.10.r1, f32[128,128]{1,0:T(8,128)S(1)} %collective-permute-done.11.r2, f32[16,16,128]{2,1,0:T(8,128)S(1)} %copy-done.1, ...), custom_call_target="tpu_custom_call" | custom-call | bytes 1024 | tf_op jit(solution)/shard_map/pallas_call | solution.py:384
  (7 shorter events, 0.1 us)
Async XLA Ops:
  0.8 0.9 %copy-start = (f32[16,16,128]{2,1,0:T(8,128)S(1)}, f32[16,16,128]{2,1,0:T(8,128)}, u32[]{:S(2)}) copy-start(f32[16,16,128]{2,1,0:T(8,128)} %est.5) | copy-start | bytes 393220
  2.3 14.2 %collective-permute-start = (f32[136,128]{1,0:T(8,128)S(1)}, f32[136,128]{1,0:T(8,128)S(1)}, u32[]{:S(2)}, u32[]{:S(2)}) collective-permute-start(f32[136,128]{1,0:T(8,128)S(1)} %get-tuple-element.25), channel_id=1, source_target_pairs={{0,32},{32,0},{64,96},{96,64},{1,33},{33,1},{65,97},{97,65},{2,34}... | collective-permute-start | bytes 208904 | tf_op jit(solution)/shard_map/ppermute | solution.py:26
  3.0 13.5 %collective-permute-start.1 = (f32[136,128]{1,0:T(8,128)S(1)}, f32[136,128]{1,0:T(8,128)S(1)}, u32[]{:S(2)}, u32[]{:S(2)}) collective-permute-start(f32[136,128]{1,0:T(8,128)S(1)} %get-tuple-element.26), channel_id=1, source_target_pairs={{32,64},{64,32},{33,65},{65,33},{34,66},{66,34},{35,67},{67,35},{3... | collective-permute-start | bytes 208904 | tf_op jit(solution)/shard_map/ppermute | solution.py:26
  16.2 0.9 %copy-start.1 = (f32[16,16,128]{2,1,0:T(8,128)S(1)}, f32[16,16,128]{2,1,0:T(8,128)}, u32[]{:S(2)}) copy-start(f32[16,16,128]{2,1,0:T(8,128)} %est.5) | copy-start | bytes 393220
  17.7 5.7 %collective-permute-start.2 = (f32[280,128]{1,0:T(8,128)S(1)}, f32[280,128]{1,0:T(8,128)S(1)}, u32[]{:S(2)}, u32[]{:S(2)}) collective-permute-start(f32[280,128]{1,0:T(8,128)S(1)} %get-tuple-element.29), channel_id=1, source_target_pairs={{0,4},{4,0},{8,12},{12,8},{16,20},{20,16},{24,28},{28,24},{1,5},{5... | collective-permute-start | bytes 430088 | tf_op jit(solution)/shard_map/ppermute | solution.py:26
  19.0 7.9 %collective-permute-start.3 = (f32[280,128]{1,0:T(8,128)S(1)}, f32[280,128]{1,0:T(8,128)S(1)}, u32[]{:S(2)}, u32[]{:S(2)}) collective-permute-start(f32[280,128]{1,0:T(8,128)S(1)} %get-tuple-element.30), channel_id=1, source_target_pairs={{4,8},{8,4},{12,16},{16,12},{20,24},{24,20},{5,9},{9,5},{13,17},{1... | collective-permute-start | bytes 430088 | tf_op jit(solution)/shard_map/ppermute | solution.py:26
  27.0 6.7 %copy-start.2 = (f32[8,16,16,128]{3,2,1,0:T(8,128)S(1)}, f32[8,16,16,128]{3,2,1,0:T(8,128)}, u32[]{:S(2)}) copy-start(f32[8,16,16,128]{3,2,1,0:T(8,128)} %observed.1) | copy-start | bytes 3145732
  27.7 4.4 %collective-permute-start.4 = (f32[8,2176]{1,0:T(8,128)S(1)}, f32[8,2176]{1,0:T(8,128)S(1)}, u32[]{:S(2)}, u32[]{:S(2)}) collective-permute-start(f32[8,2176]{1,0:T(8,128)S(1)} %get-tuple-element.33), channel_id=1, source_target_pairs={{0,1},{1,0},{2,3},{3,2},{4,5},{5,4},{6,7},{7,6},{8,9},{9,8},{10,11... | collective-permute-start | bytes 208904 | tf_op jit(solution)/shard_map/ppermute | solution.py:26
  28.0 5.7 %collective-permute-start.5 = (f32[8,2176]{1,0:T(8,128)S(1)}, f32[8,2176]{1,0:T(8,128)S(1)}, u32[]{:S(2)}, u32[]{:S(2)}) collective-permute-start(f32[8,2176]{1,0:T(8,128)S(1)} %get-tuple-element.34), channel_id=1, source_target_pairs={{1,2},{2,1},{5,6},{6,5},{9,10},{10,9},{13,14},{14,13},{17,18},{18,... | collective-permute-start | bytes 208904 | tf_op jit(solution)/shard_map/ppermute | solution.py:26
  47.9 37.0 %all-to-all-start = ((f32[128,8,128]{2,1,0:T(8,128)}), f32[128,8,128]{2,1,0:T(8,128)S(1)}, u32[]{:S(2)}, u32[]{:S(2)}) async-start(f32[128,8,128]{2,1,0:T(8,128)} %get-tuple-element.44), calls=%async_computation | async-start | bytes 1048576 | tf_op jit(solution)/shard_map/all_to_all | solution.py:372
  57.1 4.2 %collective-permute-start.6 = (f32[8,1024]{1,0:T(8,128)S(1)}, f32[8,1024]{1,0:T(8,128)S(1)}, u32[]{:S(2)}, u32[]{:S(2)}) collective-permute-start(f32[8,1024]{1,0:T(8,128)S(1)} %get-tuple-element.36), channel_id=1, source_target_pairs={{0,1},{1,0},{2,3},{3,2},{4,5},{5,4},{6,7},{7,6},{8,9},{9,8},{10,11... | collective-permute-start | bytes 98312 | tf_op jit(solution)/shard_map/ppermute | solution.py:26
  57.4 7.4 %collective-permute-start.7 = (f32[8,1024]{1,0:T(8,128)S(1)}, f32[8,1024]{1,0:T(8,128)S(1)}, u32[]{:S(2)}, u32[]{:S(2)}) collective-permute-start(f32[8,1024]{1,0:T(8,128)S(1)} %get-tuple-element.37), channel_id=1, source_target_pairs={{1,2},{2,1},{5,6},{6,5},{9,10},{10,9},{13,14},{14,13},{17,18},{18,... | collective-permute-start | bytes 98312 | tf_op jit(solution)/shard_map/ppermute | solution.py:26
  65.5 5.3 %collective-permute-start.8 = (f32[256,128]{1,0:T(8,128)S(1)}, f32[256,128]{1,0:T(8,128)S(1)}, u32[]{:S(2)}, u32[]{:S(2)}) collective-permute-start(f32[256,128]{1,0:T(8,128)S(1)} %get-tuple-element.39), channel_id=1, source_target_pairs={{0,4},{4,0},{8,12},{12,8},{16,20},{20,16},{24,28},{28,24},{1,5},{5... | collective-permute-start | bytes 393224 | tf_op jit(solution)/shard_map/ppermute | solution.py:26
  67.3 8.3 %collective-permute-start.9 = (f32[256,128]{1,0:T(8,128)S(1)}, f32[256,128]{1,0:T(8,128)S(1)}, u32[]{:S(2)}, u32[]{:S(2)}) collective-permute-start(f32[256,128]{1,0:T(8,128)S(1)} %get-tuple-element.40), channel_id=1, source_target_pairs={{4,8},{8,4},{12,16},{16,12},{20,24},{24,20},{5,9},{9,5},{13,17},{1... | collective-permute-start | bytes 393224 | tf_op jit(solution)/shard_map/ppermute | solution.py:26
  76.1 5.9 %collective-permute-start.10 = (f32[128,128]{1,0:T(8,128)S(1)}, f32[128,128]{1,0:T(8,128)S(1)}, u32[]{:S(2)}, u32[]{:S(2)}) collective-permute-start(f32[128,128]{1,0:T(8,128)S(1)} %get-tuple-element.42), channel_id=1, source_target_pairs={{0,32},{32,0},{64,96},{96,64},{1,33},{33,1},{65,97},{97,65},{2,34}... | collective-permute-start | bytes 196616 | tf_op jit(solution)/shard_map/ppermute | solution.py:26
  77.8 7.1 %collective-permute-start.11 = (f32[128,128]{1,0:T(8,128)S(1)}, f32[128,128]{1,0:T(8,128)S(1)}, u32[]{:S(2)}, u32[]{:S(2)}) collective-permute-start(f32[128,128]{1,0:T(8,128)S(1)} %get-tuple-element.43), channel_id=1, source_target_pairs={{32,64},{64,32},{33,65},{65,33},{34,66},{66,34},{35,67},{67,35},{3... | collective-permute-start | bytes 196616 | tf_op jit(solution)/shard_map/ppermute | solution.py:26
where the time goes:
time: 86.8 us; the launch traced here: 86.3 us
  starting transfers between devices  39.5 us (46%)
  Pallas kernels  18.9 us (22%)
  waiting for transfers between devices  16.2 us (19%)
  local copies, waits for them, and re-layouts  6.71 us (8%)
  other arithmetic  4.77 us (5%)
    ppermute x6, starting transfers between devices, swap(): lax.ppermute(two, axis, pairs(count, 1))  24.3 us
    ppermute x6, waiting for transfers between devices, swap(): lax.ppermute(two, axis, pairs(count, 1))  16.2 us
    pallas_call x1, Pallas kernels, on_device(): kernel_call(main_kernel, (shape(EX, EY, LANES), face, face, shape(peers,...  14.2 us
    all_to_all x1, starting transfers between devices, on_device(): sums = lax.all_to_all(sums, ALL, 0, 0)  9.15 us
    ppermute x6, starting transfers between devices, swap(): lax.ppermute(one, axis, pairs(count, 0))  6.04 us
    concatenate x1, local copies, waits for them, and re-layouts, z_bands(): jnp.concatenate([middle(low), faces(high), faces(high), faces(low), pad],...  3.52 us
  transfers between devices with their start and end apart: 13, of which 5 were waited for; matrix products, arithmetic and copies ran while one was open for 11% of the time, Pallas kernels for 2%

commit v1 on v0

v1 whole, which is shorter than its diff:
```python
import jax
import jax.numpy as jnp
from jax import lax
from jax.experimental import pallas as pl
from jax.experimental.pallas import tpu as pltpu
from jax.sharding import PartitionSpec as P

ALL = ("bx", "by", "bz")
F32, BF16 = jnp.float32, jnp.bfloat16
V, R, K = 8, 8, 17
CX, CY, CZ = 16, 16, 128
EX, EY = CX + 2 * R, CY + 2 * R
ROWS = EX * EY
LANES = 128


def pairs(count, first):
    both = []
    for i in range(first, count - 1, 2):
        both += [(i, i + 1), (i + 1, i)]
    return both


def swap(one, two, axis):
    count = lax.axis_size(axis)
    return lax.ppermute(one, axis, pairs(count, 0)), lax.ppermute(two, axis, pairs(count, 1))


def kernel_call(body, out_shape, scratch=(), in_smem=0, flops=0, n_in=0):
    vmem = pl.BlockSpec(memory_space=pltpu.VMEM)
    smem = pl.BlockSpec(memory_space=pltpu.SMEM)
    return pl.pallas_call(
        body,
        out_shape=out_shape,
        in_specs=[smem] * in_smem + [vmem] * (n_in - in_smem),
        out_specs=jax.tree.map(lambda _: vmem, out_shape),
        scratch_shapes=list(scratch),
        compiler_params=pltpu.CompilerParams(vmem_limit_bytes=48 * 1024 * 1024),
        cost_estimate=pl.CostEstimate(flops=flops, bytes_accessed=1024, transcendentals=0),
    )


def shape(*dims, dtype=F32):
    return jax.ShapeDtypeStruct(dims, dtype)


def x_pack(flag, est, w, op1, op2):
    odd = flag[0] == 1
    for a in range(R):
        low, high = est[a], est[CX - R + a]
        op1[a * CY : (a + 1) * CY, :] = jnp.where(odd, low, high)
        op2[a * CY : (a + 1) * CY, :] = jnp.where(odd, high, low)
    op1[R * CY :, :] = w[...]
    op2[R * CY :, :] = w[...]


def y_pack(flag, est, w, x1, x2, field, ws, op1, op2):
    odd_x, odd_y = flag[0] == 1, flag[1] == 1
    one, two = x1[...], x2[...]
    below, above = jnp.where(odd_x, one, two), jnp.where(odd_x, two, one)
    cells = R * CY
    field[:R] = below[:cells].reshape(R, CY, LANES)
    field[R : R + CX] = est[...]
    field[R + CX :] = above[:cells].reshape(R, CY, LANES)
    ws[...] = w[...]
    ws[:1] = below[cells : cells + 1]
    ws[1:2] = w[:1]
    ws[2:3] = above[cells : cells + 1]
    for i in range(EX):
        low, high = field[i, :R], field[i, CY - R :]
        op1[i * R : (i + 1) * R, :] = jnp.where(odd_y, low, high)
        op2[i * R : (i + 1) * R, :] = jnp.where(odd_y, high, low)
    op1[EX * R :, :] = ws[...]
    op2[EX * R :, :] = ws[...]


def z_pack(flag, fx, wx, y1, y2, field, ws, op1, op2):
    odd_y, odd_z = flag[1] == 1, flag[2] == 1
    one, two = y1[...], y2[...]
    below, above = jnp.where(odd_y, one, two), jnp.where(odd_y, two, one)
    cells = EX * R
    field[:, :R] = below[:cells].reshape(EX, R, LANES)
    field[:, R : R + CY] = fx[...]
    field[:, R + CY :] = above[:cells].reshape(EX, R, LANES)
    ws[...] = jnp.zeros_like(ws)
    ws[:3] = below[cells : cells + 3]
    ws[3:6] = wx[:3]
    ws[6:9] = above[cells : cells + 3]
    turned = jnp.transpose(field[...].reshape(ROWS, LANES))
    low, high = turned[:R], turned[CZ - R :]
    op1[:, :ROWS] = jnp.where(odd_z, low, high)
    op2[:, :ROWS] = jnp.where(odd_z, high, low)
    for b in range(2):
        cols = slice(ROWS + b * LANES, ROWS + (b + 1) * LANES)
        op1[:, cols] = ws[b * 8 : b * 8 + 8]
        op2[:, cols] = ws[b * 8 : b * 8 + 8]


def total_of(x):
    return jnp.sum(jnp.sum(x, axis=0, keepdims=True), axis=1, keepdims=True)


def split(x):
    high = x.astype(BF16)
    return high, (x - high.astype(F32)).astype(BF16)


def iota(dims, axis):
    return lax.broadcasted_iota(jnp.int32, dims, axis)


def pick(taps, base, offset):
    got = jnp.zeros(offset.shape, F32)
    for k in range(K):
        got = jnp.where(offset == k, taps[base + k], got)
    return got


def bands(taps, by, byt, wz1, wz2, tz1, tz2):
    for v in range(V):
        base = (v * 3 + 1) * K
        rows = slice(v * CY, (v + 1) * CY)
        column = iota((CY, LANES), 1)
        got = pick(taps, base, column % EY - iota((CY, LANES), 0))
        high, low = split(got)
        by[rows, :] = jnp.where(column < 2 * EY, high.astype(F32), low.astype(F32)).astype(BF16)

    def turned_y(v, got):
        lane = iota((EY, LANES), 1)
        here = pick(taps, (v * 3 + 1) * K, iota((EY, LANES), 0) - lane % CY)
        return jnp.where(lane // CY == v, here, got)

    both = lax.fori_loop(0, V, turned_y, jnp.zeros((EY, LANES), F32))
    high, low = split(both)
    byt[:EY, :] = high.astype(F32)
    byt[EY:, :] = low.astype(F32)

    def z_of(v, carry):
        base = (v * 3 + 2) * K
        row, col = iota((LANES, LANES), 0), iota((LANES, LANES), 1)
        high, low = split(pick(taps, base, row + R - col))
        wz1[v, :LANES, :] = high
        wz1[v, LANES:, :] = high
        wz2[v, :LANES, :] = low
        place = row[: 6 * R] % (2 * R)
        near = jnp.where(place < R, place, place + CZ)
        got = pick(taps, base, near - col[: 6 * R])
        high, low = split(got)
        which = row[: 6 * R] < 4 * R
        wz2[v, LANES : LANES + 6 * R, :] = jnp.where(
            which, high.astype(F32), low.astype(F32)
        ).astype(BF16)
        wz2[v, LANES + 6 * R :, :] = jnp.zeros((LANES - 6 * R, LANES), BF16)
        high, low = split(pick(taps, base, col + R - row))
        tz1[v, :LANES, :LANES] = high
        tz1[v, LANES:, :LANES] = high
        tz2[v, :, :LANES] = low
        near = jnp.where(col < R, col, col + CZ)
        got = jnp.where(col < 2 * R, pick(taps, base, near - row), 0.0)
        high, low = split(got)
        tz1[v, :LANES, LANES:] = high
        tz1[v, LANES:, LANES:] = high
        tz2[v, :, LANES:] = low
        return carry

    lax.fori_loop(0, V, z_of, 0)


BANDS = ((0, 8), (8, 24), (24, 32))


def main_kernel(
    flag, taps, field, w9, z1, z2, observed, w_own, by, byt, wz1, wz2, tz1, tz2,
    part, op1, op2, sums,
    et, gs, hs, xs, ys, wy, edge, edges, ws,
):
    odd_z = flag[2] == 1
    one, two = z1[...], z2[...]
    below, above = jnp.where(odd_z, one, two), jnp.where(odd_z, two, one)
    for b in range(2):
        cols = slice(ROWS + b * LANES, ROWS + (b + 1) * LANES)
        ws[b * 8 : b * 8 + 8] = below[:, cols]
        ws[32 + b * 8 : 40 + b * 8] = above[:, cols]
    ws[16:32] = w9[...]

    edges[:R] = below[:, :ROWS]
    edges[R:] = above[:, :ROWS]
    e = edges[...]
    et[...] = jnp.transpose(
        jnp.concatenate([e, e, e, jnp.zeros((LANES - 6 * R, ROWS), F32)], axis=0)
    )

    for bx in range(3):
        for zb in range(3):
            for j in range(3):
                at = zb * 16 + j * 3 + bx
                w_row = ws[at : at + 1, :]
                for q in range(BANDS[j][0], BANDS[j][1], 8):
                    rows = slice(zb * EY + q, zb * EY + q + 8)
                    high = w_row * byt[q : q + 8]
                    low = w_row * byt[EY + q : EY + q + 8]
                    wy[bx, rows, :LANES] = high
                    wy[bx, rows, LANES : 2 * LANES] = high
                    wy[bx, rows, 2 * LANES :] = low

    face = iota((LANES, LANES), 1)
    face_low = (face >= 2 * R) & (face < 4 * R)
    lhs = by[:, : 3 * EY]
    for x in range(EX):
        high, low = split(field[x])
        e_high, e_low = split(et[x * EY : (x + 1) * EY, :])
        top = jnp.concatenate([high, e_high], axis=1)
        rhs = jnp.concatenate([top, jnp.concatenate([low, e_low], axis=1), top], axis=0)
        got = jnp.dot(lhs, rhs, preferred_element_type=F32)
        high, low = split(got[:, :LANES])
        gs[:, x, :, :LANES] = high.reshape(V, CY, LANES)
        gs[:, x, :, LANES : 2 * LANES] = low.reshape(V, CY, LANES)
        e_got = got[:, LANES:]
        e_high = e_got.astype(BF16).astype(F32)
        both = jnp.where(face_low, e_got - e_high, e_high).astype(BF16)
        gs[:, x, :, 2 * LANES :] = both.reshape(V, CY, LANES)

    lane = iota((8, LANES), 1)
    seen = jnp.zeros((8, LANES), F32)
    for v in range(V):
        block = gs[v].reshape(EX * CY, 3 * LANES)
        got = jnp.dot(block[:, : 2 * LANES], wz1[v], preferred_element_type=F32)
        second = jnp.concatenate([block[:, :LANES], block[:, 2 * LANES :]], axis=1)
        got += jnp.dot(second, wz2[v], preferred_element_type=F32)
        hs[v] = got.reshape(EX, CY, LANES)
    for v in range(V):
        t = [taps[v * 3 * K + k] for k in range(K)]
        own = w_own[v : v + 1, :]
        for b in range(0, CY, 8):
            rows = slice(b, b + 8)
            for a in range(CX):
                acc = t[0] * hs[v, a, rows]
                for k in range(1, K):
                    acc += t[k] * hs[v, a + k, rows]
                image = observed[v, a, rows]
                seen = seen + own * image
                xs[v, a, rows] = image / acc
        for i in range(EX):
            acc = None
            for a in range(max(0, i - K + 1), min(CX, i + 1)):
                term = t[i - a] * xs[v, a]
                acc = term if acc is None else acc + term
            high, low = split(acc)
            gs[v, i, :, :LANES] = high
            gs[v, i, :, LANES : 2 * LANES] = low
        block = gs[v].reshape(EX * CY, 3 * LANES)
        got = jnp.dot(block[:, : 2 * LANES], tz1[v], preferred_element_type=F32)
        got += jnp.dot(block[:, :LANES], tz2[v], preferred_element_type=F32)
        high, low = split(got)
        ys[:, v * CY : (v + 1) * CY, :] = high.reshape(EX, CY, 2 * LANES)
        ys[:, (V + v) * CY : (V + v + 1) * CY, :] = low.reshape(EX, CY, 2 * LANES)

    sub = iota((EY, LANES), 1)
    for x in range(EX):
        bx = 0 if x < R else (1 if x < R + CX else 2)
        got = jnp.dot(wy[bx, :, : 2 * LANES].astype(BF16), ys[x], preferred_element_type=F32)
        got += jnp.dot(
            wy[bx, :, 2 * LANES :].astype(BF16), ys[x, : V * CY], preferred_element_type=F32
        )
        part[x] = got[EY : 2 * EY, :LANES]
        edge[x * EY : (x + 1) * EY, :] = jnp.where(
            sub < R, got[:EY, LANES:], got[2 * EY :, LANES:]
        )

    turned = jnp.transpose(edge[...])
    low, high = turned[:R], turned[R : 2 * R]
    op1[...] = jnp.where(odd_z, low, high)
    op2[...] = jnp.where(odd_z, high, low)

    def count_of(zb, at):
        row = ws[zb * 16 + at : zb * 16 + at + 1, :]
        return jnp.maximum(jnp.sum(row, axis=1, keepdims=True) * (1.0 / CY), 1.0)

    total = jnp.zeros((8, LANES), F32)
    place = iota((8, ROWS), 1) % EY
    y_band = jnp.where(place < R, 0, jnp.where(place < R + CY, 1, 2))
    low_sum = edges[:R] * low
    high_sum = edges[R:] * high
    for bx in range(3):
        x0, x1 = BANDS[bx]
        for j in range(3):
            y0, y1 = BANDS[j]
            at = j * 3 + bx
            block = (field[x0:x1, y0:y1] * part[x0:x1, y0:y1]).reshape((-1, 8, LANES))
            total += jnp.sum(block, axis=0) / count_of(1, at)
            lanes = slice(x0 * EY, x1 * EY)
            picked = y_band[:, lanes] == j
            for side, zb in ((low_sum, 0), (high_sum, 2)):
                cut = jnp.where(picked, side[:, lanes], 0.0)
                folded = cut[:, :LANES]
                for q in range(1, cut.shape[1] // LANES):
                    folded = folded + cut[:, q * LANES : (q + 1) * LANES]
                total += folded / count_of(zb, at)
    target = seen / count_of(1, 4)
    both = jnp.where(lane < 64, total_of(target), total_of(total))
    for p in range(sums.shape[0]):
        sums[p] = both


def z_add(flag, part, r1, r2, mid, op1, op2):
    odd_y, odd_z = flag[1] == 1, flag[2] == 1
    one, two = r1[...], r2[...]
    below, above = jnp.where(odd_z, one, two), jnp.where(odd_z, two, one)
    stacked = jnp.concatenate([below, jnp.zeros((CZ - 2 * R, ROWS), F32), above], axis=0)
    added = jnp.transpose(stacked).reshape(EX, EY, LANES)
    for i in range(EX):
        plane = part[i] + added[i]
        mid[i] = plane[R : R + CY]
        low, high = plane[:R], plane[R + CY :]
        op1[i * R : (i + 1) * R, :] = jnp.where(odd_y, low, high)
        op2[i * R : (i + 1) * R, :] = jnp.where(odd_y, high, low)


def y_add(flag, part, r1, r2, mid, op1, op2):
    odd_x, odd_y = flag[0] == 1, flag[1] == 1
    for i in range(EX):
        one, two = r1[i * R : (i + 1) * R], r2[i * R : (i + 1) * R]
        first = part[i, :R] + jnp.where(odd_y, one, two)
        second = part[i, R:] + jnp.where(odd_y, two, one)
        if i < R:
            at = i
            rows = slice(at * CY, at * CY + R), slice(at * CY + R, (at + 1) * CY)
            op2[rows[0], :] = first
            op2[rows[1], :] = second
        elif i < R + CX:
            mid[i - R, :R] = first
            mid[i - R, R:] = second
        else:
            at = i - R - CX
            rows = slice(at * CY, at * CY + R), slice(at * CY + R, (at + 1) * CY)
            for row, new in zip(rows, (first, second)):
                low = op2[row, :]
                op1[row, :] = jnp.where(odd_x, low, new)
                op2[row, :] = jnp.where(odd_x, new, low)


def x_add(flag, part, r1, r2, est, count, sums, out):
    odd_x = flag[0] == 1
    gathered = jnp.sum(sums[...], axis=0)[:1]
    lane = lax.broadcasted_iota(jnp.int32, (1, LANES), 1)
    target = jnp.sum(jnp.where(lane == 0, gathered, 0.0), axis=1, keepdims=True)
    total = jnp.sum(jnp.where(lane == 64, gathered, 0.0), axis=1, keepdims=True)
    scale = target / total
    counts = jnp.sum(count[...], axis=0, keepdims=True)
    for a in range(CX):
        rows = slice((a % R) * CY, (a % R + 1) * CY)
        one, two = r1[rows, :], r2[rows, :]
        got = jnp.where(odd_x, one, two) if a < R else jnp.where(odd_x, two, one)
        out[a] = est[a] * ((part[a] + got) / counts) * scale


def on_device(estimate, observed, coverage, psf_taps):
    taps = (psf_taps / jnp.sum(psf_taps, axis=2, keepdims=True)).reshape(-1)
    flag = jnp.stack([lax.axis_index(axis) % 2 for axis in ALL]).astype(jnp.int32)
    cover = coverage.reshape(V).astype(F32)
    w_own = jnp.broadcast_to(cover[:, None], (V, LANES))
    w_row = jnp.broadcast_to(jnp.repeat(cover, CY)[None], (8, LANES))
    peers = lax.axis_size(ALL)

    op = shape(R * CY + 8, LANES)
    x1, x2 = kernel_call(x_pack, (op, op), n_in=3, in_smem=1)(flag, estimate, w_row)
    x1, x2 = swap(x1, x2, "bx")
    tables = kernel_call(
        bands,
        (
            shape(V * CY, LANES, dtype=BF16),
            shape(2 * EY, LANES),
            shape(V, 2 * LANES, LANES, dtype=BF16),
            shape(V, 2 * LANES, LANES, dtype=BF16),
            shape(V, 2 * LANES, 2 * LANES, dtype=BF16),
            shape(V, LANES, 2 * LANES, dtype=BF16),
        ),
        n_in=1,
        in_smem=1,
        flops=2 * 10**8,
    )(taps)
    op = shape(EX * R + 8, LANES)
    fx, wx, y1, y2 = kernel_call(
        y_pack, (shape(EX, CY, LANES), shape(8, LANES), op, op), n_in=5, in_smem=1
    )(flag, estimate, w_row, x1, x2)
    y1, y2 = swap(y1, y2, "by")
    op = shape(R, ROWS + 2 * LANES)
    field, w9, z1, z2 = kernel_call(
        z_pack, (shape(EX, EY, LANES), shape(16, LANES), op, op), n_in=5, in_smem=1
    )(flag, fx, wx, y1, y2)
    z1, z2 = swap(z1, z2, "bz")

    face = shape(R, ROWS)
    part, z1, z2, sums = kernel_call(
        main_kernel,
        (shape(EX, EY, LANES), face, face, shape(peers, 8, LANES)),
        scratch=(
            pltpu.VMEM((ROWS, LANES), F32),
            pltpu.VMEM((V, EX, CY, 3 * LANES), BF16),
            pltpu.VMEM((V, EX, CY, LANES), F32),
            pltpu.VMEM((V, CX, CY, LANES), F32),
            pltpu.VMEM((EX, 2 * V * CY, 2 * LANES), BF16),
            pltpu.VMEM((3, 3 * EY, 3 * LANES), F32),
            pltpu.VMEM((ROWS, LANES), F32),
            pltpu.VMEM((2 * R, ROWS), F32),
            pltpu.VMEM((48, LANES), F32),
        ),
        n_in=14,
        in_smem=2,
        flops=2 * 10**9,
    )(flag, taps, field, w9, z1, z2, observed, w_own, *tables)

    sums = lax.all_to_all(sums, ALL, 0, 0)
    z1, z2 = swap(z1, z2, "bz")
    op = shape(EX * R, LANES)
    part, y1, y2 = kernel_call(z_add, (shape(EX, CY, LANES), op, op), n_in=4, in_smem=1)(
        flag, part, z1, z2
    )
    y1, y2 = swap(y1, y2, "by")
    op = shape(R * CY, LANES)
    part, x1, x2 = kernel_call(y_add, (shape(CX, CY, LANES), op, op), n_in=4, in_smem=1)(
        flag, part, y1, y2
    )
    x1, x2 = swap(x1, x2, "bx")
    return kernel_call(x_add, shape(CX, CY, LANES), n_in=7, in_smem=1)(
        flag, part, x1, x2, estimate, w_own, sums
    )


def solution(mesh):
    spec = P("bx", "by", "bz")
    views_spec = P(None, "bx", "by", "bz")
    return jax.shard_map(
        on_device,
        mesh=mesh,
        in_specs=(spec, views_spec, views_spec, P()),
        out_specs=spec,
        check_vma=False,
    )
```

time: 86.8 us -> 75.4 us (0.87)
  local copies, waits for them, and re-layouts: 6.71 us -> 1.91 us
  other arithmetic: 4.77 us -> 0.24 us
  Pallas kernels: 18.9 us -> 14.9 us
  waiting for transfers between devices: 16.2 us -> 17.9 us
    pallas_call x1, Pallas kernels: 14.2 us -> 7.67 us  [on_device(): kernel_call(main_kernel, (shape(EX, EY, LANES), face, face, shape(peers,...]
    concatenate x3 -> x0, local copies, waits for them, and re-layouts: 3.68 us -> none  [the longest x1 3.52 us: z_bands(): jnp.concatenate([middle(low), faces(high), faces(high), faces(low), pad],...]
    pallas_call x3 -> x4, Pallas kernels: 1.88 us -> 4.45 us  [the longest x1 2.56 us: on_device(): kernel_call(bands, (shape(V * CY, LANES, dtype=BF16), shape(2 * EY, LANES...]
    reduce_sum x2 -> x1, other arithmetic: 2.37 us -> 0.09 us  [on_device(): taps = (psf_taps / jnp.sum(psf_taps, axis=2, keepdims=True)).reshape(-1)]
    ppermute x6, waiting for transfers between devices: 16.2 us -> 17.9 us  [swap(): lax.ppermute(two, axis, pairs(count, 1))]
    all_to_all x1, starting transfers between devices: 9.15 us -> 10.3 us  [on_device(): sums = lax.all_to_all(sums, ALL, 0, 0)]
  transfers between devices with their start and end apart: 13 -> 13, of which waited for: 5 -> 5; matrix products, arithmetic and copies ran while one was open for 11% -> 0% of each run, Pallas kernels for 2% -> 5%
where the time goes in v1:
time: 75.4 us; the launch traced here: 75.1 us
  starting transfers between devices  40 us (53%)
  waiting for transfers between devices  17.9 us (24%)
  Pallas kernels  14.9 us (20%)
  local copies, waits for them, and re-layouts  1.91 us (3%)
    ppermute x6, starting transfers between devices, swap(): lax.ppermute(two, axis, pairs(count, 1))  23.6 us
    ppermute x6, waiting for transfers between devices, swap(): lax.ppermute(two, axis, pairs(count, 1))  17.9 us
    all_to_all x1, starting transfers between devices, on_device(): sums = lax.all_to_all(sums, ALL, 0, 0)  10.3 us
    pallas_call x1, Pallas kernels, on_device(): kernel_call(main_kernel, (shape(EX, EY, LANES), face, face, shape(peers,...  7.67 us
    ppermute x6, starting transfers between devices, swap(): lax.ppermute(one, axis, pairs(count, 0))  6.04 us
    pallas_call x1, Pallas kernels, on_device(): kernel_call(bands, (shape(V * CY, LANES, dtype=BF16), shape(2 * EY, LANES...  2.56 us
    unnamed x10, local copies, waits for them, and re-layouts  1.57 us
  transfers between devices with their start and end apart: 13, of which 5 were waited for; matrix products, arithmetic and copies ran while one was open for 0% of the time, Pallas kernels for 5%

profile of v1, /device:TPU:41, one launch (start us, length us, event | category | flops | bytes accessed | tf_op | source)
XLA Modules:
  0.0 75.1 jit_solution(12961248131346842391)
XLA Ops:
  0.0 0.0 copy-start.4
  0.0 0.7 copy-done.4
  0.7 0.1 broadcast_in_dim.8
  0.7 0.1 broadcast_in_dim.18
  0.8 0.0 copy-start.3
  0.8 0.1 pad_add_fusion.flag
  0.9 0.0 copy-start
  0.9 0.9 %copy-done = f32[16,16,128]{2,1,0:T(8,128)S(1)} copy-done((f32[16,16,128]{2,1,0:T(8,128)S(1)}, f32[16,16,128]{2,1,0:T(8,128)}, u32[]{:S(2)}) %copy-start) | copy-done | bytes 131096
  1.8 0.0 copy-start.2
  1.8 0.6 shard_map.46
  2.4 0.8 %collective-permute-start = (f32[136,128]{1,0:T(8,128)S(1)}, f32[136,128]{1,0:T(8,128)S(1)}, u32[]{:S(2)}, u32[]{:S(2)}) collective-permute-start(f32[136,128]{1,0:T(8,128)S(1)} %get-tuple-element.31), channel_id=1, source_target_pairs={{0,32},{32,0},{64,96},{96,64},{1,33},{33,1},{65,97},{97,65},{2,34}... | collective-permute-start | bytes 208904 | tf_op jit(solution)/shard_map/ppermute | solution.py:26
  3.1 4.5 %collective-permute-start.1 = (f32[136,128]{1,0:T(8,128)S(1)}, f32[136,128]{1,0:T(8,128)S(1)}, u32[]{:S(2)}, u32[]{:S(2)}) collective-permute-start(f32[136,128]{1,0:T(8,128)S(1)} %get-tuple-element.32), channel_id=1, source_target_pairs={{32,64},{64,32},{33,65},{65,33},{34,66},{66,34},{35,67},{67,35},{3... | collective-permute-start | bytes 208904 | tf_op jit(solution)/shard_map/ppermute | solution.py:26
  7.6 0.0 collective-permute-done.x1
  7.6 2.6 %collective-permute-done.1.x2 = f32[136,128]{1,0:T(8,128)S(1)} collective-permute-done((f32[136,128]{1,0:T(8,128)S(1)}, f32[136,128]{1,0:T(8,128)S(1)}, u32[]{:S(2)}, u32[]{:S(2)}) %collective-permute-start.1) | collective-permute-done | bytes 69664 | tf_op jit(solution)/shard_map/ppermute | solution.py:26
  10.2 0.6 shard_map.47
  10.8 1.3 %collective-permute-start.2 = (f32[264,128]{1,0:T(8,128)S(1)}, f32[264,128]{1,0:T(8,128)S(1)}, u32[]{:S(2)}, u32[]{:S(2)}) collective-permute-start(f32[264,128]{1,0:T(8,128)S(1)} %get-tuple-element.35), channel_id=1, source_target_pairs={{0,4},{4,0},{8,12},{12,8},{16,20},{20,16},{24,28},{28,24},{1,5},{5... | collective-permute-start | bytes 405512 | tf_op jit(solution)/shard_map/ppermute | solution.py:26
  12.1 3.5 %collective-permute-start.3 = (f32[264,128]{1,0:T(8,128)S(1)}, f32[264,128]{1,0:T(8,128)S(1)}, u32[]{:S(2)}, u32[]{:S(2)}) collective-permute-start(f32[264,128]{1,0:T(8,128)S(1)} %get-tuple-element.36), channel_id=1, source_target_pairs={{4,8},{8,4},{12,16},{16,12},{20,24},{24,20},{5,9},{9,5},{13,17},{1... | collective-permute-start | bytes 405512 | tf_op jit(solution)/shard_map/ppermute | solution.py:26
  15.7 0.0 copy-done.3
  15.7 0.1 reduce_sum.9
  15.8 0.0 collective-permute-done.2.y1
  15.8 4.2 %collective-permute-done.3.y2 = f32[264,128]{1,0:T(8,128)S(1)} collective-permute-done((f32[264,128]{1,0:T(8,128)S(1)}, f32[264,128]{1,0:T(8,128)S(1)}, u32[]{:S(2)}, u32[]{:S(2)}) %collective-permute-start.3) | collective-permute-done | bytes 135200 | tf_op jit(solution)/shard_map/ppermute | solution.py:26
  20.0 0.7 shard_map.48
  20.7 0.2 collective-permute-start.4
  21.0 4.0 %collective-permute-start.5 = (f32[8,1280]{1,0:T(8,128)S(1)}, f32[8,1280]{1,0:T(8,128)S(1)}, u32[]{:S(2)}, u32[]{:S(2)}) collective-permute-start(f32[8,1280]{1,0:T(8,128)S(1)} %get-tuple-element.40), channel_id=1, source_target_pairs={{1,2},{2,1},{5,6},{6,5},{9,10},{10,9},{13,14},{14,13},{17,18},{18,... | collective-permute-start | bytes 122888 | tf_op jit(solution)/shard_map/ppermute | solution.py:26
  25.0 0.1 broadcast_divide_fusion
  25.1 0.1 reshape.12.taps
  25.2 2.6 %shard_map.49 = (bf16[128,128]{1,0:T(8,128)(2,1)S(1)}, f32[64,128]{1,0:T(8,128)S(1)}, bf16[8,256,128]{2,1,0:T(8,128)(2,1)S(1)}, bf16[8,256,128]{2,1,0:T(8,128)(2...) custom-call(f32[408]{0:T(512)S(1)} %reshape.12.taps), custom_call_target="tpu_custom_call" | custom-call | flops 200000000 | bytes 1024 | tf_op jit(solution)/shard_map/pallas_call | solution.py:368
  27.8 0.0 collective-permute-done.4.z1
  27.8 0.0 collective-permute-done.5.z2
  27.8 0.1 broadcast_in_dim.20.w_own.count
  27.9 0.0 copy-done.2
  27.9 7.7 %shard_map.50 = (f32[32,32,128]{2,1,0:T(8,128)S(1)}, f32[8,1024]{1,0:T(8,128)S(1)}, f32[8,1024]{1,0:T(8,128)S(1)}, f32[128,8,128]{2,1,0:T(8,128)}) custom-call(s32[3]{0:T(128)S(1)} %pad_add_fusion.flag, f32[408]{0:T(512)S(1)} %reshape.12.taps, f32[32,32,128]{2,1,0:T(8,128)S(1)} %get-tuple-element.37.field, f32[16,128]{1,0:T(8,128)S(1)} %get-tuple-element.38.w9, ...), custom_call_target="tpu_custom_call" | custom-call | flops 2000000000 | bytes 1024 | tf_op jit(solution)/shard_map/pallas_call | solution.py:394
  35.5 10.3 %all-to-all-start = ((f32[128,8,128]{2,1,0:T(8,128)}), f32[128,8,128]{2,1,0:T(8,128)S(1)}, u32[]{:S(2)}, u32[]{:S(2)}) async-start(f32[128,8,128]{2,1,0:T(8,128)} %get-tuple-element.56), calls=%async_computation | async-start | bytes 1048576 | tf_op jit(solution)/shard_map/all_to_all | solution.py:413
  45.9 0.3 collective-permute-start.6
  46.2 3.9 %collective-permute-start.7 = (f32[8,1024]{1,0:T(8,128)S(1)}, f32[8,1024]{1,0:T(8,128)S(1)}, u32[]{:S(2)}, u32[]{:S(2)}) collective-permute-start(f32[8,1024]{1,0:T(8,128)S(1)} %get-tuple-element.49), channel_id=1, source_target_pairs={{1,2},{2,1},{5,6},{6,5},{9,10},{10,9},{13,14},{14,13},{17,18},{18,... | collective-permute-start | bytes 98312 | tf_op jit(solution)/shard_map/ppermute | solution.py:26
  50.1 0.0 collective-permute-done.6.r1
  50.1 3.5 %collective-permute-done.7.r2 = f32[8,1024]{1,0:T(8,128)S(1)} collective-permute-done((f32[8,1024]{1,0:T(8,128)S(1)}, f32[8,1024]{1,0:T(8,128)S(1)}, u32[]{:S(2)}, u32[]{:S(2)}) %collective-permute-start.7) | collective-permute-done | bytes 32800 | tf_op jit(solution)/shard_map/ppermute | solution.py:26
  53.6 0.7 shard_map.51
  54.3 1.8 %collective-permute-start.8 = (f32[256,128]{1,0:T(8,128)S(1)}, f32[256,128]{1,0:T(8,128)S(1)}, u32[]{:S(2)}, u32[]{:S(2)}) collective-permute-start(f32[256,128]{1,0:T(8,128)S(1)} %get-tuple-element.51), channel_id=1, source_target_pairs={{0,4},{4,0},{8,12},{12,8},{16,20},{20,16},{24,28},{28,24},{1,5},{5... | collective-permute-start | bytes 393224 | tf_op jit(solution)/shard_map/ppermute | solution.py:26
  56.1 3.5 %collective-permute-start.9 = (f32[256,128]{1,0:T(8,128)S(1)}, f32[256,128]{1,0:T(8,128)S(1)}, u32[]{:S(2)}, u32[]{:S(2)}) collective-permute-start(f32[256,128]{1,0:T(8,128)S(1)} %get-tuple-element.52), channel_id=1, source_target_pairs={{4,8},{8,4},{12,16},{16,12},{20,24},{24,20},{5,9},{9,5},{13,17},{1... | collective-permute-start | bytes 393224 | tf_op jit(solution)/shard_map/ppermute | solution.py:26
  59.6 0.0 collective-permute-done.8.r1
  59.6 4.8 %collective-permute-done.9.r2 = f32[256,128]{1,0:T(8,128)S(1)} collective-permute-done((f32[256,128]{1,0:T(8,128)S(1)}, f32[256,128]{1,0:T(8,128)S(1)}, u32[]{:S(2)}, u32[]{:S(2)}) %collective-permute-start.9) | collective-permute-done | bytes 131104 | tf_op jit(solution)/shard_map/ppermute | solution.py:26
  64.3 0.0 copy-start.1
  64.4 0.6 shard_map.52
  64.9 1.7 %collective-permute-start.10 = (f32[128,128]{1,0:T(8,128)S(1)}, f32[128,128]{1,0:T(8,128)S(1)}, u32[]{:S(2)}, u32[]{:S(2)}) collective-permute-start(f32[128,128]{1,0:T(8,128)S(1)} %get-tuple-element.54), channel_id=1, source_target_pairs={{0,32},{32,0},{64,96},{96,64},{1,33},{33,1},{65,97},{97,65},{2,34}... | collective-permute-start | bytes 196616 | tf_op jit(solution)/shard_map/ppermute | solution.py:26
  66.6 4.2 %collective-permute-start.11 = (f32[128,128]{1,0:T(8,128)S(1)}, f32[128,128]{1,0:T(8,128)S(1)}, u32[]{:S(2)}, u32[]{:S(2)}) collective-permute-start(f32[128,128]{1,0:T(8,128)S(1)} %get-tuple-element.55), channel_id=1, source_target_pairs={{32,64},{64,32},{33,65},{65,33},{34,66},{66,34},{35,67},{67,35},{3... | collective-permute-start | bytes 196616 | tf_op jit(solution)/shard_map/ppermute | solution.py:26
  70.8 0.0 collective-permute-done.10.r1
  70.8 2.9 %collective-permute-done.11.r2 = f32[128,128]{1,0:T(8,128)S(1)} collective-permute-done((f32[128,128]{1,0:T(8,128)S(1)}, f32[128,128]{1,0:T(8,128)S(1)}, u32[]{:S(2)}, u32[]{:S(2)}) %collective-permute-start.11) | collective-permute-done | bytes 65568 | tf_op jit(solution)/shard_map/ppermute | solution.py:26
  73.7 0.0 all-to-all-done.sums
  73.7 0.0 copy-done.1
  73.7 1.4 %shard_map.53 = f32[16,16,128]{2,1,0:T(8,128)} custom-call(s32[3]{0:T(128)S(1)} %pad_add_fusion.flag, f32[16,16,128]{2,1,0:T(8,128)S(1)} %get-tuple-element.53.part, f32[128,128]{1,0:T(8,128)S(1)} %collective-permute-done.10.r1, f32[128,128]{1,0:T(8,128)S(1)} %collective-permute-done.11.r2, f32[16,16,128]{2,1,0:T(8,128)S(1)} %copy-done.1, ...), custom_call_target="tpu_custom_call" | custom-call | bytes 1024 | tf_op jit(solution)/shard_map/pallas_call | solution.py:425
  (3 shorter events, 0.0 us)
Async XLA Ops:
  0.0 0.7 copy-start.4
  0.8 14.8 %copy-start.3 = (f32[8,3,17]{2,0,1:T(8,128)S(1)}, f32[8,3,17]{2,0,1:T(8,128)}, u32[]{:S(2)}) copy-start(f32[8,3,17]{2,0,1:T(8,128)} %param.7) | copy-start | bytes 4900
  0.9 0.9 %copy-start = (f32[16,16,128]{2,1,0:T(8,128)S(1)}, f32[16,16,128]{2,1,0:T(8,128)}, u32[]{:S(2)}) copy-start(f32[16,16,128]{2,1,0:T(8,128)} %est.5) | copy-start | bytes 393220
  1.8 26.1 %copy-start.2 = (f32[8,16,16,128]{3,2,1,0:T(8,128)S(1)}, f32[8,16,16,128]{3,2,1,0:T(8,128)}, u32[]{:S(2)}) copy-start(f32[8,16,16,128]{3,2,1,0:T(8,128)} %observed.1) | copy-start | bytes 3145732
  2.4 5.3 %collective-permute-start = (f32[136,128]{1,0:T(8,128)S(1)}, f32[136,128]{1,0:T(8,128)S(1)}, u32[]{:S(2)}, u32[]{:S(2)}) collective-permute-start(f32[136,128]{1,0:T(8,128)S(1)} %get-tuple-element.31), channel_id=1, source_target_pairs={{0,32},{32,0},{64,96},{96,64},{1,33},{33,1},{65,97},{97,65},{2,34}... | collective-permute-start | bytes 208904 | tf_op jit(solution)/shard_map/ppermute | solution.py:26
  3.1 7.1 %collective-permute-start.1 = (f32[136,128]{1,0:T(8,128)S(1)}, f32[136,128]{1,0:T(8,128)S(1)}, u32[]{:S(2)}, u32[]{:S(2)}) collective-permute-start(f32[136,128]{1,0:T(8,128)S(1)} %get-tuple-element.32), channel_id=1, source_target_pairs={{32,64},{64,32},{33,65},{65,33},{34,66},{66,34},{35,67},{67,35},{3... | collective-permute-start | bytes 208904 | tf_op jit(solution)/shard_map/ppermute | solution.py:26
  10.8 4.9 %collective-permute-start.2 = (f32[264,128]{1,0:T(8,128)S(1)}, f32[264,128]{1,0:T(8,128)S(1)}, u32[]{:S(2)}, u32[]{:S(2)}) collective-permute-start(f32[264,128]{1,0:T(8,128)S(1)} %get-tuple-element.35), channel_id=1, source_target_pairs={{0,4},{4,0},{8,12},{12,8},{16,20},{20,16},{24,28},{28,24},{1,5},{5... | collective-permute-start | bytes 405512 | tf_op jit(solution)/shard_map/ppermute | solution.py:26
  12.1 7.9 %collective-permute-start.3 = (f32[264,128]{1,0:T(8,128)S(1)}, f32[264,128]{1,0:T(8,128)S(1)}, u32[]{:S(2)}, u32[]{:S(2)}) collective-permute-start(f32[264,128]{1,0:T(8,128)S(1)} %get-tuple-element.36), channel_id=1, source_target_pairs={{4,8},{8,4},{12,16},{16,12},{20,24},{24,20},{5,9},{9,5},{13,17},{1... | collective-permute-start | bytes 405512 | tf_op jit(solution)/shard_map/ppermute | solution.py:26
  20.7 7.0 %collective-permute-start.4 = (f32[8,1280]{1,0:T(8,128)S(1)}, f32[8,1280]{1,0:T(8,128)S(1)}, u32[]{:S(2)}, u32[]{:S(2)}) collective-permute-start(f32[8,1280]{1,0:T(8,128)S(1)} %get-tuple-element.39), channel_id=1, source_target_pairs={{0,1},{1,0},{2,3},{3,2},{4,5},{5,4},{6,7},{7,6},{8,9},{9,8},{10,11... | collective-permute-start | bytes 122888 | tf_op jit(solution)/shard_map/ppermute | solution.py:26
  21.0 6.8 %collective-permute-start.5 = (f32[8,1280]{1,0:T(8,128)S(1)}, f32[8,1280]{1,0:T(8,128)S(1)}, u32[]{:S(2)}, u32[]{:S(2)}) collective-permute-start(f32[8,1280]{1,0:T(8,128)S(1)} %get-tuple-element.40), channel_id=1, source_target_pairs={{1,2},{2,1},{5,6},{6,5},{9,10},{10,9},{13,14},{14,13},{17,18},{18,... | collective-permute-start | bytes 122888 | tf_op jit(solution)/shard_map/ppermute | solution.py:26
  35.5 38.2 %all-to-all-start = ((f32[128,8,128]{2,1,0:T(8,128)}), f32[128,8,128]{2,1,0:T(8,128)S(1)}, u32[]{:S(2)}, u32[]{:S(2)}) async-start(f32[128,8,128]{2,1,0:T(8,128)} %get-tuple-element.56), calls=%async_computation | async-start | bytes 1048576 | tf_op jit(solution)/shard_map/all_to_all | solution.py:413
  45.9 4.2 %collective-permute-start.6 = (f32[8,1024]{1,0:T(8,128)S(1)}, f32[8,1024]{1,0:T(8,128)S(1)}, u32[]{:S(2)}, u32[]{:S(2)}) collective-permute-start(f32[8,1024]{1,0:T(8,128)S(1)} %get-tuple-element.48), channel_id=1, source_target_pairs={{0,1},{1,0},{2,3},{3,2},{4,5},{5,4},{6,7},{7,6},{8,9},{9,8},{10,11... | collective-permute-start | bytes 98312 | tf_op jit(solution)/shard_map/ppermute | solution.py:26
  46.2 7.4 %collective-permute-start.7 = (f32[8,1024]{1,0:T(8,128)S(1)}, f32[8,1024]{1,0:T(8,128)S(1)}, u32[]{:S(2)}, u32[]{:S(2)}) collective-permute-start(f32[8,1024]{1,0:T(8,128)S(1)} %get-tuple-element.49), channel_id=1, source_target_pairs={{1,2},{2,1},{5,6},{6,5},{9,10},{10,9},{13,14},{14,13},{17,18},{18,... | collective-permute-start | bytes 98312 | tf_op jit(solution)/shard_map/ppermute | solution.py:26
  54.3 5.3 %collective-permute-start.8 = (f32[256,128]{1,0:T(8,128)S(1)}, f32[256,128]{1,0:T(8,128)S(1)}, u32[]{:S(2)}, u32[]{:S(2)}) collective-permute-start(f32[256,128]{1,0:T(8,128)S(1)} %get-tuple-element.51), channel_id=1, source_target_pairs={{0,4},{4,0},{8,12},{12,8},{16,20},{20,16},{24,28},{28,24},{1,5},{5... | collective-permute-start | bytes 393224 | tf_op jit(solution)/shard_map/ppermute | solution.py:26
  56.1 8.3 %collective-permute-start.9 = (f32[256,128]{1,0:T(8,128)S(1)}, f32[256,128]{1,0:T(8,128)S(1)}, u32[]{:S(2)}, u32[]{:S(2)}) collective-permute-start(f32[256,128]{1,0:T(8,128)S(1)} %get-tuple-element.52), channel_id=1, source_target_pairs={{4,8},{8,4},{12,16},{16,12},{20,24},{24,20},{5,9},{9,5},{13,17},{1... | collective-permute-start | bytes 393224 | tf_op jit(solution)/shard_map/ppermute | solution.py:26
  64.3 9.4 %copy-start.1 = (f32[16,16,128]{2,1,0:T(8,128)S(1)}, f32[16,16,128]{2,1,0:T(8,128)}, u32[]{:S(2)}) copy-start(f32[16,16,128]{2,1,0:T(8,128)} %est.5) | copy-start | bytes 393220
  64.9 5.9 %collective-permute-start.10 = (f32[128,128]{1,0:T(8,128)S(1)}, f32[128,128]{1,0:T(8,128)S(1)}, u32[]{:S(2)}, u32[]{:S(2)}) collective-permute-start(f32[128,128]{1,0:T(8,128)S(1)} %get-tuple-element.54), channel_id=1, source_target_pairs={{0,32},{32,0},{64,96},{96,64},{1,33},{33,1},{65,97},{97,65},{2,34}... | collective-permute-start | bytes 196616 | tf_op jit(solution)/shard_map/ppermute | solution.py:26
  66.6 7.1 %collective-permute-start.11 = (f32[128,128]{1,0:T(8,128)S(1)}, f32[128,128]{1,0:T(8,128)S(1)}, u32[]{:S(2)}, u32[]{:S(2)}) collective-permute-start(f32[128,128]{1,0:T(8,128)S(1)} %get-tuple-element.55), channel_id=1, source_target_pairs={{32,64},{64,32},{33,65},{65,33},{34,66},{66,34},{35,67},{67,35},{3... | collective-permute-start | bytes 196616 | tf_op jit(solution)/shard_map/ppermute | solution.py:26

commit v2 on v1

--- a/solution.py
+++ b/solution.py
@@ -4,6 +4,7 @@
 from jax.experimental import pallas as pl
 from jax.experimental.pallas import tpu as pltpu
 from jax.sharding import PartitionSpec as P
+
 
 ALL = ("bx", "by", "bz")
 F32, BF16 = jnp.float32, jnp.bfloat16
@@ -44,47 +45,56 @@
     return jax.ShapeDtypeStruct(dims, dtype)
 
 
-def x_pack(flag, est, w, op1, op2):
-    odd = flag[0] == 1
+def spread_cover(cover):
+    lane = iota((8, LANES), 1) // CY
+    row = jnp.zeros((8, LANES), F32)
+    for v in range(V):
+        row = jnp.where(lane == v, cover[v].astype(F32), row)
+    return row
+
+
+def y_pack(flag, cover, est, op1, op2):
+    odd = flag[1] == 1
+    for i in range(CX):
+        low, high = est[i, :R], est[i, CY - R :]
+        op1[i * R : (i + 1) * R, :] = jnp.where(odd, low, high)
+        op2[i * R : (i + 1) * R, :] = jnp.where(odd, high, low)
+    row = spread_cover(cover)
+    op1[CX * R :, :] = row
+    op2[CX * R :, :] = row
+
+
+def x_pack(flag, cover, est, y1, y2, field, ws, op1, op2):
+    odd_x, odd_y = flag[0] == 1, flag[1] == 1
+    one, two = y1[...], y2[...]
+    below, above = jnp.where(odd_y, one, two), jnp.where(odd_y, two, one)
+    cells = CX * R
+    field[:, :R] = below[:cells].reshape(CX, R, LANES)
+    field[:, R : R + CY] = est[...]
+    field[:, R + CY :] = above[:cells].reshape(CX, R, LANES)
+    ws[...] = jnp.zeros_like(ws)
+    ws[:1] = below[cells : cells + 1]
+    ws[1:2] = spread_cover(cover)[:1]
+    ws[2:3] = above[cells : cells + 1]
     for a in range(R):
-        low, high = est[a], est[CX - R + a]
-        op1[a * CY : (a + 1) * CY, :] = jnp.where(odd, low, high)
-        op2[a * CY : (a + 1) * CY, :] = jnp.where(odd, high, low)
-    op1[R * CY :, :] = w[...]
-    op2[R * CY :, :] = w[...]
-
-
-def y_pack(flag, est, w, x1, x2, field, ws, op1, op2):
-    odd_x, odd_y = flag[0] == 1, flag[1] == 1
+        low, high = field[a], field[CX - R + a]
+        op1[a * EY : (a + 1) * EY, :] = jnp.where(odd_x, low, high)
+        op2[a * EY : (a + 1) * EY, :] = jnp.where(odd_x, high, low)
+    op1[R * EY :, :] = ws[...]
+    op2[R * EY :, :] = ws[...]
+
+
+def z_pack(flag, fy, wy, x1, x2, field, ws, op1, op2):
+    odd_x, odd_z = flag[0] == 1, flag[2] == 1
     one, two = x1[...], x2[...]
     below, above = jnp.where(odd_x, one, two), jnp.where(odd_x, two, one)
-    cells = R * CY
-    field[:R] = below[:cells].reshape(R, CY, LANES)
-    field[R : R + CX] = est[...]
-    field[R + CX :] = above[:cells].reshape(R, CY, LANES)
-    ws[...] = w[...]
-    ws[:1] = below[cells : cells + 1]
-    ws[1:2] = w[:1]
-    ws[2:3] = above[cells : cells + 1]
-    for i in range(EX):
-        low, high = field[i, :R], field[i, CY - R :]
-        op1[i * R : (i + 1) * R, :] = jnp.where(odd_y, low, high)
-        op2[i * R : (i + 1) * R, :] = jnp.where(odd_y, high, low)
-    op1[EX * R :, :] = ws[...]
-    op2[EX * R :, :] = ws[...]
-
-
-def z_pack(flag, fx, wx, y1, y2, field, ws, op1, op2):
-    odd_y, odd_z = flag[1] == 1, flag[2] == 1
-    one, two = y1[...], y2[...]
-    below, above = jnp.where(odd_y, one, two), jnp.where(odd_y, two, one)
-    cells = EX * R
-    field[:, :R] = below[:cells].reshape(EX, R, LANES)
-    field[:, R : R + CY] = fx[...]
-    field[:, R + CY :] = above[:cells].reshape(EX, R, LANES)
+    cells = R * EY
+    field[:R] = below[:cells].reshape(R, EY, LANES)
+    field[R : R + CX] = fy[...]
+    field[R + CX :] = above[:cells].reshape(R, EY, LANES)
     ws[...] = jnp.zeros_like(ws)
     ws[:3] = below[cells : cells + 3]
-    ws[3:6] = wx[:3]
+    ws[3:6] = wy[:3]
     ws[6:9] = above[cells : cells + 3]
     turned = jnp.transpose(field[...].reshape(ROWS, LANES))
     low, high = turned[:R], turned[CZ - R :]
@@ -109,25 +119,33 @@
     return lax.broadcasted_iota(jnp.int32, dims, axis)
 
 
-def pick(taps, base, offset):
+def pick(taps, v, d, offset, scale):
     got = jnp.zeros(offset.shape, F32)
     for k in range(K):
-        got = jnp.where(offset == k, taps[base + k], got)
-    return got
+        got = jnp.where(offset == k, taps[v, d, k], got)
+    return got * scale
+
+
+def inverse_sum(taps, v, d):
+    total = taps[v, d, 0]
+    for k in range(1, K):
+        total = total + taps[v, d, k]
+    return 1.0 / jnp.full((8, LANES), total, F32)[:1]
 
 
 def bands(taps, by, byt, wz1, wz2, tz1, tz2):
     for v in range(V):
-        base = (v * 3 + 1) * K
         rows = slice(v * CY, (v + 1) * CY)
+        scale = inverse_sum(taps, v, 0) * inverse_sum(taps, v, 1)
         column = iota((CY, LANES), 1)
-        got = pick(taps, base, column % EY - iota((CY, LANES), 0))
+        got = pick(taps, v, 1, column % EY - iota((CY, LANES), 0), scale)
         high, low = split(got)
         by[rows, :] = jnp.where(column < 2 * EY, high.astype(F32), low.astype(F32)).astype(BF16)
 
     def turned_y(v, got):
         lane = iota((EY, LANES), 1)
-        here = pick(taps, (v * 3 + 1) * K, iota((EY, LANES), 0) - lane % CY)
+        scale = inverse_sum(taps, v, 0) * inverse_sum(taps, v, 1)
+        here = pick(taps, v, 1, iota((EY, LANES), 0) - lane % CY, scale)
         return jnp.where(lane // CY == v, here, got)
 
     both = lax.fori_loop(0, V, turned_y, jnp.zeros((EY, LANES), F32))
@@ -136,27 +154,27 @@
     byt[EY:, :] = low.astype(F32)
 
     def z_of(v, carry):
-        base = (v * 3 + 2) * K
+        scale = inverse_sum(taps, v, 2)
         row, col = iota((LANES, LANES), 0), iota((LANES, LANES), 1)
-        high, low = split(pick(taps, base, row + R - col))
+        high, low = split(pick(taps, v, 2, row + R - col, scale))
         wz1[v, :LANES, :] = high
         wz1[v, LANES:, :] = high
         wz2[v, :LANES, :] = low
         place = row[: 6 * R] % (2 * R)
         near = jnp.where(place < R, place, place + CZ)
-        got = pick(taps, base, near - col[: 6 * R])
+        got = pick(taps, v, 2, near - col[: 6 * R], scale)
         high, low = split(got)
         which = row[: 6 * R] < 4 * R
         wz2[v, LANES : LANES + 6 * R, :] = jnp.where(
             which, high.astype(F32), low.astype(F32)
         ).astype(BF16)
         wz2[v, LANES + 6 * R :, :] = jnp.zeros((LANES - 6 * R, LANES), BF16)
-        high, low = split(pick(taps, base, col + R - row))
+        high, low = split(pick(taps, v, 2, col + R - row, scale))
         tz1[v, :LANES, :LANES] = high
         tz1[v, LANES:, :LANES] = high
         tz2[v, :, :LANES] = low
         near = jnp.where(col < R, col, col + CZ)
-        got = jnp.where(col < 2 * R, pick(taps, base, near - row), 0.0)
+        got = jnp.where(col < 2 * R, pick(taps, v, 2, near - row, scale), 0.0)
         high, low = split(got)
         tz1[v, :LANES, LANES:] = high
         tz1[v, LANES:, LANES:] = high
@@ -170,7 +188,7 @@
 
 
 def main_kernel(
-    flag, taps, field, w9, z1, z2, observed, w_own, by, byt, wz1, wz2, tz1, tz2,
+    flag, taps, cover, field, w9, z1, z2, observed, by, byt, wz1, wz2, tz1, tz2,
     part, op1, op2, sums,
     et, gs, hs, xs, ys, wy, edge, edges, ws,
 ):
@@ -193,7 +211,7 @@
     for bx in range(3):
         for zb in range(3):
             for j in range(3):
-                at = zb * 16 + j * 3 + bx
+                at = zb * 16 + bx * 3 + j
                 w_row = ws[at : at + 1, :]
                 for q in range(BANDS[j][0], BANDS[j][1], 8):
                     rows = slice(zb * EY + q, zb * EY + q + 8)
@@ -229,8 +247,8 @@
         got += jnp.dot(second, wz2[v], preferred_element_type=F32)
         hs[v] = got.reshape(EX, CY, LANES)
     for v in range(V):
-        t = [taps[v * 3 * K + k] for k in range(K)]
-        own = w_own[v : v + 1, :]
+        t = [taps[v, 0, k] for k in range(K)]
+        own = cover[v].astype(F32)
         for b in range(0, CY, 8):
             rows = slice(b, b + 8)
             for a in range(CX):
@@ -285,7 +303,7 @@
         x0, x1 = BANDS[bx]
         for j in range(3):
             y0, y1 = BANDS[j]
-            at = j * 3 + bx
+            at = bx * 3 + j
             block = (field[x0:x1, y0:y1] * part[x0:x1, y0:y1]).reshape((-1, 8, LANES))
             total += jnp.sum(block, axis=0) / count_of(1, at)
             lanes = slice(x0 * EY, x1 * EY)
@@ -303,68 +321,56 @@
 
 
 def z_add(flag, part, r1, r2, mid, op1, op2):
-    odd_y, odd_z = flag[1] == 1, flag[2] == 1
+    odd_x, odd_z = flag[0] == 1, flag[2] == 1
     one, two = r1[...], r2[...]
     below, above = jnp.where(odd_z, one, two), jnp.where(odd_z, two, one)
     stacked = jnp.concatenate([below, jnp.zeros((CZ - 2 * R, ROWS), F32), above], axis=0)
     added = jnp.transpose(stacked).reshape(EX, EY, LANES)
-    for i in range(EX):
-        plane = part[i] + added[i]
-        mid[i] = plane[R : R + CY]
+    mid[...] = part[R : R + CX] + added[R : R + CX]
+    for i in range(R):
+        low, high = part[i] + added[i], part[R + CX + i] + added[R + CX + i]
+        op1[i * EY : (i + 1) * EY, :] = jnp.where(odd_x, low, high)
+        op2[i * EY : (i + 1) * EY, :] = jnp.where(odd_x, high, low)
+
+
+def x_add(flag, part, r1, r2, mid, op1, op2):
+    odd_x, odd_y = flag[0] == 1, flag[1] == 1
+    for a in range(CX):
+        rows = slice((a % R) * EY, (a % R + 1) * EY)
+        one, two = r1[rows, :], r2[rows, :]
+        plane = part[a] + (jnp.where(odd_x, one, two) if a < R else jnp.where(odd_x, two, one))
+        mid[a] = plane[R : R + CY]
         low, high = plane[:R], plane[R + CY :]
-        op1[i * R : (i + 1) * R, :] = jnp.where(odd_y, low, high)
-        op2[i * R : (i + 1) * R, :] = jnp.where(odd_y, high, low)
-
-
-def y_add(flag, part, r1, r2, mid, op1, op2):
-    odd_x, odd_y = flag[0] == 1, flag[1] == 1
-    for i in range(EX):
-        one, two = r1[i * R : (i + 1) * R], r2[i * R : (i + 1) * R]
-        first = part[i, :R] + jnp.where(odd_y, one, two)
-        second = part[i, R:] + jnp.where(odd_y, two, one)
-        if i < R:
-            at = i
-            rows = slice(at * CY, at * CY + R), slice(at * CY + R, (at + 1) * CY)
-            op2[rows[0], :] = first
-            op2[rows[1], :] = second
-        elif i < R + CX:
-            mid[i - R, :R] = first
-            mid[i - R, R:] = second
-        else:
-            at = i - R - CX
-            rows = slice(at * CY, at * CY + R), slice(at * CY + R, (at + 1) * CY)
-            for row, new in zip(rows, (first, second)):
-                low = op2[row, :]
-                op1[row, :] = jnp.where(odd_x, low, new)
-                op2[row, :] = jnp.where(odd_x, new, low)
-
-
-def x_add(flag, part, r1, r2, est, count, sums, out):
-    odd_x = flag[0] == 1
-    gathered = jnp.sum(sums[...], axis=0)[:1]
-    lane = lax.broadcasted_iota(jnp.int32, (1, LANES), 1)
+        op1[a * R : (a + 1) * R, :] = jnp.where(odd_y, low, high)
+        op2[a * R : (a + 1) * R, :] = jnp.where(odd_y, high, low)
+
+
+def scale_of(cover, sums, scale):
+    gathered = jnp.sum(sums[...], axis=0)
+    lane = iota((8, LANES), 1)
     target = jnp.sum(jnp.where(lane == 0, gathered, 0.0), axis=1, keepdims=True)
     total = jnp.sum(jnp.where(lane == 64, gathered, 0.0), axis=1, keepdims=True)
-    scale = target / total
-    counts = jnp.sum(count[...], axis=0, keepdims=True)
+    count = jnp.sum(spread_cover(cover), axis=1, keepdims=True) * (1.0 / CY)
+    scale[...] = jnp.broadcast_to(target / total / count, (8, LANES))
+
+
+def y_add(flag, part, r1, r2, est, scale, out):
+    odd = flag[1] == 1
+    by = scale[...]
     for a in range(CX):
-        rows = slice((a % R) * CY, (a % R + 1) * CY)
-        one, two = r1[rows, :], r2[rows, :]
-        got = jnp.where(odd_x, one, two) if a < R else jnp.where(odd_x, two, one)
-        out[a] = est[a] * ((part[a] + got) / counts) * scale
+        one, two = r1[a * R : (a + 1) * R, :], r2[a * R : (a + 1) * R, :]
+        out[a, :R] = est[a, :R] * (part[a, :R] + jnp.where(odd, one, two)) * by
+        out[a, R:] = est[a, R:] * (part[a, R:] + jnp.where(odd, two, one)) * by
 
 
 def on_device(estimate, observed, coverage, psf_taps):
-    taps = (psf_taps / jnp.sum(psf_taps, axis=2, keepdims=True)).reshape(-1)
     flag = jnp.stack([lax.axis_index(axis) % 2 for axis in ALL]).astype(jnp.int32)
-    cover = coverage.reshape(V).astype(F32)
-    w_own = jnp.broadcast_to(cover[:, None], (V, LANES))
-    w_row = jnp.broadcast_to(jnp.repeat(cover, CY)[None], (8, LANES))
+    cover = coverage.reshape(V)
     peers = lax.axis_size(ALL)
 
-    op = shape(R * CY + 8, LANES)
-    x1, x2 = kernel_call(x_pack, (op, op), n_in=3, in_smem=1)(flag, estimate, w_row)
-    x1, x2 = swap(x1, x2, "bx")
+    op = shape(R * CX + 8, LANES)
+    y1, y2 = kernel_call(y_pack, (op, op), n_in=3, in_smem=2)(flag, cover, estimate)
+    y1, y2 = swap(y1, y2, "by")
     tables = kernel_call(
         bands,
         (
@@ -378,16 +384,16 @@
         n_in=1,
         in_smem=1,
         flops=2 * 10**8,
-    )(taps)
-    op = shape(EX * R + 8, LANES)
-    fx, wx, y1, y2 = kernel_call(
-        y_pack, (shape(EX, CY, LANES), shape(8, LANES), op, op), n_in=5, in_smem=1
-    )(flag, estimate, w_row, x1, x2)
-    y1, y2 = swap(y1, y2, "by")
+    )(psf_taps)
+    op = shape(EY * R + 8, LANES)
+    fy, wy, x1, x2 = kernel_call(
+        x_pack, (shape(CX, EY, LANES), shape(8, LANES), op, op), n_in=5, in_smem=2
+    )(flag, cover, estimate, y1, y2)
+    x1, x2 = swap(x1, x2, "bx")
     op = shape(R, ROWS + 2 * LANES)
     field, w9, z1, z2 = kernel_call(
         z_pack, (shape(EX, EY, LANES), shape(16, LANES), op, op), n_in=5, in_smem=1
-    )(flag, fx, wx, y1, y2)
+    )(flag, fy, wy, x1, x2)
     z1, z2 = swap(z1, z2, "bz")
 
     face = shape(R, ROWS)
@@ -406,30 +412,32 @@
             pltpu.VMEM((48, LANES), F32),
         ),
         n_in=14,
-        in_smem=2,
+        in_smem=3,
         flops=2 * 10**9,
-    )(flag, taps, field, w9, z1, z2, observed, w_own, *tables)
-
+    )(flag, psf_taps, cover, field, w9, z1, z2, observed, *tables)
+
+    z1, z2 = swap(z1, z2, "bz")
     sums = lax.all_to_all(sums, ALL, 0, 0)
-    z1, z2 = swap(z1, z2, "bz")
-    op = shape(EX * R, LANES)
-    part, y1, y2 = kernel_call(z_add, (shape(EX, CY, LANES), op, op), n_in=4, in_smem=1)(
+    op = shape(EY * R, LANES)
+    part, x1, x2 = kernel_call(z_add, (shape(CX, EY, LANES), op, op), n_in=4, in_smem=1)(
         flag, part, z1, z2
     )
+    x1, x2 = swap(x1, x2, "bx")
+    scale = kernel_call(scale_of, shape(8, LANES), n_in=2, in_smem=1, flops=10**6)(cover, sums)
+    op = shape(R * CX, LANES)
+    part, y1, y2 = kernel_call(x_add, (shape(CX, CY, LANES), op, op), n_in=4, in_smem=1)(
+        flag, part, x1, x2
+    )
     y1, y2 = swap(y1, y2, "by")
-    op = shape(R * CY, LANES)
-    part, x1, x2 = kernel_call(y_add, (shape(CX, CY, LANES), op, op), n_in=4, in_smem=1)(
-        flag, part, y1, y2
-    )
-    x1, x2 = swap(x1, x2, "bx")
-    return kernel_call(x_add, shape(CX, CY, LANES), n_in=7, in_smem=1)(
-        flag, part, x1, x2, estimate, w_own, sums
+    return kernel_call(y_add, shape(CX, CY, LANES), n_in=6, in_smem=1)(
+        flag, part, y1, y2, estimate, scale
     )
 
 
 def solution(mesh):
     spec = P("bx", "by", "bz")
     views_spec = P(None, "bx", "by", "bz")
+
     return jax.shard_map(
         on_device,
         mesh=mesh,

time: 75.4 us -> 74.1 us (0.983)
  starting transfers between devices: 40 us -> 38.5 us
  Pallas kernels: 14.9 us -> 16 us
  waiting for transfers between devices: 17.9 us -> 17 us
    all_to_all x1, starting transfers between devices: 10.3 us -> 8.6 us  [on_device(): sums = lax.all_to_all(sums, ALL, 0, 0)]
    ppermute x6, waiting for transfers between devices: 17.9 us -> 17 us  [swap(): lax.ppermute(two, axis, pairs(count, 1))]
    pallas_call x5 -> x6, Pallas kernels: 3.88 us -> 4.45 us  [the longest x1 1.22 us: on_device(): kernel_call(y_add, shape(CX, CY, LANES), n_in=6, in_smem=1)]
    unnamed x10 -> x11, local copies, waits for them, and re-layouts: 1.57 us -> 1.58 us
  transfers between devices with their start and end apart: 13 -> 13, of which waited for: 5 -> 5; matrix products, arithmetic and copies ran while one was open for 0% -> 0% of each run, Pallas kernels for 5% -> 7%
where the time goes in v2:
time: 74.1 us; the launch traced here: 73.4 us
  starting transfers between devices  38.5 us (52%)
  waiting for transfers between devices  17 us (23%)
  Pallas kernels  16 us (22%)
  local copies, waits for them, and re-layouts  1.58 us (2%)
    ppermute x6, starting transfers between devices, swap(): lax.ppermute(two, axis, pairs(count, 1))  23.6 us
    ppermute x6, waiting for transfers between devices, swap(): lax.ppermute(two, axis, pairs(count, 1))  17 us
    all_to_all x1, starting transfers between devices, on_device(): sums = lax.all_to_all(sums, ALL, 0, 0)  8.6 us
    pallas_call x1, Pallas kernels, on_device(): kernel_call(main_kernel, (shape(EX, EY, LANES), face, face, shape(peers,...  7.83 us
    ppermute x6, starting transfers between devices, swap(): lax.ppermute(one, axis, pairs(count, 0))  6.34 us
    pallas_call x1, Pallas kernels, on_device(): kernel_call(bands, (shape(V * CY, LANES, dtype=BF16), shape(2 * EY, LANES...  3.01 us
    unnamed x11, local copies, waits for them, and re-layouts  1.58 us
  transfers between devices with their start and end apart: 13, of which 5 were waited for; matrix products, arithmetic and copies ran while one was open for 0% of the time, Pallas kernels for 7%

profile of v2, /device:TPU:41, one launch (start us, length us, event | category | flops | bytes accessed | tf_op | source)
XLA Modules:
  0.0 73.4 jit_solution(13369287101814953189)
XLA Ops:
  0.0 0.0 copy-start.4
  0.0 0.1 pad_add_fusion.flag
  0.1 0.0 copy-start.2
  0.1 0.7 copy-done.2
  0.7 0.0 copy-start
  0.7 0.9 %copy-done = f32[16,16,128]{2,1,0:T(8,128)S(1)} copy-done((f32[16,16,128]{2,1,0:T(8,128)S(1)}, f32[16,16,128]{2,1,0:T(8,128)}, u32[]{:S(2)}) %copy-start) | copy-done | bytes 131096
  1.6 0.0 copy-start.3
  1.6 0.6 shard_map.46
  2.2 1.3 %collective-permute-start = (f32[136,128]{1,0:T(8,128)S(1)}, f32[136,128]{1,0:T(8,128)S(1)}, u32[]{:S(2)}, u32[]{:S(2)}) collective-permute-start(f32[136,128]{1,0:T(8,128)S(1)} %get-tuple-element.31), channel_id=1, source_target_pairs={{0,4},{4,0},{8,12},{12,8},{16,20},{20,16},{24,28},{28,24},{1,5},{5... | collective-permute-start | bytes 208904 | tf_op jit(solution)/shard_map/ppermute | solution.py:27
  3.5 3.3 %collective-permute-start.1 = (f32[136,128]{1,0:T(8,128)S(1)}, f32[136,128]{1,0:T(8,128)S(1)}, u32[]{:S(2)}, u32[]{:S(2)}) collective-permute-start(f32[136,128]{1,0:T(8,128)S(1)} %get-tuple-element.32), channel_id=1, source_target_pairs={{4,8},{8,4},{12,16},{16,12},{20,24},{24,20},{5,9},{9,5},{13,17},{1... | collective-permute-start | bytes 208904 | tf_op jit(solution)/shard_map/ppermute | solution.py:27
  6.8 0.0 collective-permute-done.y1
  6.8 3.9 %collective-permute-done.1.y2 = f32[136,128]{1,0:T(8,128)S(1)} collective-permute-done((f32[136,128]{1,0:T(8,128)S(1)}, f32[136,128]{1,0:T(8,128)S(1)}, u32[]{:S(2)}, u32[]{:S(2)}) %collective-permute-start.1) | collective-permute-done | bytes 69664 | tf_op jit(solution)/shard_map/ppermute | solution.py:27
  10.7 0.6 shard_map.47
  11.3 2.2 %collective-permute-start.2 = (f32[264,128]{1,0:T(8,128)S(1)}, f32[264,128]{1,0:T(8,128)S(1)}, u32[]{:S(2)}, u32[]{:S(2)}) collective-permute-start(f32[264,128]{1,0:T(8,128)S(1)} %get-tuple-element.35), channel_id=1, source_target_pairs={{0,32},{32,0},{64,96},{96,64},{1,33},{33,1},{65,97},{97,65},{2,34}... | collective-permute-start | bytes 405512 | tf_op jit(solution)/shard_map/ppermute | solution.py:27
  13.4 4.6 %collective-permute-start.3 = (f32[264,128]{1,0:T(8,128)S(1)}, f32[264,128]{1,0:T(8,128)S(1)}, u32[]{:S(2)}, u32[]{:S(2)}) collective-permute-start(f32[264,128]{1,0:T(8,128)S(1)} %get-tuple-element.36), channel_id=1, source_target_pairs={{32,64},{64,32},{33,65},{65,33},{34,66},{66,34},{35,67},{67,35},{3... | collective-permute-start | bytes 405512 | tf_op jit(solution)/shard_map/ppermute | solution.py:27
  18.1 0.0 collective-permute-done.2.x1
  18.1 3.2 %collective-permute-done.3.x2 = f32[264,128]{1,0:T(8,128)S(1)} collective-permute-done((f32[264,128]{1,0:T(8,128)S(1)}, f32[264,128]{1,0:T(8,128)S(1)}, u32[]{:S(2)}, u32[]{:S(2)}) %collective-permute-start.3) | collective-permute-done | bytes 135200 | tf_op jit(solution)/shard_map/ppermute | solution.py:27
  21.3 0.7 %shard_map.48 = (f32[32,32,128]{2,1,0:T(8,128)S(1)}, f32[16,128]{1,0:T(8,128)S(1)}, f32[8,1280]{1,0:T(8,128)S(1)}, f32[8,1280]{1,0:T(8,128)S(1)}) custom-call(s32[3]{0:T(128)S(1)} %pad_add_fusion.flag, f32[16,32,128]{2,1,0:T(8,128)S(1)} %get-tuple-element.33.fy, f32[8,128]{1,0:T(8,128)S(1)} %get-tuple-element.34.wy, ...), custom_call_target="tpu_custom_call" | custom-call | bytes 1024 | tf_op jit(solution)/shard_map/pallas_call | solution.py:394
  22.0 0.2 collective-permute-start.4
  22.3 4.0 %collective-permute-start.5 = (f32[8,1280]{1,0:T(8,128)S(1)}, f32[8,1280]{1,0:T(8,128)S(1)}, u32[]{:S(2)}, u32[]{:S(2)}) collective-permute-start(f32[8,1280]{1,0:T(8,128)S(1)} %get-tuple-element.40), channel_id=1, source_target_pairs={{1,2},{2,1},{5,6},{6,5},{9,10},{10,9},{13,14},{14,13},{17,18},{18,... | collective-permute-start | bytes 122888 | tf_op jit(solution)/shard_map/ppermute | solution.py:27
  26.3 0.0 copy-done.4
  26.3 3.0 %shard_map.49 = (bf16[128,128]{1,0:T(8,128)(2,1)S(1)}, f32[64,128]{1,0:T(8,128)S(1)}, bf16[8,256,128]{2,1,0:T(8,128)(2,1)S(1)}, bf16[8,256,128]{2,1,0:T(8,128)(2...) custom-call(f32[8,3,17]{2,1,0:T(4,128)S(1)} %copy.6.taps), custom_call_target="tpu_custom_call" | custom-call | flops 200000000 | bytes 1024 | tf_op jit(solution)/shard_map/pallas_call | solution.py:374
  29.3 0.0 collective-permute-done.4.z1
  29.3 0.0 collective-permute-done.5.z2
  29.4 0.0 copy-done.3
  29.4 7.8 %shard_map.50 = (f32[32,32,128]{2,1,0:T(8,128)S(1)}, f32[8,1024]{1,0:T(8,128)S(1)}, f32[8,1024]{1,0:T(8,128)S(1)}, f32[128,8,128]{2,1,0:T(8,128)}) custom-call(s32[3]{0:T(128)S(1)} %pad_add_fusion.flag, f32[8,3,17]{2,1,0:T(4,128)S(1)} %copy.6.taps, s32[8]{0:T(128)S(1)} %bitcast.6, f32[32,32,128]{2,1,0:T(8,128)S(1)} %get-tuple-element.37.field, ...), custom_call_target="tpu_custom_call" | custom-call | flops 2000000000 | bytes 1024 | tf_op jit(solution)/shard_map/pallas_call | solution.py:400
  37.2 8.6 %all-to-all-start = ((f32[128,8,128]{2,1,0:T(8,128)}), f32[128,8,128]{2,1,0:T(8,128)S(1)}, u32[]{:S(2)}, u32[]{:S(2)}) async-start(f32[128,8,128]{2,1,0:T(8,128)} %get-tuple-element.56), calls=%async_computation | async-start | bytes 1048576 | tf_op jit(solution)/shard_map/all_to_all | solution.py:420
  45.8 0.3 collective-permute-start.6
  46.1 3.9 %collective-permute-start.7 = (f32[8,1024]{1,0:T(8,128)S(1)}, f32[8,1024]{1,0:T(8,128)S(1)}, u32[]{:S(2)}, u32[]{:S(2)}) collective-permute-start(f32[8,1024]{1,0:T(8,128)S(1)} %get-tuple-element.49), channel_id=1, source_target_pairs={{1,2},{2,1},{5,6},{6,5},{9,10},{10,9},{13,14},{14,13},{17,18},{18,... | collective-permute-start | bytes 98312 | tf_op jit(solution)/shard_map/ppermute | solution.py:27
  50.0 0.0 collective-permute-done.6.r1
  50.0 3.5 %collective-permute-done.7.r2 = f32[8,1024]{1,0:T(8,128)S(1)} collective-permute-done((f32[8,1024]{1,0:T(8,128)S(1)}, f32[8,1024]{1,0:T(8,128)S(1)}, u32[]{:S(2)}, u32[]{:S(2)}) %collective-permute-start.7) | collective-permute-done | bytes 32800 | tf_op jit(solution)/shard_map/ppermute | solution.py:27
  53.5 0.7 %shard_map.51 = (f32[16,32,128]{2,1,0:T(8,128)S(1)}, f32[256,128]{1,0:T(8,128)S(1)}, f32[256,128]{1,0:T(8,128)S(1)}) custom-call(s32[3]{0:T(128)S(1)} %pad_add_fusion.flag, f32[32,32,128]{2,1,0:T(8,128)S(1)} %get-tuple-element.47.part, f32[8,1024]{1,0:T(8,128)S(1)} %collective-permute-done.6.r1, f32[8,1024]{1,0:T(8,128)S(1)} %collective-permute-done.7.r2), custom_call_target="tpu_custom_call" | custom-call | bytes 1024 | tf_op jit(solution)/shard_map/pallas_call | solution.py:422
  54.2 1.3 %collective-permute-start.8 = (f32[256,128]{1,0:T(8,128)S(1)}, f32[256,128]{1,0:T(8,128)S(1)}, u32[]{:S(2)}, u32[]{:S(2)}) collective-permute-start(f32[256,128]{1,0:T(8,128)S(1)} %get-tuple-element.51), channel_id=1, source_target_pairs={{0,32},{32,0},{64,96},{96,64},{1,33},{33,1},{65,97},{97,65},{2,34}... | collective-permute-start | bytes 393224 | tf_op jit(solution)/shard_map/ppermute | solution.py:27
  55.6 4.1 %collective-permute-start.9 = (f32[256,128]{1,0:T(8,128)S(1)}, f32[256,128]{1,0:T(8,128)S(1)}, u32[]{:S(2)}, u32[]{:S(2)}) collective-permute-start(f32[256,128]{1,0:T(8,128)S(1)} %get-tuple-element.52), channel_id=1, source_target_pairs={{32,64},{64,32},{33,65},{65,33},{34,66},{66,34},{35,67},{67,35},{3... | collective-permute-start | bytes 393224 | tf_op jit(solution)/shard_map/ppermute | solution.py:27
  59.7 0.0 collective-permute-done.8.r1
  59.7 3.6 %collective-permute-done.9.r2 = f32[256,128]{1,0:T(8,128)S(1)} collective-permute-done((f32[256,128]{1,0:T(8,128)S(1)}, f32[256,128]{1,0:T(8,128)S(1)}, u32[]{:S(2)}, u32[]{:S(2)}) %collective-permute-start.9) | collective-permute-done | bytes 131104 | tf_op jit(solution)/shard_map/ppermute | solution.py:27
  63.4 0.6 shard_map.52
  63.9 1.0 %collective-permute-start.10 = (f32[128,128]{1,0:T(8,128)S(1)}, f32[128,128]{1,0:T(8,128)S(1)}, u32[]{:S(2)}, u32[]{:S(2)}) collective-permute-start(f32[128,128]{1,0:T(8,128)S(1)} %get-tuple-element.54), channel_id=1, source_target_pairs={{0,4},{4,0},{8,12},{12,8},{16,20},{20,16},{24,28},{28,24},{1,5},{5... | collective-permute-start | bytes 196616 | tf_op jit(solution)/shard_map/ppermute | solution.py:27
  64.9 0.0 copy-start.1
  64.9 3.7 %collective-permute-start.11 = (f32[128,128]{1,0:T(8,128)S(1)}, f32[128,128]{1,0:T(8,128)S(1)}, u32[]{:S(2)}, u32[]{:S(2)}) collective-permute-start(f32[128,128]{1,0:T(8,128)S(1)} %get-tuple-element.55), channel_id=1, source_target_pairs={{4,8},{8,4},{12,16},{16,12},{20,24},{24,20},{5,9},{9,5},{13,17},{1... | collective-permute-start | bytes 196616 | tf_op jit(solution)/shard_map/ppermute | solution.py:27
  68.6 0.0 all-to-all-done.sums
  68.6 0.8 %shard_map.53.scale = f32[8,128]{1,0:T(8,128)S(1)} custom-call(s32[8]{0:T(128)S(1)} %bitcast.7, f32[128,8,128]{2,1,0:T(8,128)S(1)} %all-to-all-done.sums), custom_call_target="tpu_custom_call" | custom-call | flops 1000000 | bytes 1024 | tf_op jit(solution)/shard_map/pallas_call | solution.py:426
  69.4 0.0 collective-permute-done.10.r1
  69.4 2.8 %collective-permute-done.11.r2 = f32[128,128]{1,0:T(8,128)S(1)} collective-permute-done((f32[128,128]{1,0:T(8,128)S(1)}, f32[128,128]{1,0:T(8,128)S(1)}, u32[]{:S(2)}, u32[]{:S(2)}) %collective-permute-start.11) | collective-permute-done | bytes 65568 | tf_op jit(solution)/shard_map/ppermute | solution.py:27
  72.1 0.0 copy-done.1
  72.2 1.2 %shard_map.54 = f32[16,16,128]{2,1,0:T(8,128)} custom-call(s32[3]{0:T(128)S(1)} %pad_add_fusion.flag, f32[16,16,128]{2,1,0:T(8,128)S(1)} %get-tuple-element.53.part, f32[128,128]{1,0:T(8,128)S(1)} %collective-permute-done.10.r1, f32[128,128]{1,0:T(8,128)S(1)} %collective-permute-done.11.r2, f32[16,16,128]{2,1,0:T(8,128)S(1)} %copy-done.1, ...), custom_call_target="tpu_custom_call" | custom-call | bytes 1024 | tf_op jit(solution)/shard_map/pallas_call | solution.py:432
  (1 shorter events, 0.0 us)
Async XLA Ops:
  0.0 26.3 %copy-start.4 = (f32[8,3,17]{2,0,1:T(8,128)S(1)}, f32[8,3,17]{2,0,1:T(8,128)}, u32[]{:S(2)}) copy-start(f32[8,3,17]{2,0,1:T(8,128)} %param.7) | copy-start | bytes 4900
  0.1 0.7 copy-start.2
  0.7 0.9 %copy-start = (f32[16,16,128]{2,1,0:T(8,128)S(1)}, f32[16,16,128]{2,1,0:T(8,128)}, u32[]{:S(2)}) copy-start(f32[16,16,128]{2,1,0:T(8,128)} %est.5) | copy-start | bytes 393220
  1.6 27.7 %copy-start.3 = (f32[8,16,16,128]{3,2,1,0:T(8,128)S(1)}, f32[8,16,16,128]{3,2,1,0:T(8,128)}, u32[]{:S(2)}) copy-start(f32[8,16,16,128]{3,2,1,0:T(8,128)} %observed.1) | copy-start | bytes 3145732
  2.2 4.6 %collective-permute-start = (f32[136,128]{1,0:T(8,128)S(1)}, f32[136,128]{1,0:T(8,128)S(1)}, u32[]{:S(2)}, u32[]{:S(2)}) collective-permute-start(f32[136,128]{1,0:T(8,128)S(1)} %get-tuple-element.31), channel_id=1, source_target_pairs={{0,4},{4,0},{8,12},{12,8},{16,20},{20,16},{24,28},{28,24},{1,5},{5... | collective-permute-start | bytes 208904 | tf_op jit(solution)/shard_map/ppermute | solution.py:27
  3.5 7.2 %collective-permute-start.1 = (f32[136,128]{1,0:T(8,128)S(1)}, f32[136,128]{1,0:T(8,128)S(1)}, u32[]{:S(2)}, u32[]{:S(2)}) collective-permute-start(f32[136,128]{1,0:T(8,128)S(1)} %get-tuple-element.32), channel_id=1, source_target_pairs={{4,8},{8,4},{12,16},{16,12},{20,24},{24,20},{5,9},{9,5},{13,17},{1... | collective-permute-start | bytes 208904 | tf_op jit(solution)/shard_map/ppermute | solution.py:27
  11.3 6.8 %collective-permute-start.2 = (f32[264,128]{1,0:T(8,128)S(1)}, f32[264,128]{1,0:T(8,128)S(1)}, u32[]{:S(2)}, u32[]{:S(2)}) collective-permute-start(f32[264,128]{1,0:T(8,128)S(1)} %get-tuple-element.35), channel_id=1, source_target_pairs={{0,32},{32,0},{64,96},{96,64},{1,33},{33,1},{65,97},{97,65},{2,34}... | collective-permute-start | bytes 405512 | tf_op jit(solution)/shard_map/ppermute | solution.py:27
  13.4 7.8 %collective-permute-start.3 = (f32[264,128]{1,0:T(8,128)S(1)}, f32[264,128]{1,0:T(8,128)S(1)}, u32[]{:S(2)}, u32[]{:S(2)}) collective-permute-start(f32[264,128]{1,0:T(8,128)S(1)} %get-tuple-element.36), channel_id=1, source_target_pairs={{32,64},{64,32},{33,65},{65,33},{34,66},{66,34},{35,67},{67,35},{3... | collective-permute-start | bytes 405512 | tf_op jit(solution)/shard_map/ppermute | solution.py:27
  22.0 7.3 %collective-permute-start.4 = (f32[8,1280]{1,0:T(8,128)S(1)}, f32[8,1280]{1,0:T(8,128)S(1)}, u32[]{:S(2)}, u32[]{:S(2)}) collective-permute-start(f32[8,1280]{1,0:T(8,128)S(1)} %get-tuple-element.39), channel_id=1, source_target_pairs={{0,1},{1,0},{2,3},{3,2},{4,5},{5,4},{6,7},{7,6},{8,9},{9,8},{10,11... | collective-permute-start | bytes 122888 | tf_op jit(solution)/shard_map/ppermute | solution.py:27
  22.3 7.1 %collective-permute-start.5 = (f32[8,1280]{1,0:T(8,128)S(1)}, f32[8,1280]{1,0:T(8,128)S(1)}, u32[]{:S(2)}, u32[]{:S(2)}) collective-permute-start(f32[8,1280]{1,0:T(8,128)S(1)} %get-tuple-element.40), channel_id=1, source_target_pairs={{1,2},{2,1},{5,6},{6,5},{9,10},{10,9},{13,14},{14,13},{17,18},{18,... | collective-permute-start | bytes 122888 | tf_op jit(solution)/shard_map/ppermute | solution.py:27
  37.2 31.4 %all-to-all-start = ((f32[128,8,128]{2,1,0:T(8,128)}), f32[128,8,128]{2,1,0:T(8,128)S(1)}, u32[]{:S(2)}, u32[]{:S(2)}) async-start(f32[128,8,128]{2,1,0:T(8,128)} %get-tuple-element.56), calls=%async_computation | async-start | bytes 1048576 | tf_op jit(solution)/shard_map/all_to_all | solution.py:420
  45.8 4.2 %collective-permute-start.6 = (f32[8,1024]{1,0:T(8,128)S(1)}, f32[8,1024]{1,0:T(8,128)S(1)}, u32[]{:S(2)}, u32[]{:S(2)}) collective-permute-start(f32[8,1024]{1,0:T(8,128)S(1)} %get-tuple-element.48), channel_id=1, source_target_pairs={{0,1},{1,0},{2,3},{3,2},{4,5},{5,4},{6,7},{7,6},{8,9},{9,8},{10,11... | collective-permute-start | bytes 98312 | tf_op jit(solution)/shard_map/ppermute | solution.py:27
  46.1 7.4 %collective-permute-start.7 = (f32[8,1024]{1,0:T(8,128)S(1)}, f32[8,1024]{1,0:T(8,128)S(1)}, u32[]{:S(2)}, u32[]{:S(2)}) collective-permute-start(f32[8,1024]{1,0:T(8,128)S(1)} %get-tuple-element.49), channel_id=1, source_target_pairs={{1,2},{2,1},{5,6},{6,5},{9,10},{10,9},{13,14},{14,13},{17,18},{18,... | collective-permute-start | bytes 98312 | tf_op jit(solution)/shard_map/ppermute | solution.py:27
  54.2 5.5 %collective-permute-start.8 = (f32[256,128]{1,0:T(8,128)S(1)}, f32[256,128]{1,0:T(8,128)S(1)}, u32[]{:S(2)}, u32[]{:S(2)}) collective-permute-start(f32[256,128]{1,0:T(8,128)S(1)} %get-tuple-element.51), channel_id=1, source_target_pairs={{0,32},{32,0},{64,96},{96,64},{1,33},{33,1},{65,97},{97,65},{2,34}... | collective-permute-start | bytes 393224 | tf_op jit(solution)/shard_map/ppermute | solution.py:27
  55.6 7.8 %collective-permute-start.9 = (f32[256,128]{1,0:T(8,128)S(1)}, f32[256,128]{1,0:T(8,128)S(1)}, u32[]{:S(2)}, u32[]{:S(2)}) collective-permute-start(f32[256,128]{1,0:T(8,128)S(1)} %get-tuple-element.52), channel_id=1, source_target_pairs={{32,64},{64,32},{33,65},{65,33},{34,66},{66,34},{35,67},{67,35},{3... | collective-permute-start | bytes 393224 | tf_op jit(solution)/shard_map/ppermute | solution.py:27
  63.9 5.4 %collective-permute-start.10 = (f32[128,128]{1,0:T(8,128)S(1)}, f32[128,128]{1,0:T(8,128)S(1)}, u32[]{:S(2)}, u32[]{:S(2)}) collective-permute-start(f32[128,128]{1,0:T(8,128)S(1)} %get-tuple-element.54), channel_id=1, source_target_pairs={{0,4},{4,0},{8,12},{12,8},{16,20},{20,16},{24,28},{28,24},{1,5},{5... | collective-permute-start | bytes 196616 | tf_op jit(solution)/shard_map/ppermute | solution.py:27
  64.9 7.2 %copy-start.1 = (f32[16,16,128]{2,1,0:T(8,128)S(1)}, f32[16,16,128]{2,1,0:T(8,128)}, u32[]{:S(2)}) copy-start(f32[16,16,128]{2,1,0:T(8,128)} %est.5) | copy-start | bytes 393220
  64.9 7.2 %collective-permute-start.11 = (f32[128,128]{1,0:T(8,128)S(1)}, f32[128,128]{1,0:T(8,128)S(1)}, u32[]{:S(2)}, u32[]{:S(2)}) collective-permute-start(f32[128,128]{1,0:T(8,128)S(1)} %get-tuple-element.55), channel_id=1, source_target_pairs={{4,8},{8,4},{12,16},{16,12},{20,24},{24,20},{5,9},{9,5},{13,17},{1... | collective-permute-start | bytes 196616 | tf_op jit(solution)/shard_map/ppermute | solution.py:27

commit v3 on v2

--- a/solution.py
+++ b/solution.py
@@ -97,13 +97,18 @@
     ws[3:6] = wy[:3]
     ws[6:9] = above[cells : cells + 3]
     turned = jnp.transpose(field[...].reshape(ROWS, LANES))
-    low, high = turned[:R], turned[CZ - R :]
-    op1[:, :ROWS] = jnp.where(odd_z, low, high)
-    op2[:, :ROWS] = jnp.where(odd_z, high, low)
-    for b in range(2):
-        cols = slice(ROWS + b * LANES, ROWS + (b + 1) * LANES)
-        op1[:, cols] = ws[b * 8 : b * 8 + 8]
-        op2[:, cols] = ws[b * 8 : b * 8 + 8]
+    low, high = turned[: 2 * R], turned[CZ - 2 * R :]
+    op1[...] = jnp.where(odd_z, low, high)
+    op2[...] = jnp.where(odd_z, high, low)
+
+
+def image_pack(flag, observed, op1, op2):
+    odd = flag[2] == 1
+    for v in range(V):
+        turned = jnp.transpose(observed[v].reshape(CX * CY, LANES))
+        low, high = turned[:R], turned[CZ - R :]
+        op1[v * R : (v + 1) * R, :] = jnp.where(odd, low, high)
+        op2[v * R : (v + 1) * R, :] = jnp.where(odd, high, low)
 
 
 def total_of(x):
@@ -133,7 +138,7 @@
     return 1.0 / jnp.full((8, LANES), total, F32)[:1]
 
 
-def bands(taps, by, byt, wz1, wz2, tz1, tz2):
+def bands(taps, by, byt, wz1, wz2, tz1, tz2, tz3, tx):
     for v in range(V):
         rows = slice(v * CY, (v + 1) * CY)
         scale = inverse_sum(taps, v, 0) * inverse_sum(taps, v, 1)
@@ -153,32 +158,47 @@
     byt[:EY, :] = high.astype(F32)
     byt[EY:, :] = low.astype(F32)
 
+    owner = iota((8, LANES), 1) // (2 * R)
+    for k in range(K):
+        row = jnp.zeros((8, LANES), F32)
+        for v in range(V):
+            row = jnp.where(owner == v, taps[v, 0, k], row)
+        tx[k : k + 1, :] = row[:1]
+    tx[K:, :] = jnp.zeros((24 - K, LANES), F32)
+
     def z_of(v, carry):
         scale = inverse_sum(taps, v, 2)
         row, col = iota((LANES, LANES), 0), iota((LANES, LANES), 1)
-        high, low = split(pick(taps, v, 2, row + R - col, scale))
-        wz1[v, :LANES, :] = high
-        wz1[v, LANES:, :] = high
-        wz2[v, :LANES, :] = low
-        place = row[: 6 * R] % (2 * R)
-        near = jnp.where(place < R, place, place + CZ)
-        got = pick(taps, v, 2, near - col[: 6 * R], scale)
-        high, low = split(got)
-        which = row[: 6 * R] < 4 * R
-        wz2[v, LANES : LANES + 6 * R, :] = jnp.where(
-            which, high.astype(F32), low.astype(F32)
-        ).astype(BF16)
-        wz2[v, LANES + 6 * R :, :] = jnp.zeros((LANES - 6 * R, LANES), BF16)
-        high, low = split(pick(taps, v, 2, col + R - row, scale))
-        tz1[v, :LANES, :LANES] = high
-        tz1[v, LANES:, :LANES] = high
-        tz2[v, :, :LANES] = low
-        near = jnp.where(col < R, col, col + CZ)
-        got = jnp.where(col < 2 * R, pick(taps, v, 2, near - row, scale), 0.0)
-        high, low = split(got)
-        tz1[v, :LANES, LANES:] = high
-        tz1[v, LANES:, LANES:] = high
-        tz2[v, :, LANES:] = low
+
+        def slot(lane):
+            place = lane - 2 * R * v
+            z = jnp.where(place < R, place - R, place - R + CZ)
+            return jnp.where((place >= 0) & (place < 2 * R), z, 4 * CZ)
+
+        def past(lane):
+            return jnp.where(lane < 2 * R, lane - 2 * R, lane - 2 * R + CZ)
+
+        ends = row[: 12 * R]
+        z_end = past(ends % (4 * R))
+        first = ends < 8 * R
+        for half, z_out in ((slice(0, LANES), col), (slice(LANES, 2 * LANES), slot(col))):
+            high, low = split(pick(taps, v, 2, row - z_out + R, scale))
+            wz1[v, :LANES, half] = high
+            wz1[v, LANES:, half] = high
+            wz2[v, :LANES, half] = low
+            high, low = split(pick(taps, v, 2, z_end - z_out[: 12 * R] + R, scale))
+            wz2[v, LANES : LANES + 12 * R, half] = jnp.where(
+                first, high.astype(F32), low.astype(F32)
+            ).astype(BF16)
+            wz2[v, LANES + 12 * R :, half] = jnp.zeros((LANES - 12 * R, LANES), BF16)
+        high, low = split(pick(taps, v, 2, col - row + R, scale))
+        tz1[v, :LANES, :] = high
+        tz1[v, LANES:, :] = high
+        tz2[v, :LANES, :] = low
+        high, low = split(pick(taps, v, 2, col - slot(row) + R, scale))
+        tz2[v, LANES:, :] = high
+        tz3[v, :LANES, :] = low
+        tz3[v, LANES:, :] = high
         return carry
 
     lax.fori_loop(0, V, z_of, 0)
@@ -188,41 +208,36 @@
 
 
 def main_kernel(
-    flag, taps, cover, field, w9, z1, z2, observed, by, byt, wz1, wz2, tz1, tz2,
-    part, op1, op2, sums,
-    et, gs, hs, xs, ys, wy, edge, edges, ws,
+    flag, taps, cover, field, w9, z1, z2, i1, i2, observed, by, byt, wz1, wz2, tz1, tz2, tz3, tx,
+    mid, op1, op2, sums,
+    et, image_e, gs, hs, hp, xs, xe, pe, ys, wy, part,
 ):
-    odd_z = flag[2] == 1
+    odd_x, odd_z = flag[0] == 1, flag[2] == 1
     one, two = z1[...], z2[...]
     below, above = jnp.where(odd_z, one, two), jnp.where(odd_z, two, one)
-    for b in range(2):
-        cols = slice(ROWS + b * LANES, ROWS + (b + 1) * LANES)
-        ws[b * 8 : b * 8 + 8] = below[:, cols]
-        ws[32 + b * 8 : 40 + b * 8] = above[:, cols]
-    ws[16:32] = w9[...]
-
-    edges[:R] = below[:, :ROWS]
-    edges[R:] = above[:, :ROWS]
-    e = edges[...]
+    e = jnp.concatenate([below, above], axis=0)
     et[...] = jnp.transpose(
-        jnp.concatenate([e, e, e, jnp.zeros((LANES - 6 * R, ROWS), F32)], axis=0)
+        jnp.concatenate([e, e, e, jnp.zeros((LANES - 12 * R, ROWS), F32)], axis=0)
     )
+    one, two = i1[...], i2[...]
+    below, above = jnp.where(odd_z, one, two), jnp.where(odd_z, two, one)
+    rows_e = []
+    for v in range(V):
+        rows_e += [below[v * R : (v + 1) * R], above[v * R : (v + 1) * R]]
+    image_e[...] = jnp.transpose(jnp.concatenate(rows_e, axis=0)).reshape(CX, CY, LANES)
 
     for bx in range(3):
-        for zb in range(3):
-            for j in range(3):
-                at = zb * 16 + bx * 3 + j
-                w_row = ws[at : at + 1, :]
-                for q in range(BANDS[j][0], BANDS[j][1], 8):
-                    rows = slice(zb * EY + q, zb * EY + q + 8)
-                    high = w_row * byt[q : q + 8]
-                    low = w_row * byt[EY + q : EY + q + 8]
-                    wy[bx, rows, :LANES] = high
-                    wy[bx, rows, LANES : 2 * LANES] = high
-                    wy[bx, rows, 2 * LANES :] = low
+        for j in range(3):
+            w_row = w9[bx * 3 + j : bx * 3 + j + 1, :]
+            for q in range(BANDS[j][0], BANDS[j][1], 8):
+                rows = slice(q, q + 8)
+                high = w_row * byt[q : q + 8]
+                wy[bx, rows, :LANES] = high
+                wy[bx, rows, LANES : 2 * LANES] = high
+                wy[bx, rows, 2 * LANES :] = w_row * byt[EY + q : EY + q + 8]
 
     face = iota((LANES, LANES), 1)
-    face_low = (face >= 2 * R) & (face < 4 * R)
+    face_low = (face >= 4 * R) & (face < 8 * R)
     lhs = by[:, : 3 * EY]
     for x in range(EX):
         high, low = split(field[x])
@@ -238,14 +253,37 @@
         both = jnp.where(face_low, e_got - e_high, e_high).astype(BF16)
         gs[:, x, :, 2 * LANES :] = both.reshape(V, CY, LANES)
 
-    lane = iota((8, LANES), 1)
-    seen = jnp.zeros((8, LANES), F32)
     for v in range(V):
         block = gs[v].reshape(EX * CY, 3 * LANES)
         got = jnp.dot(block[:, : 2 * LANES], wz1[v], preferred_element_type=F32)
         second = jnp.concatenate([block[:, :LANES], block[:, 2 * LANES :]], axis=1)
         got += jnp.dot(second, wz2[v], preferred_element_type=F32)
-        hs[v] = got.reshape(EX, CY, LANES)
+        hs[v] = got[:, :LANES].reshape(EX, CY, LANES)
+        ends = got[:, LANES:].reshape(EX, CY, LANES)
+        if v == 0:
+            hp[...] = ends
+        else:
+            hp[...] += ends
+
+    for b in range(0, CY, 8):
+        rows = slice(b, b + 8)
+        for a in range(CX):
+            acc = tx[0:1, :] * hp[a, rows]
+            for k in range(1, K):
+                acc += tx[k : k + 1, :] * hp[a + k, rows]
+            xe[a, rows] = image_e[a, rows] / acc
+    for i in range(EX):
+        acc = None
+        for a in range(max(0, i - K + 1), min(CX, i + 1)):
+            term = tx[i - a : i - a + 1, :] * xe[a]
+            acc = term if acc is None else acc + term
+        high, low = split(acc)
+        pe[i, :, :LANES] = high
+        pe[i, :, LANES:] = low
+
+    lane = iota((8, LANES), 1)
+    seen = jnp.zeros((8, LANES), F32)
+    packed = pe[...].reshape(EX * CY, 2 * LANES)
     for v in range(V):
         t = [taps[v, 0, k] for k in range(K)]
         own = cover[v].astype(F32)
@@ -268,69 +306,47 @@
             gs[v, i, :, LANES : 2 * LANES] = low
         block = gs[v].reshape(EX * CY, 3 * LANES)
         got = jnp.dot(block[:, : 2 * LANES], tz1[v], preferred_element_type=F32)
-        got += jnp.dot(block[:, :LANES], tz2[v], preferred_element_type=F32)
-        high, low = split(got)
-        ys[:, v * CY : (v + 1) * CY, :] = high.reshape(EX, CY, 2 * LANES)
-        ys[:, (V + v) * CY : (V + v + 1) * CY, :] = low.reshape(EX, CY, 2 * LANES)
-
-    sub = iota((EY, LANES), 1)
-    for x in range(EX):
+        second = jnp.concatenate([block[:, :LANES], packed[:, :LANES]], axis=1)
+        got += jnp.dot(second, tz2[v], preferred_element_type=F32)
+        got += jnp.dot(packed, tz3[v], preferred_element_type=F32)
+        for q, piece in enumerate(split(got)):
+            piece = piece.reshape(EX // 2, 2, CY, LANES)
+            rows = slice((q * V + v) * CY, (q * V + v + 1) * CY)
+            ys[:, rows, :LANES] = piece[:, 0]
+            ys[:, rows, LANES:] = piece[:, 1]
+
+    for x in range(0, EX, 2):
         bx = 0 if x < R else (1 if x < R + CX else 2)
-        got = jnp.dot(wy[bx, :, : 2 * LANES].astype(BF16), ys[x], preferred_element_type=F32)
+        got = jnp.dot(
+            wy[bx, :, : 2 * LANES].astype(BF16), ys[x // 2], preferred_element_type=F32
+        )
         got += jnp.dot(
-            wy[bx, :, 2 * LANES :].astype(BF16), ys[x, : V * CY], preferred_element_type=F32
+            wy[bx, :, 2 * LANES :].astype(BF16), ys[x // 2, : V * CY], preferred_element_type=F32
         )
-        part[x] = got[EY : 2 * EY, :LANES]
-        edge[x * EY : (x + 1) * EY, :] = jnp.where(
-            sub < R, got[:EY, LANES:], got[2 * EY :, LANES:]
-        )
-
-    turned = jnp.transpose(edge[...])
-    low, high = turned[:R], turned[R : 2 * R]
-    op1[...] = jnp.where(odd_z, low, high)
-    op2[...] = jnp.where(odd_z, high, low)
-
-    def count_of(zb, at):
-        row = ws[zb * 16 + at : zb * 16 + at + 1, :]
+        part[x] = got[:, :LANES]
+        part[x + 1] = got[:, LANES:]
+
+    mid[...] = part[R : R + CX]
+    for i in range(R):
+        low, high = part[i], part[R + CX + i]
+        op1[i * EY : (i + 1) * EY, :] = jnp.where(odd_x, low, high)
+        op2[i * EY : (i + 1) * EY, :] = jnp.where(odd_x, high, low)
+
+    def count_of(at):
+        row = w9[at : at + 1, :]
         return jnp.maximum(jnp.sum(row, axis=1, keepdims=True) * (1.0 / CY), 1.0)
 
     total = jnp.zeros((8, LANES), F32)
-    place = iota((8, ROWS), 1) % EY
-    y_band = jnp.where(place < R, 0, jnp.where(place < R + CY, 1, 2))
-    low_sum = edges[:R] * low
-    high_sum = edges[R:] * high
     for bx in range(3):
         x0, x1 = BANDS[bx]
         for j in range(3):
             y0, y1 = BANDS[j]
-            at = bx * 3 + j
             block = (field[x0:x1, y0:y1] * part[x0:x1, y0:y1]).reshape((-1, 8, LANES))
-            total += jnp.sum(block, axis=0) / count_of(1, at)
-            lanes = slice(x0 * EY, x1 * EY)
-            picked = y_band[:, lanes] == j
-            for side, zb in ((low_sum, 0), (high_sum, 2)):
-                cut = jnp.where(picked, side[:, lanes], 0.0)
-                folded = cut[:, :LANES]
-                for q in range(1, cut.shape[1] // LANES):
-                    folded = folded + cut[:, q * LANES : (q + 1) * LANES]
-                total += folded / count_of(zb, at)
-    target = seen / count_of(1, 4)
-    both = jnp.where(lane < 64, total_of(target), total_of(total))
+            total += jnp.sum(block, axis=0) / count_of(bx * 3 + j)
+    target = seen / count_of(4)
+    both = jnp.where(lane < 64, total_of(target), total_of(total))[:4]
     for p in range(sums.shape[0]):
         sums[p] = both
-
-
-def z_add(flag, part, r1, r2, mid, op1, op2):
-    odd_x, odd_z = flag[0] == 1, flag[2] == 1
-    one, two = r1[...], r2[...]
-    below, above = jnp.where(odd_z, one, two), jnp.where(odd_z, two, one)
-    stacked = jnp.concatenate([below, jnp.zeros((CZ - 2 * R, ROWS), F32), above], axis=0)
-    added = jnp.transpose(stacked).reshape(EX, EY, LANES)
-    mid[...] = part[R : R + CX] + added[R : R + CX]
-    for i in range(R):
-        low, high = part[i] + added[i], part[R + CX + i] + added[R + CX + i]
-        op1[i * EY : (i + 1) * EY, :] = jnp.where(odd_x, low, high)
-        op2[i * EY : (i + 1) * EY, :] = jnp.where(odd_x, high, low)
 
 
 def x_add(flag, part, r1, r2, mid, op1, op2):
@@ -346,11 +362,11 @@
 
 
 def scale_of(cover, sums, scale):
-    gathered = jnp.sum(sums[...], axis=0)
-    lane = iota((8, LANES), 1)
+    gathered = jnp.sum(sums[...], axis=0)[:1]
+    lane = iota((1, LANES), 1)
     target = jnp.sum(jnp.where(lane == 0, gathered, 0.0), axis=1, keepdims=True)
     total = jnp.sum(jnp.where(lane == 64, gathered, 0.0), axis=1, keepdims=True)
-    count = jnp.sum(spread_cover(cover), axis=1, keepdims=True) * (1.0 / CY)
+    count = jnp.sum(spread_cover(cover)[:1], axis=1, keepdims=True) * (1.0 / CY)
     scale[...] = jnp.broadcast_to(target / total / count, (8, LANES))
 
 
@@ -371,15 +387,22 @@
     op = shape(R * CX + 8, LANES)
     y1, y2 = kernel_call(y_pack, (op, op), n_in=3, in_smem=2)(flag, cover, estimate)
     y1, y2 = swap(y1, y2, "by")
+    op = shape(V * R, CX * CY)
+    i1, i2 = kernel_call(image_pack, (op, op), n_in=2, in_smem=1, flops=10**7)(flag, observed)
+    i1, i2 = swap(i1, i2, "bz")
+    square = shape(V, 2 * LANES, LANES, dtype=BF16)
+    wide = shape(V, 2 * LANES, 2 * LANES, dtype=BF16)
     tables = kernel_call(
         bands,
         (
             shape(V * CY, LANES, dtype=BF16),
             shape(2 * EY, LANES),
-            shape(V, 2 * LANES, LANES, dtype=BF16),
-            shape(V, 2 * LANES, LANES, dtype=BF16),
-            shape(V, 2 * LANES, 2 * LANES, dtype=BF16),
-            shape(V, LANES, 2 * LANES, dtype=BF16),
+            wide,
+            wide,
+            square,
+            square,
+            square,
+            shape(24, LANES),
         ),
         n_in=1,
         in_smem=1,
@@ -390,39 +413,36 @@
         x_pack, (shape(CX, EY, LANES), shape(8, LANES), op, op), n_in=5, in_smem=2
     )(flag, cover, estimate, y1, y2)
     x1, x2 = swap(x1, x2, "bx")
-    op = shape(R, ROWS + 2 * LANES)
+    op = shape(2 * R, ROWS)
     field, w9, z1, z2 = kernel_call(
         z_pack, (shape(EX, EY, LANES), shape(16, LANES), op, op), n_in=5, in_smem=1
     )(flag, fy, wy, x1, x2)
     z1, z2 = swap(z1, z2, "bz")
 
-    face = shape(R, ROWS)
-    part, z1, z2, sums = kernel_call(
+    op = shape(EY * R, LANES)
+    part, x1, x2, sums = kernel_call(
         main_kernel,
-        (shape(EX, EY, LANES), face, face, shape(peers, 8, LANES)),
+        (shape(CX, EY, LANES), op, op, shape(peers, 4, LANES)),
         scratch=(
             pltpu.VMEM((ROWS, LANES), F32),
+            pltpu.VMEM((CX, CY, LANES), F32),
             pltpu.VMEM((V, EX, CY, 3 * LANES), BF16),
             pltpu.VMEM((V, EX, CY, LANES), F32),
+            pltpu.VMEM((EX, CY, LANES), F32),
             pltpu.VMEM((V, CX, CY, LANES), F32),
-            pltpu.VMEM((EX, 2 * V * CY, 2 * LANES), BF16),
-            pltpu.VMEM((3, 3 * EY, 3 * LANES), F32),
-            pltpu.VMEM((ROWS, LANES), F32),
-            pltpu.VMEM((2 * R, ROWS), F32),
-            pltpu.VMEM((48, LANES), F32),
+            pltpu.VMEM((CX, CY, LANES), F32),
+            pltpu.VMEM((EX, CY, 2 * LANES), BF16),
+            pltpu.VMEM((EX // 2, 2 * V * CY, 2 * LANES), BF16),
+            pltpu.VMEM((3, EY, 3 * LANES), F32),
+            pltpu.VMEM((EX, EY, LANES), F32),
         ),
-        n_in=14,
+        n_in=18,
         in_smem=3,
         flops=2 * 10**9,
-    )(flag, psf_taps, cover, field, w9, z1, z2, observed, *tables)
-
-    z1, z2 = swap(z1, z2, "bz")
+    )(flag, psf_taps, cover, field, w9, z1, z2, i1, i2, observed, *tables)
+
+    x1, x2 = swap(x1, x2, "bx")
     sums = lax.all_to_all(sums, ALL, 0, 0)
-    op = shape(EY * R, LANES)
-    part, x1, x2 = kernel_call(z_add, (shape(CX, EY, LANES), op, op), n_in=4, in_smem=1)(
-        flag, part, z1, z2
-    )
-    x1, x2 = swap(x1, x2, "bx")
     scale = kernel_call(scale_of, shape(8, LANES), n_in=2, in_smem=1, flops=10**6)(cover, sums)
     op = shape(R * CX, LANES)
     part, y1, y2 = kernel_call(x_add, (shape(CX, CY, LANES), op, op), n_in=4, in_smem=1)(

time: 74.1 us -> 69.4 us (0.937)
  waiting for transfers between devices: 17 us -> 11.3 us
  starting transfers between devices: 38.5 us -> 33.8 us
  Pallas kernels: 16 us -> 19.5 us
  local copies, waits for them, and re-layouts: 1.58 us -> 3.8 us
    ppermute x6, waiting for transfers between devices: 17 us -> 11.3 us  [swap(): lax.ppermute(two, axis, pairs(count, 1))]
    pallas_call x1, Pallas kernels: 3.01 us -> 5.49 us  [on_device(): kernel_call(bands, (shape(V * CY, LANES, dtype=BF16), shape(2 * EY, LANES...]
    unnamed x11 -> x15, local copies, waits for them, and re-layouts: 1.58 us -> 3.8 us
    ppermute x6, starting transfers between devices: 23.6 us -> 21.7 us  [swap(): lax.ppermute(two, axis, pairs(count, 1))]
    all_to_all x1, starting transfers between devices: 8.6 us -> 7.02 us  [on_device(): sums = lax.all_to_all(sums, ALL, 0, 0)]
    ppermute x6, starting transfers between devices: 6.34 us -> 5.06 us  [swap(): lax.ppermute(one, axis, pairs(count, 0))]
    pallas_call x2, Pallas kernels: 8.57 us -> 9.54 us  [the longest x1 8.67 us: on_device(): kernel_call(main_kernel, (shape(CX, EY, LANES), op, op, shape(peers, 4, L...]
  transfers between devices with their start and end apart: 13 -> 13, of which waited for: 5 -> 3; matrix products, arithmetic and copies ran while one was open for 0% -> 0% of each run, Pallas kernels for 7% -> 12%
where the time goes in v3:
time: 69.4 us; the launch traced here: 68.6 us
  starting transfers between devices  33.8 us (49%)
  Pallas kernels  19.5 us (28%)
  waiting for transfers between devices  11.3 us (16%)
  local copies, waits for them, and re-layouts  3.8 us (5%)
    ppermute x6, starting transfers between devices, swap(): lax.ppermute(two, axis, pairs(count, 1))  21.7 us
    ppermute x6, waiting for transfers between devices, swap(): lax.ppermute(two, axis, pairs(count, 1))  11.3 us
    pallas_call x1, Pallas kernels, on_device(): kernel_call(main_kernel, (shape(CX, EY, LANES), op, op, shape(peers, 4, L...  8.67 us
    all_to_all x1, starting transfers between devices, on_device(): sums = lax.all_to_all(sums, ALL, 0, 0)  7.02 us
    pallas_call x1, Pallas kernels, on_device(): kernel_call(bands, (shape(V * CY, LANES, dtype=BF16), shape(2 * EY, LANES...  5.49 us
    ppermute x6, starting transfers between devices, swap(): lax.ppermute(one, axis, pairs(count, 0))  5.06 us
    unnamed x15, local copies, waits for them, and re-layouts  3.8 us
  transfers between devices with their start and end apart: 13, of which 3 were waited for; matrix products, arithmetic and copies ran while one was open for 0% of the time, Pallas kernels for 12%

profile of v3, /device:TPU:41, one launch (start us, length us, event | category | flops | bytes accessed | tf_op | source)
XLA Modules:
  0.0 68.6 jit_solution(10051797547914755806)
XLA Ops:
  0.0 0.1 pad_add_fusion.flag
  0.1 0.0 copy-start.4
  0.1 0.7 copy-done.4
  0.7 0.0 copy-start
  0.7 0.9 %copy-done = f32[16,16,128]{2,1,0:T(8,128)S(1)} copy-done((f32[16,16,128]{2,1,0:T(8,128)S(1)}, f32[16,16,128]{2,1,0:T(8,128)}, u32[]{:S(2)}) %copy-start) | copy-done | bytes 131096
  1.6 0.6 shard_map.46
  2.2 1.3 %collective-permute-start = (f32[136,128]{1,0:T(8,128)S(1)}, f32[136,128]{1,0:T(8,128)S(1)}, u32[]{:S(2)}, u32[]{:S(2)}) collective-permute-start(f32[136,128]{1,0:T(8,128)S(1)} %get-tuple-element.32), channel_id=1, source_target_pairs={{0,4},{4,0},{8,12},{12,8},{16,20},{20,16},{24,28},{28,24},{1,5},{5... | collective-permute-start | bytes 208904 | tf_op jit(solution)/shard_map/ppermute | solution.py:27
  3.5 3.3 %collective-permute-start.1 = (f32[136,128]{1,0:T(8,128)S(1)}, f32[136,128]{1,0:T(8,128)S(1)}, u32[]{:S(2)}, u32[]{:S(2)}) collective-permute-start(f32[136,128]{1,0:T(8,128)S(1)} %get-tuple-element.33), channel_id=1, source_target_pairs={{4,8},{8,4},{12,16},{16,12},{20,24},{24,20},{5,9},{9,5},{13,17},{1... | collective-permute-start | bytes 208904 | tf_op jit(solution)/shard_map/ppermute | solution.py:27
  6.8 0.0 collective-permute-done.y1
  6.8 3.9 %collective-permute-done.1.y2 = f32[136,128]{1,0:T(8,128)S(1)} collective-permute-done((f32[136,128]{1,0:T(8,128)S(1)}, f32[136,128]{1,0:T(8,128)S(1)}, u32[]{:S(2)}, u32[]{:S(2)}) %collective-permute-start.1) | collective-permute-done | bytes 69664 | tf_op jit(solution)/shard_map/ppermute | solution.py:27
  10.6 0.6 shard_map.47
  11.2 2.2 %collective-permute-start.2 = (f32[264,128]{1,0:T(8,128)S(1)}, f32[264,128]{1,0:T(8,128)S(1)}, u32[]{:S(2)}, u32[]{:S(2)}) collective-permute-start(f32[264,128]{1,0:T(8,128)S(1)} %get-tuple-element.36), channel_id=1, source_target_pairs={{0,32},{32,0},{64,96},{96,64},{1,33},{33,1},{65,97},{97,65},{2,34}... | collective-permute-start | bytes 405512 | tf_op jit(solution)/shard_map/ppermute | solution.py:27
  13.4 4.6 %collective-permute-start.3 = (f32[264,128]{1,0:T(8,128)S(1)}, f32[264,128]{1,0:T(8,128)S(1)}, u32[]{:S(2)}, u32[]{:S(2)}) collective-permute-start(f32[264,128]{1,0:T(8,128)S(1)} %get-tuple-element.37), channel_id=1, source_target_pairs={{32,64},{64,32},{33,65},{65,33},{34,66},{66,34},{35,67},{67,35},{3... | collective-permute-start | bytes 405512 | tf_op jit(solution)/shard_map/ppermute | solution.py:27
  18.0 0.0 copy-start.2
  18.1 1.2 %copy-done.2 = f32[8,16,16,128]{3,2,1,0:T(8,128)S(1)} copy-done((f32[8,16,16,128]{3,2,1,0:T(8,128)S(1)}, f32[8,16,16,128]{3,2,1,0:T(8,128)}, u32[]{:S(2)}) %copy-start.2) | copy-done | bytes 1048600
  19.3 0.0 copy-start.3
  19.3 0.9 %shard_map.49 = (f32[64,256]{1,0:T(8,128)S(1)}, f32[64,256]{1,0:T(8,128)S(1)}) custom-call(s32[3]{0:T(128)S(1)} %pad_add_fusion.flag, f32[8,16,16,128]{3,2,1,0:T(8,128)S(1)} %copy-done.2), custom_call_target="tpu_custom_call" | custom-call | flops 10000000 | bytes 1024 | tf_op jit(solution)/shard_map/pallas_call | solution.py:391
  20.2 0.2 collective-permute-start.6
  20.4 4.0 %collective-permute-start.7 = (f32[64,256]{1,0:T(8,128)S(1)}, f32[64,256]{1,0:T(8,128)S(1)}, u32[]{:S(2)}, u32[]{:S(2)}) collective-permute-start(f32[64,256]{1,0:T(8,128)S(1)} %get-tuple-element.43), channel_id=1, source_target_pairs={{1,2},{2,1},{5,6},{6,5},{9,10},{10,9},{13,14},{14,13},{17,18},{18,... | collective-permute-start | bytes 196616 | tf_op jit(solution)/shard_map/ppermute | solution.py:27
  24.4 0.0 collective-permute-done.2.x1
  24.4 0.0 collective-permute-done.3.x2
  24.5 0.0 copy-start.6
  24.5 0.7 %shard_map.48 = (f32[32,32,128]{2,1,0:T(8,128)S(1)}, f32[16,128]{1,0:T(8,128)S(1)}, f32[16,1024]{1,0:T(8,128)S(1)}, f32[16,1024]{1,0:T(8,128)S(1)}) custom-call(s32[3]{0:T(128)S(1)} %pad_add_fusion.flag, f32[16,32,128]{2,1,0:T(8,128)S(1)} %get-tuple-element.34.fy, f32[8,128]{1,0:T(8,128)S(1)} %get-tuple-element.35.wy, ...), custom_call_target="tpu_custom_call" | custom-call | bytes 1024 | tf_op jit(solution)/shard_map/pallas_call | solution.py:417
  25.2 0.1 collective-permute-start.4
  25.3 1.9 %collective-permute-start.5 = (f32[16,1024]{1,0:T(8,128)S(1)}, f32[16,1024]{1,0:T(8,128)S(1)}, u32[]{:S(2)}, u32[]{:S(2)}) collective-permute-start(f32[16,1024]{1,0:T(8,128)S(1)} %get-tuple-element.41), channel_id=1, source_target_pairs={{1,2},{2,1},{5,6},{6,5},{9,10},{10,9},{13,14},{14,13},{17,18},{18,... | collective-permute-start | bytes 196616 | tf_op jit(solution)/shard_map/ppermute | solution.py:27
  27.2 0.0 copy-done.6
  27.3 5.5 %shard_map.50 = (bf16[128,128]{1,0:T(8,128)(2,1)S(1)}, f32[64,128]{1,0:T(8,128)S(1)}, bf16[8,256,256]{2,1,0:T(8,128)(2,1)S(1)}, bf16[8,256,256]{2,1,0:T(8,128)(2...) custom-call(f32[8,3,17]{2,1,0:T(4,128)S(1)} %copy.6.taps), custom_call_target="tpu_custom_call" | custom-call | flops 200000000 | bytes 1024 | tf_op jit(solution)/shard_map/pallas_call | solution.py:395
  32.8 0.0 copy-start.5
  32.8 1.0 %copy-done.5 = bf16[8,256,256]{2,1,0:T(8,128)(2,1)} copy-done((bf16[8,256,256]{2,1,0:T(8,128)(2,1)}, bf16[8,256,256]{2,1,0:T(8,128)(2,1)S(1)}, u32[]{:S(2)}) %copy-start.5) | copy-done | bytes 1048600
  33.8 0.0 collective-permute-done.6.i1
  33.8 0.0 collective-permute-done.7.i2
  33.8 0.0 collective-permute-done.4.z1
  33.8 0.0 collective-permute-done.5.z2
  33.8 0.0 copy-done.3
  33.8 8.7 %shard_map.51 = (f32[16,32,128]{2,1,0:T(8,128)S(1)}, f32[256,128]{1,0:T(8,128)S(1)}, f32[256,128]{1,0:T(8,128)S(1)}, f32[128,4,128]{2,1,0:T(4,128)}) custom-call(s32[3]{0:T(128)S(1)} %pad_add_fusion.flag, f32[8,3,17]{2,1,0:T(4,128)S(1)} %copy.6.taps, s32[8]{0:T(128)S(1)} %bitcast.6, f32[32,32,128]{2,1,0:T(8,128)S(1)} %get-tuple-element.38.field, ...), custom_call_target="tpu_custom_call" | custom-call | flops 2000000000 | bytes 1024 | tf_op jit(solution)/shard_map/pallas_call | solution.py:423
  42.5 7.0 %all-to-all-start = ((f32[128,4,128]{2,1,0:T(4,128)}), f32[128,4,128]{2,1,0:T(4,128)S(1)}, u32[]{:S(2)}, u32[]{:S(2)}) async-start(f32[128,4,128]{2,1,0:T(4,128)} %get-tuple-element.58), calls=%async_computation | async-start | bytes 524288 | tf_op jit(solution)/shard_map/all_to_all | solution.py:445
  49.5 0.5 collective-permute-start.8
  50.0 4.2 %collective-permute-start.9 = (f32[256,128]{1,0:T(8,128)S(1)}, f32[256,128]{1,0:T(8,128)S(1)}, u32[]{:S(2)}, u32[]{:S(2)}) collective-permute-start(f32[256,128]{1,0:T(8,128)S(1)} %get-tuple-element.54), channel_id=1, source_target_pairs={{32,64},{64,32},{33,65},{65,33},{34,66},{66,34},{35,67},{67,35},{3... | collective-permute-start | bytes 393224 | tf_op jit(solution)/shard_map/ppermute | solution.py:27
  54.2 0.0 collective-permute-done.8.r1
  54.2 4.6 %collective-permute-done.9.r2 = f32[256,128]{1,0:T(8,128)S(1)} collective-permute-done((f32[256,128]{1,0:T(8,128)S(1)}, f32[256,128]{1,0:T(8,128)S(1)}, u32[]{:S(2)}, u32[]{:S(2)}) %collective-permute-start.9) | collective-permute-done | bytes 131104 | tf_op jit(solution)/shard_map/ppermute | solution.py:27
  58.8 0.6 shard_map.52
  59.4 0.8 %collective-permute-start.10 = (f32[128,128]{1,0:T(8,128)S(1)}, f32[128,128]{1,0:T(8,128)S(1)}, u32[]{:S(2)}, u32[]{:S(2)}) collective-permute-start(f32[128,128]{1,0:T(8,128)S(1)} %get-tuple-element.56), channel_id=1, source_target_pairs={{0,4},{4,0},{8,12},{12,8},{16,20},{20,16},{24,28},{28,24},{1,5},{5... | collective-permute-start | bytes 196616 | tf_op jit(solution)/shard_map/ppermute | solution.py:27
  60.2 0.0 copy-start.1
  60.2 3.6 %collective-permute-start.11 = (f32[128,128]{1,0:T(8,128)S(1)}, f32[128,128]{1,0:T(8,128)S(1)}, u32[]{:S(2)}, u32[]{:S(2)}) collective-permute-start(f32[128,128]{1,0:T(8,128)S(1)} %get-tuple-element.57), channel_id=1, source_target_pairs={{4,8},{8,4},{12,16},{16,12},{20,24},{24,20},{5,9},{9,5},{13,17},{1... | collective-permute-start | bytes 196616 | tf_op jit(solution)/shard_map/ppermute | solution.py:27
  63.8 0.0 all-to-all-done.sums
  63.8 0.8 %shard_map.53.scale = f32[8,128]{1,0:T(8,128)S(1)} custom-call(s32[8]{0:T(128)S(1)} %bitcast.7, f32[128,4,128]{2,1,0:T(4,128)S(1)} %all-to-all-done.sums), custom_call_target="tpu_custom_call" | custom-call | flops 1000000 | bytes 1024 | tf_op jit(solution)/shard_map/pallas_call | solution.py:446
  64.6 0.0 collective-permute-done.10.r1
  64.6 2.8 %collective-permute-done.11.r2 = f32[128,128]{1,0:T(8,128)S(1)} collective-permute-done((f32[128,128]{1,0:T(8,128)S(1)}, f32[128,128]{1,0:T(8,128)S(1)}, u32[]{:S(2)}, u32[]{:S(2)}) %collective-permute-start.11) | collective-permute-done | bytes 65568 | tf_op jit(solution)/shard_map/ppermute | solution.py:27
  67.4 0.0 copy-done.1
  67.4 1.2 %shard_map.54 = f32[16,16,128]{2,1,0:T(8,128)} custom-call(s32[3]{0:T(128)S(1)} %pad_add_fusion.flag, f32[16,16,128]{2,1,0:T(8,128)S(1)} %get-tuple-element.55.part, f32[128,128]{1,0:T(8,128)S(1)} %collective-permute-done.10.r1, f32[128,128]{1,0:T(8,128)S(1)} %collective-permute-done.11.r2, f32[16,16,128]{2,1,0:T(8,128)S(1)} %copy-done.1, ...), custom_call_target="tpu_custom_call" | custom-call | bytes 1024 | tf_op jit(solution)/shard_map/pallas_call | solution.py:452
  (1 shorter events, 0.0 us)
Async XLA Ops:
  0.1 0.7 copy-start.4
  0.7 0.9 %copy-start = (f32[16,16,128]{2,1,0:T(8,128)S(1)}, f32[16,16,128]{2,1,0:T(8,128)}, u32[]{:S(2)}) copy-start(f32[16,16,128]{2,1,0:T(8,128)} %est.5) | copy-start | bytes 393220
  2.2 4.6 %collective-permute-start = (f32[136,128]{1,0:T(8,128)S(1)}, f32[136,128]{1,0:T(8,128)S(1)}, u32[]{:S(2)}, u32[]{:S(2)}) collective-permute-start(f32[136,128]{1,0:T(8,128)S(1)} %get-tuple-element.32), channel_id=1, source_target_pairs={{0,4},{4,0},{8,12},{12,8},{16,20},{20,16},{24,28},{28,24},{1,5},{5... | collective-permute-start | bytes 208904 | tf_op jit(solution)/shard_map/ppermute | solution.py:27
  3.5 7.2 %collective-permute-start.1 = (f32[136,128]{1,0:T(8,128)S(1)}, f32[136,128]{1,0:T(8,128)S(1)}, u32[]{:S(2)}, u32[]{:S(2)}) collective-permute-start(f32[136,128]{1,0:T(8,128)S(1)} %get-tuple-element.33), channel_id=1, source_target_pairs={{4,8},{8,4},{12,16},{16,12},{20,24},{24,20},{5,9},{9,5},{13,17},{1... | collective-permute-start | bytes 208904 | tf_op jit(solution)/shard_map/ppermute | solution.py:27
  11.2 13.2 %collective-permute-start.2 = (f32[264,128]{1,0:T(8,128)S(1)}, f32[264,128]{1,0:T(8,128)S(1)}, u32[]{:S(2)}, u32[]{:S(2)}) collective-permute-start(f32[264,128]{1,0:T(8,128)S(1)} %get-tuple-element.36), channel_id=1, source_target_pairs={{0,32},{32,0},{64,96},{96,64},{1,33},{33,1},{65,97},{97,65},{2,34}... | collective-permute-start | bytes 405512 | tf_op jit(solution)/shard_map/ppermute | solution.py:27
  13.4 11.0 %collective-permute-start.3 = (f32[264,128]{1,0:T(8,128)S(1)}, f32[264,128]{1,0:T(8,128)S(1)}, u32[]{:S(2)}, u32[]{:S(2)}) collective-permute-start(f32[264,128]{1,0:T(8,128)S(1)} %get-tuple-element.37), channel_id=1, source_target_pairs={{32,64},{64,32},{33,65},{65,33},{34,66},{66,34},{35,67},{67,35},{3... | collective-permute-start | bytes 405512 | tf_op jit(solution)/shard_map/ppermute | solution.py:27
  18.0 1.2 %copy-start.2 = (f32[8,16,16,128]{3,2,1,0:T(8,128)S(1)}, f32[8,16,16,128]{3,2,1,0:T(8,128)}, u32[]{:S(2)}) copy-start(f32[8,16,16,128]{3,2,1,0:T(8,128)} %observed.3) | copy-start | bytes 3145732
  19.3 14.5 %copy-start.3 = (f32[8,16,16,128]{3,2,1,0:T(8,128)S(1)}, f32[8,16,16,128]{3,2,1,0:T(8,128)}, u32[]{:S(2)}) copy-start(f32[8,16,16,128]{3,2,1,0:T(8,128)} %observed.3) | copy-start | bytes 3145732
  20.2 13.6 %collective-permute-start.6 = (f32[64,256]{1,0:T(8,128)S(1)}, f32[64,256]{1,0:T(8,128)S(1)}, u32[]{:S(2)}, u32[]{:S(2)}) collective-permute-start(f32[64,256]{1,0:T(8,128)S(1)} %get-tuple-element.42), channel_id=1, source_target_pairs={{0,1},{1,0},{2,3},{3,2},{4,5},{5,4},{6,7},{7,6},{8,9},{9,8},{10,11... | collective-permute-start | bytes 196616 | tf_op jit(solution)/shard_map/ppermute | solution.py:27
  20.4 13.4 %collective-permute-start.7 = (f32[64,256]{1,0:T(8,128)S(1)}, f32[64,256]{1,0:T(8,128)S(1)}, u32[]{:S(2)}, u32[]{:S(2)}) collective-permute-start(f32[64,256]{1,0:T(8,128)S(1)} %get-tuple-element.43), channel_id=1, source_target_pairs={{1,2},{2,1},{5,6},{6,5},{9,10},{10,9},{13,14},{14,13},{17,18},{18,... | collective-permute-start | bytes 196616 | tf_op jit(solution)/shard_map/ppermute | solution.py:27
  24.5 2.8 %copy-start.6 = (f32[8,3,17]{2,0,1:T(8,128)S(1)}, f32[8,3,17]{2,0,1:T(8,128)}, u32[]{:S(2)}) copy-start(f32[8,3,17]{2,0,1:T(8,128)} %param.7) | copy-start | bytes 4900
  25.2 8.6 %collective-permute-start.4 = (f32[16,1024]{1,0:T(8,128)S(1)}, f32[16,1024]{1,0:T(8,128)S(1)}, u32[]{:S(2)}, u32[]{:S(2)}) collective-permute-start(f32[16,1024]{1,0:T(8,128)S(1)} %get-tuple-element.40), channel_id=1, source_target_pairs={{0,1},{1,0},{2,3},{3,2},{4,5},{5,4},{6,7},{7,6},{8,9},{9,8},{10,11... | collective-permute-start | bytes 196616 | tf_op jit(solution)/shard_map/ppermute | solution.py:27
  25.3 8.5 %collective-permute-start.5 = (f32[16,1024]{1,0:T(8,128)S(1)}, f32[16,1024]{1,0:T(8,128)S(1)}, u32[]{:S(2)}, u32[]{:S(2)}) collective-permute-start(f32[16,1024]{1,0:T(8,128)S(1)} %get-tuple-element.41), channel_id=1, source_target_pairs={{1,2},{2,1},{5,6},{6,5},{9,10},{10,9},{13,14},{14,13},{17,18},{18,... | collective-permute-start | bytes 196616 | tf_op jit(solution)/shard_map/ppermute | solution.py:27
  32.8 1.0 %copy-start.5 = (bf16[8,256,256]{2,1,0:T(8,128)(2,1)}, bf16[8,256,256]{2,1,0:T(8,128)(2,1)S(1)}, u32[]{:S(2)}) copy-start(bf16[8,256,256]{2,1,0:T(8,128)(2,1)S(1)} %get-tuple-element.47.wz2) | copy-start | bytes 3145732
  42.5 21.3 %all-to-all-start = ((f32[128,4,128]{2,1,0:T(4,128)}), f32[128,4,128]{2,1,0:T(4,128)S(1)}, u32[]{:S(2)}, u32[]{:S(2)}) async-start(f32[128,4,128]{2,1,0:T(4,128)} %get-tuple-element.58), calls=%async_computation | async-start | bytes 524288 | tf_op jit(solution)/shard_map/all_to_all | solution.py:445
  49.5 4.7 %collective-permute-start.8 = (f32[256,128]{1,0:T(8,128)S(1)}, f32[256,128]{1,0:T(8,128)S(1)}, u32[]{:S(2)}, u32[]{:S(2)}) collective-permute-start(f32[256,128]{1,0:T(8,128)S(1)} %get-tuple-element.53), channel_id=1, source_target_pairs={{0,32},{32,0},{64,96},{96,64},{1,33},{33,1},{65,97},{97,65},{2,34}... | collective-permute-start | bytes 393224 | tf_op jit(solution)/shard_map/ppermute | solution.py:27
  50.0 8.8 %collective-permute-start.9 = (f32[256,128]{1,0:T(8,128)S(1)}, f32[256,128]{1,0:T(8,128)S(1)}, u32[]{:S(2)}, u32[]{:S(2)}) collective-permute-start(f32[256,128]{1,0:T(8,128)S(1)} %get-tuple-element.54), channel_id=1, source_target_pairs={{32,64},{64,32},{33,65},{65,33},{34,66},{66,34},{35,67},{67,35},{3... | collective-permute-start | bytes 393224 | tf_op jit(solution)/shard_map/ppermute | solution.py:27
  59.4 5.2 %collective-permute-start.10 = (f32[128,128]{1,0:T(8,128)S(1)}, f32[128,128]{1,0:T(8,128)S(1)}, u32[]{:S(2)}, u32[]{:S(2)}) collective-permute-start(f32[128,128]{1,0:T(8,128)S(1)} %get-tuple-element.56), channel_id=1, source_target_pairs={{0,4},{4,0},{8,12},{12,8},{16,20},{20,16},{24,28},{28,24},{1,5},{5... | collective-permute-start | bytes 196616 | tf_op jit(solution)/shard_map/ppermute | solution.py:27
  60.2 7.2 %copy-start.1 = (f32[16,16,128]{2,1,0:T(8,128)S(1)}, f32[16,16,128]{2,1,0:T(8,128)}, u32[]{:S(2)}) copy-start(f32[16,16,128]{2,1,0:T(8,128)} %est.5) | copy-start | bytes 393220
  60.2 7.2 %collective-permute-start.11 = (f32[128,128]{1,0:T(8,128)S(1)}, f32[128,128]{1,0:T(8,128)S(1)}, u32[]{:S(2)}, u32[]{:S(2)}) collective-permute-start(f32[128,128]{1,0:T(8,128)S(1)} %get-tuple-element.57), channel_id=1, source_target_pairs={{4,8},{8,4},{12,16},{16,12},{20,24},{24,20},{5,9},{9,5},{13,17},{1... | collective-permute-start | bytes 196616 | tf_op jit(solution)/shard_map/ppermute | solution.py:27

commit v4 on v3

--- a/solution.py
+++ b/solution.py
@@ -27,16 +27,17 @@
     return lax.ppermute(one, axis, pairs(count, 0)), lax.ppermute(two, axis, pairs(count, 1))
 
 
-def kernel_call(body, out_shape, scratch=(), in_smem=0, flops=0, n_in=0):
+def kernel_call(body, out_shape, scratch=(), in_smem=0, flops=0, n_in=0, in_hbm=0, mib=8):
     vmem = pl.BlockSpec(memory_space=pltpu.VMEM)
     smem = pl.BlockSpec(memory_space=pltpu.SMEM)
+    hbm = pl.BlockSpec(memory_space=pltpu.HBM)
     return pl.pallas_call(
         body,
         out_shape=out_shape,
-        in_specs=[smem] * in_smem + [vmem] * (n_in - in_smem),
+        in_specs=[smem] * in_smem + [hbm] * in_hbm + [vmem] * (n_in - in_smem - in_hbm),
         out_specs=jax.tree.map(lambda _: vmem, out_shape),
         scratch_shapes=list(scratch),
-        compiler_params=pltpu.CompilerParams(vmem_limit_bytes=48 * 1024 * 1024),
+        compiler_params=pltpu.CompilerParams(vmem_limit_bytes=mib * 1024 * 1024),
         cost_estimate=pl.CostEstimate(flops=flops, bytes_accessed=1024, transcendentals=0),
     )
 
@@ -53,7 +54,15 @@
     return row
 
 
-def y_pack(flag, cover, est, op1, op2):
+def y_pack(flag, cover_hbm, est_hbm, op1, op2, cover, est, sems):
+    copies = (
+        pltpu.make_async_copy(est_hbm, est, sems.at[0]),
+        pltpu.make_async_copy(cover_hbm, cover, sems.at[1]),
+    )
+    for copy in copies:
+        copy.start()
+    for copy in copies:
+        copy.wait()
     odd = flag[1] == 1
     for i in range(CX):
         low, high = est[i, :R], est[i, CY - R :]
@@ -166,39 +175,55 @@
         tx[k : k + 1, :] = row[:1]
     tx[K:, :] = jnp.zeros((24 - K, LANES), F32)
 
+    wz1[...] = jnp.zeros_like(wz1)
+    wz2[...] = jnp.zeros_like(wz2)
+    tz2[...] = jnp.zeros_like(tz2)
+    tz3[...] = jnp.zeros_like(tz3)
+    row, col = iota((LANES, LANES), 0), iota((LANES, LANES), 1)
+    short_row, short_col = row[: 2 * R], col[: 2 * R]
+    end = row[: 4 * R]
+    z_end = jnp.where(end < 2 * R, end - 2 * R, end - 2 * R + CZ)
+    near_row = jnp.where(short_row < R, short_row, short_row - 2 * R + CZ)
+    slot_row = jnp.where(short_row < R, short_row - R, short_row - R + CZ)
+
     def z_of(v, carry):
         scale = inverse_sum(taps, v, 2)
-        row, col = iota((LANES, LANES), 0), iota((LANES, LANES), 1)
-
-        def slot(lane):
-            place = lane - 2 * R * v
-            z = jnp.where(place < R, place - R, place - R + CZ)
-            return jnp.where((place >= 0) & (place < 2 * R), z, 4 * CZ)
-
-        def past(lane):
-            return jnp.where(lane < 2 * R, lane - 2 * R, lane - 2 * R + CZ)
-
-        ends = row[: 12 * R]
-        z_end = past(ends % (4 * R))
-        first = ends < 8 * R
-        for half, z_out in ((slice(0, LANES), col), (slice(LANES, 2 * LANES), slot(col))):
-            high, low = split(pick(taps, v, 2, row - z_out + R, scale))
-            wz1[v, :LANES, half] = high
-            wz1[v, LANES:, half] = high
-            wz2[v, :LANES, half] = low
-            high, low = split(pick(taps, v, 2, z_end - z_out[: 12 * R] + R, scale))
-            wz2[v, LANES : LANES + 12 * R, half] = jnp.where(
-                first, high.astype(F32), low.astype(F32)
-            ).astype(BF16)
-            wz2[v, LANES + 12 * R :, half] = jnp.zeros((LANES - 12 * R, LANES), BF16)
-        high, low = split(pick(taps, v, 2, col - row + R, scale))
+        place = short_col[:1] - 2 * R * v
+        z = jnp.where(place < R, place - R, place - R + CZ)
+        slot_col = jnp.where((place >= 0) & (place < 2 * R), z, 4 * CZ)
+
+        middle = pick(taps, v, 2, row - col + R, scale)
+        high, low = split(middle)
+        wz1[v, :LANES, :LANES] = high
+        wz1[v, LANES:, :LANES] = high
+        wz2[v, :LANES, :LANES] = low
+        high, low = split(jnp.transpose(middle))
         tz1[v, :LANES, :] = high
         tz1[v, LANES:, :] = high
         tz2[v, :LANES, :] = low
-        high, low = split(pick(taps, v, 2, col - slot(row) + R, scale))
-        tz2[v, LANES:, :] = high
-        tz3[v, :LANES, :] = low
-        tz3[v, LANES:, :] = high
+
+        near = pick(taps, v, 2, near_row - slot_col + R, scale)
+        zeros = jnp.zeros((R, LANES), F32)
+        for at, piece in (
+            (0, jnp.concatenate([near[:R], zeros], axis=0)),
+            (LANES - 2 * R, jnp.concatenate([zeros, near[R:]], axis=0)),
+        ):
+            high, low = split(piece)
+            wz1[v, at : at + 2 * R, LANES:] = high
+            wz1[v, LANES + at : LANES + at + 2 * R, LANES:] = high
+            wz2[v, at : at + 2 * R, LANES:] = low
+
+        for half, z_out in ((slice(0, LANES), col[:1]), (slice(LANES, 2 * LANES), slot_col)):
+            high, low = split(pick(taps, v, 2, z_end - z_out + R, scale))
+            wz2[v, LANES : LANES + 4 * R, half] = high
+            wz2[v, LANES + 4 * R : LANES + 8 * R, half] = high
+            wz2[v, LANES + 8 * R : LANES + 12 * R, half] = low
+
+        high, low = split(pick(taps, v, 2, short_col - slot_row + R, scale))
+        first = pl.multiple_of(v * 2 * R, 2 * R)
+        tz2[v, pl.ds(LANES + first, 2 * R), :] = high
+        tz3[v, pl.ds(first, 2 * R), :] = low
+        tz3[v, pl.ds(LANES + first, 2 * R), :] = high
         return carry
 
     lax.fori_loop(0, V, z_of, 0)
@@ -361,18 +386,14 @@
         op2[a * R : (a + 1) * R, :] = jnp.where(odd_y, high, low)
 
 
-def scale_of(cover, sums, scale):
+def y_add(flag, cover, part, r1, r2, est, sums, out):
+    odd = flag[1] == 1
     gathered = jnp.sum(sums[...], axis=0)[:1]
     lane = iota((1, LANES), 1)
     target = jnp.sum(jnp.where(lane == 0, gathered, 0.0), axis=1, keepdims=True)
     total = jnp.sum(jnp.where(lane == 64, gathered, 0.0), axis=1, keepdims=True)
     count = jnp.sum(spread_cover(cover)[:1], axis=1, keepdims=True) * (1.0 / CY)
-    scale[...] = jnp.broadcast_to(target / total / count, (8, LANES))
-
-
-def y_add(flag, part, r1, r2, est, scale, out):
-    odd = flag[1] == 1
-    by = scale[...]
+    by = jnp.broadcast_to(target / total / count, (8, LANES))
     for a in range(CX):
         one, two = r1[a * R : (a + 1) * R, :], r2[a * R : (a + 1) * R, :]
         out[a, :R] = est[a, :R] * (part[a, :R] + jnp.where(odd, one, two)) * by
@@ -385,7 +406,19 @@
     peers = lax.axis_size(ALL)
 
     op = shape(R * CX + 8, LANES)
-    y1, y2 = kernel_call(y_pack, (op, op), n_in=3, in_smem=2)(flag, cover, estimate)
+    y1, y2 = kernel_call(
+        y_pack,
+        (op, op),
+        scratch=(
+            pltpu.SMEM((V,), jnp.int32),
+            pltpu.VMEM((CX, CY, CZ), F32),
+            pltpu.SemaphoreType.DMA((2,)),
+        ),
+        n_in=3,
+        in_smem=1,
+        in_hbm=2,
+        mib=60,
+    )(flag, cover, estimate)
     y1, y2 = swap(y1, y2, "by")
     op = shape(V * R, CX * CY)
     i1, i2 = kernel_call(image_pack, (op, op), n_in=2, in_smem=1, flops=10**7)(flag, observed)
@@ -438,19 +471,19 @@
         ),
         n_in=18,
         in_smem=3,
+        mib=30,
         flops=2 * 10**9,
     )(flag, psf_taps, cover, field, w9, z1, z2, i1, i2, observed, *tables)
 
     x1, x2 = swap(x1, x2, "bx")
     sums = lax.all_to_all(sums, ALL, 0, 0)
-    scale = kernel_call(scale_of, shape(8, LANES), n_in=2, in_smem=1, flops=10**6)(cover, sums)
     op = shape(R * CX, LANES)
     part, y1, y2 = kernel_call(x_add, (shape(CX, CY, LANES), op, op), n_in=4, in_smem=1)(
         flag, part, x1, x2
     )
     y1, y2 = swap(y1, y2, "by")
-    return kernel_call(y_add, shape(CX, CY, LANES), n_in=6, in_smem=1)(
-        flag, part, y1, y2, estimate, scale
+    return kernel_call(y_add, shape(CX, CY, LANES), n_in=7, in_smem=2)(
+        flag, cover, part, y1, y2, estimate, sums
     )
 
 

time: 69.4 us -> 67.3 us (0.970)
  local copies, waits for them, and re-layouts: 3.8 us -> 1.25 us
  Pallas kernels: 19.5 us -> 17.9 us
  waiting for transfers between devices: 11.3 us -> 12.3 us
    unnamed x15 -> x13, local copies, waits for them, and re-layouts: 3.8 us -> 1.25 us
    pallas_call x1, Pallas kernels: 5.49 us -> 3.24 us  [on_device(): kernel_call(bands, (shape(V * CY, LANES, dtype=BF16), shape(2 * EY, LANES...]
    pallas_call x3 -> x2, Pallas kernels: 2.54 us -> 3.69 us  [the longest x1 2.26 us: on_device(): kernel_call(y_pack, (op, op), scratch=(pltpu.SMEM((V,), jnp.int32), pltpu...]
    ppermute x6, waiting for transfers between devices: 11.3 us -> 12.2 us  [swap(): lax.ppermute(two, axis, pairs(count, 1))]
  transfers between devices with their start and end apart: 13 -> 13, of which waited for: 3 -> 3; matrix products, arithmetic and copies ran while one was open for 0% -> 0% of each run, Pallas kernels for 12% -> 8%
where the time goes in v4:
time: 67.3 us; the launch traced here: 66.6 us
  starting transfers between devices  34.3 us (51%)
  Pallas kernels  17.9 us (27%)
  waiting for transfers between devices  12.3 us (18%)
  local copies, waits for them, and re-layouts  1.25 us (2%)
    ppermute x6, starting transfers between devices, swap(): lax.ppermute(two, axis, pairs(count, 1))  21.5 us
    ppermute x6, waiting for transfers between devices, swap(): lax.ppermute(two, axis, pairs(count, 1))  12.2 us
    pallas_call x1, Pallas kernels, on_device(): kernel_call(main_kernel, (shape(CX, EY, LANES), op, op, shape(peers, 4, L...  8.17 us
    all_to_all x1, starting transfers between devices, on_device(): sums = lax.all_to_all(sums, ALL, 0, 0)  7.67 us
    ppermute x6, starting transfers between devices, swap(): lax.ppermute(one, axis, pairs(count, 0))  5.06 us
    pallas_call x1, Pallas kernels, on_device(): kernel_call(bands, (shape(V * CY, LANES, dtype=BF16), shape(2 * EY, LANES...  3.24 us
    pallas_call x1, Pallas kernels, on_device(): kernel_call(y_pack, (op, op), scratch=(pltpu.SMEM((V,), jnp.int32), pltpu...  2.26 us
    pallas_call x1, Pallas kernels, on_device(): kernel_call(y_add, shape(CX, CY, LANES), n_in=7, in_smem=2)  1.43 us
  transfers between devices with their start and end apart: 13, of which 3 were waited for; matrix products, arithmetic and copies ran while one was open for 0% of the time, Pallas kernels for 8%

profile of v4, /device:TPU:41, one launch (start us, length us, event | category | flops | bytes accessed | tf_op | source)
XLA Modules:
  0.0 66.6 jit_solution(18310220458218727236)
XLA Ops:
  0.0 0.0 copy-start
  0.0 0.7 %pad_add_fusion.flag = s32[3]{0:T(128)} fusion(s32[1]{0:T(128)} %bitcast.2, s32[1]{0:T(128)} %bitcast.1, s32[1]{0:T(128)} %bitcast), kind=kLoop, calls=%fused_computation | loop fusion | flops 6 | bytes 24 | tf_op jit(solution)/shard_map/stack | solution.py:404
  0.7 2.3 %shard_map.46 = (f32[136,128]{1,0:T(8,128)}, f32[136,128]{1,0:T(8,128)}) custom-call(s32[3]{0:T(128)} %pad_add_fusion.flag, s32[8]{0:T(128)} %bitcast.4, f32[16,16,128]{2,1,0:T(8,128)} %est.3), custom_call_target="tpu_custom_call" | custom-call | bytes 1024 | tf_op jit(solution)/shard_map/pallas_call | solution.py:409
  2.9 0.0 copy-start.3
  2.9 0.0 copy-start.4
  3.0 1.3 %collective-permute-start = (f32[136,128]{1,0:T(8,128)}, f32[136,128]{1,0:T(8,128)S(1)}, u32[]{:S(2)}, u32[]{:S(2)}) collective-permute-start(f32[136,128]{1,0:T(8,128)} %get-tuple-element.32), channel_id=1, source_target_pairs={{0,4},{4,0},{8,12},{12,8},{16,20},{20,16},{24,28},{28,24},{1,5},{5... | collective-permute-start | bytes 208904 | tf_op jit(solution)/shard_map/ppermute | solution.py:27
  4.3 3.3 %collective-permute-start.1 = (f32[136,128]{1,0:T(8,128)}, f32[136,128]{1,0:T(8,128)S(1)}, u32[]{:S(2)}, u32[]{:S(2)}) collective-permute-start(f32[136,128]{1,0:T(8,128)} %get-tuple-element.33), channel_id=1, source_target_pairs={{4,8},{8,4},{12,16},{16,12},{20,24},{24,20},{5,9},{9,5},{13,17},{1... | collective-permute-start | bytes 208904 | tf_op jit(solution)/shard_map/ppermute | solution.py:27
  7.5 0.0 collective-permute-done.y1
  7.5 4.1 %collective-permute-done.1.y2 = f32[136,128]{1,0:T(8,128)S(1)} collective-permute-done((f32[136,128]{1,0:T(8,128)}, f32[136,128]{1,0:T(8,128)S(1)}, u32[]{:S(2)}, u32[]{:S(2)}) %collective-permute-start.1) | collective-permute-done | bytes 69664 | tf_op jit(solution)/shard_map/ppermute | solution.py:27
  11.6 0.0 copy-done
  11.6 0.0 copy-done.3
  11.6 0.0 copy-done.4
  11.6 0.6 shard_map.47
  12.2 2.2 %collective-permute-start.2 = (f32[264,128]{1,0:T(8,128)S(1)}, f32[264,128]{1,0:T(8,128)S(1)}, u32[]{:S(2)}, u32[]{:S(2)}) collective-permute-start(f32[264,128]{1,0:T(8,128)S(1)} %get-tuple-element.36), channel_id=1, source_target_pairs={{0,32},{32,0},{64,96},{96,64},{1,33},{33,1},{65,97},{97,65},{2,34}... | collective-permute-start | bytes 405512 | tf_op jit(solution)/shard_map/ppermute | solution.py:27
  14.4 4.6 %collective-permute-start.3 = (f32[264,128]{1,0:T(8,128)S(1)}, f32[264,128]{1,0:T(8,128)S(1)}, u32[]{:S(2)}, u32[]{:S(2)}) collective-permute-start(f32[264,128]{1,0:T(8,128)S(1)} %get-tuple-element.37), channel_id=1, source_target_pairs={{32,64},{64,32},{33,65},{65,33},{34,66},{66,34},{35,67},{67,35},{3... | collective-permute-start | bytes 405512 | tf_op jit(solution)/shard_map/ppermute | solution.py:27
  19.0 0.0 copy-start.1
  19.0 1.2 %copy-done.1 = f32[8,16,16,128]{3,2,1,0:T(8,128)S(1)} copy-done((f32[8,16,16,128]{3,2,1,0:T(8,128)S(1)}, f32[8,16,16,128]{3,2,1,0:T(8,128)}, u32[]{:S(2)}) %copy-start.1) | copy-done | bytes 1048600
  20.3 0.0 copy-start.2
  20.3 0.9 %shard_map.49 = (f32[64,256]{1,0:T(8,128)S(1)}, f32[64,256]{1,0:T(8,128)S(1)}) custom-call(s32[3]{0:T(128)S(1)} %copy-done.3, f32[8,16,16,128]{3,2,1,0:T(8,128)S(1)} %copy-done.1), custom_call_target="tpu_custom_call" | custom-call | flops 10000000 | bytes 1024 | tf_op jit(solution)/shard_map/pallas_call | solution.py:424
  21.1 0.2 collective-permute-start.6
  21.4 4.0 %collective-permute-start.7 = (f32[64,256]{1,0:T(8,128)S(1)}, f32[64,256]{1,0:T(8,128)S(1)}, u32[]{:S(2)}, u32[]{:S(2)}) collective-permute-start(f32[64,256]{1,0:T(8,128)S(1)} %get-tuple-element.43), channel_id=1, source_target_pairs={{1,2},{2,1},{5,6},{6,5},{9,10},{10,9},{13,14},{14,13},{17,18},{18,... | collective-permute-start | bytes 196616 | tf_op jit(solution)/shard_map/ppermute | solution.py:27
  25.4 0.0 collective-permute-done.2.x1
  25.4 0.0 collective-permute-done.3.x2
  25.4 0.0 copy-start.5
  25.4 0.7 %shard_map.48 = (f32[32,32,128]{2,1,0:T(8,128)S(1)}, f32[16,128]{1,0:T(8,128)S(1)}, f32[16,1024]{1,0:T(8,128)S(1)}, f32[16,1024]{1,0:T(8,128)S(1)}) custom-call(s32[3]{0:T(128)S(1)} %copy-done.3, f32[16,32,128]{2,1,0:T(8,128)S(1)} %get-tuple-element.34.fy, f32[8,128]{1,0:T(8,128)S(1)} %get-tuple-element.35.wy, f32[264,128]{1,0:T(8,128)S(1)} %collective-permute-done.2.x1, ...), custom_call_target="tpu_custom_call" | custom-call | bytes 1024 | tf_op jit(solution)/shard_map/pallas_call | solution.py:450
  26.2 0.1 collective-permute-start.4
  26.3 1.9 %collective-permute-start.5 = (f32[16,1024]{1,0:T(8,128)S(1)}, f32[16,1024]{1,0:T(8,128)S(1)}, u32[]{:S(2)}, u32[]{:S(2)}) collective-permute-start(f32[16,1024]{1,0:T(8,128)S(1)} %get-tuple-element.41), channel_id=1, source_target_pairs={{1,2},{2,1},{5,6},{6,5},{9,10},{10,9},{13,14},{14,13},{17,18},{18,... | collective-permute-start | bytes 196616 | tf_op jit(solution)/shard_map/ppermute | solution.py:27
  28.2 0.0 copy-done.5
  28.2 3.2 %shard_map.50 = (bf16[128,128]{1,0:T(8,128)(2,1)S(1)}, f32[64,128]{1,0:T(8,128)S(1)}, bf16[8,256,256]{2,1,0:T(8,128)(2,1)S(1)}, bf16[8,256,256]{2,1,0:T(8,128)(2...) custom-call(f32[8,3,17]{2,1,0:T(4,128)S(1)} %copy.6.taps), custom_call_target="tpu_custom_call" | custom-call | flops 200000000 | bytes 1024 | tf_op jit(solution)/shard_map/pallas_call | solution.py:428
  31.5 0.0 collective-permute-done.6.i1
  31.5 0.0 collective-permute-done.7.i2
  31.5 0.0 collective-permute-done.4.z1
  31.5 0.0 collective-permute-done.5.z2
  31.5 0.0 copy-done.2
  31.5 8.2 %shard_map.51 = (f32[16,32,128]{2,1,0:T(8,128)S(1)}, f32[256,128]{1,0:T(8,128)S(1)}, f32[256,128]{1,0:T(8,128)S(1)}, f32[128,4,128]{2,1,0:T(4,128)}) custom-call(s32[3]{0:T(128)S(1)} %copy-done.3, f32[8,3,17]{2,1,0:T(4,128)S(1)} %copy.6.taps, s32[8]{0:T(128)S(1)} %bitcast.6, f32[32,32,128]{2,1,0:T(8,128)S(1)} %get-tuple-element.38.field, ...), custom_call_target="tpu_custom_call" | custom-call | flops 2000000000 | bytes 1024 | tf_op jit(solution)/shard_map/pallas_call | solution.py:456
  39.7 7.7 %all-to-all-start = ((f32[128,4,128]{2,1,0:T(4,128)}), f32[128,4,128]{2,1,0:T(4,128)S(1)}, u32[]{:S(2)}, u32[]{:S(2)}) async-start(f32[128,4,128]{2,1,0:T(4,128)} %get-tuple-element.58), calls=%async_computation | async-start | bytes 524288 | tf_op jit(solution)/shard_map/all_to_all | solution.py:479
  47.4 0.5 collective-permute-start.8
  47.9 4.2 %collective-permute-start.9 = (f32[256,128]{1,0:T(8,128)S(1)}, f32[256,128]{1,0:T(8,128)S(1)}, u32[]{:S(2)}, u32[]{:S(2)}) collective-permute-start(f32[256,128]{1,0:T(8,128)S(1)} %get-tuple-element.54), channel_id=1, source_target_pairs={{32,64},{64,32},{33,65},{65,33},{34,66},{66,34},{35,67},{67,35},{3... | collective-permute-start | bytes 393224 | tf_op jit(solution)/shard_map/ppermute | solution.py:27
  52.1 0.0 collective-permute-done.8.r1
  52.1 4.6 %collective-permute-done.9.r2 = f32[256,128]{1,0:T(8,128)S(1)} collective-permute-done((f32[256,128]{1,0:T(8,128)S(1)}, f32[256,128]{1,0:T(8,128)S(1)}, u32[]{:S(2)}, u32[]{:S(2)}) %collective-permute-start.9) | collective-permute-done | bytes 131104 | tf_op jit(solution)/shard_map/ppermute | solution.py:27
  56.7 0.6 shard_map.52
  57.3 0.8 %collective-permute-start.10 = (f32[128,128]{1,0:T(8,128)S(1)}, f32[128,128]{1,0:T(8,128)S(1)}, u32[]{:S(2)}, u32[]{:S(2)}) collective-permute-start(f32[128,128]{1,0:T(8,128)S(1)} %get-tuple-element.56), channel_id=1, source_target_pairs={{0,4},{4,0},{8,12},{12,8},{16,20},{20,16},{24,28},{28,24},{1,5},{5... | collective-permute-start | bytes 196616 | tf_op jit(solution)/shard_map/ppermute | solution.py:27
  58.0 3.5 %collective-permute-start.11 = (f32[128,128]{1,0:T(8,128)S(1)}, f32[128,128]{1,0:T(8,128)S(1)}, u32[]{:S(2)}, u32[]{:S(2)}) collective-permute-start(f32[128,128]{1,0:T(8,128)S(1)} %get-tuple-element.57), channel_id=1, source_target_pairs={{4,8},{8,4},{12,16},{16,12},{20,24},{24,20},{5,9},{9,5},{13,17},{1... | collective-permute-start | bytes 196616 | tf_op jit(solution)/shard_map/ppermute | solution.py:27
  61.5 0.0 collective-permute-done.10.r1
  61.6 3.6 %collective-permute-done.11.r2 = f32[128,128]{1,0:T(8,128)S(1)} collective-permute-done((f32[128,128]{1,0:T(8,128)S(1)}, f32[128,128]{1,0:T(8,128)S(1)}, u32[]{:S(2)}, u32[]{:S(2)}) %collective-permute-start.11) | collective-permute-done | bytes 65568 | tf_op jit(solution)/shard_map/ppermute | solution.py:27
  65.1 0.0 all-to-all-done.sums
  65.2 1.4 %shard_map.53 = f32[16,16,128]{2,1,0:T(8,128)} custom-call(s32[3]{0:T(128)S(1)} %copy-done.3, s32[8]{0:T(128)S(1)} %bitcast.7, f32[16,16,128]{2,1,0:T(8,128)S(1)} %get-tuple-element.55.part, f32[128,128]{1,0:T(8,128)S(1)} %collective-permute-done.10.r1, f32[128,128]{1,0:T(8,128)S(1)} %collective-permute-done.11.r2, f32[16,16,128]{2,1,0:T(8,128)S(1)} %copy-done, ...), custom_call_target="tpu_custom_call" | custom-call | bytes 1024 | tf_op jit(solution)/shard_map/pallas_call | solution.py:485
  (1 shorter events, 0.0 us)
Async XLA Ops:
  0.0 11.6 %copy-start = (f32[16,16,128]{2,1,0:T(8,128)S(1)}, f32[16,16,128]{2,1,0:T(8,128)}, u32[]{:S(2)}) copy-start(f32[16,16,128]{2,1,0:T(8,128)} %est.3) | copy-start | bytes 393220
  2.9 8.7 %copy-start.3 = (s32[3]{0:T(128)S(1)}, s32[3]{0:T(128)}, u32[]{:S(2)}) copy-start(s32[3]{0:T(128)} %pad_add_fusion.flag) | copy-start | bytes 40
  2.9 8.7 %copy-start.4 = (s32[8,1,1,1]{0,3,2,1:T(1,128)S(1)}, s32[8,1,1,1]{0,3,2,1:T(1,128)}, u32[]{:S(2)}) copy-start(s32[8,1,1,1]{0,3,2,1:T(1,128)} %param.6) | copy-start | bytes 100
  3.0 4.6 %collective-permute-start = (f32[136,128]{1,0:T(8,128)}, f32[136,128]{1,0:T(8,128)S(1)}, u32[]{:S(2)}, u32[]{:S(2)}) collective-permute-start(f32[136,128]{1,0:T(8,128)} %get-tuple-element.32), channel_id=1, source_target_pairs={{0,4},{4,0},{8,12},{12,8},{16,20},{20,16},{24,28},{28,24},{1,5},{5... | collective-permute-start | bytes 208904 | tf_op jit(solution)/shard_map/ppermute | solution.py:27
  4.3 7.4 %collective-permute-start.1 = (f32[136,128]{1,0:T(8,128)}, f32[136,128]{1,0:T(8,128)S(1)}, u32[]{:S(2)}, u32[]{:S(2)}) collective-permute-start(f32[136,128]{1,0:T(8,128)} %get-tuple-element.33), channel_id=1, source_target_pairs={{4,8},{8,4},{12,16},{16,12},{20,24},{24,20},{5,9},{9,5},{13,17},{1... | collective-permute-start | bytes 208904 | tf_op jit(solution)/shard_map/ppermute | solution.py:27
  12.2 13.2 %collective-permute-start.2 = (f32[264,128]{1,0:T(8,128)S(1)}, f32[264,128]{1,0:T(8,128)S(1)}, u32[]{:S(2)}, u32[]{:S(2)}) collective-permute-start(f32[264,128]{1,0:T(8,128)S(1)} %get-tuple-element.36), channel_id=1, source_target_pairs={{0,32},{32,0},{64,96},{96,64},{1,33},{33,1},{65,97},{97,65},{2,34}... | collective-permute-start | bytes 405512 | tf_op jit(solution)/shard_map/ppermute | solution.py:27
  14.4 11.0 %collective-permute-start.3 = (f32[264,128]{1,0:T(8,128)S(1)}, f32[264,128]{1,0:T(8,128)S(1)}, u32[]{:S(2)}, u32[]{:S(2)}) collective-permute-start(f32[264,128]{1,0:T(8,128)S(1)} %get-tuple-element.37), channel_id=1, source_target_pairs={{32,64},{64,32},{33,65},{65,33},{34,66},{66,34},{35,67},{67,35},{3... | collective-permute-start | bytes 405512 | tf_op jit(solution)/shard_map/ppermute | solution.py:27
  19.0 1.2 %copy-start.1 = (f32[8,16,16,128]{3,2,1,0:T(8,128)S(1)}, f32[8,16,16,128]{3,2,1,0:T(8,128)}, u32[]{:S(2)}) copy-start(f32[8,16,16,128]{3,2,1,0:T(8,128)} %observed.3) | copy-start | bytes 3145732
  20.3 11.3 %copy-start.2 = (f32[8,16,16,128]{3,2,1,0:T(8,128)S(1)}, f32[8,16,16,128]{3,2,1,0:T(8,128)}, u32[]{:S(2)}) copy-start(f32[8,16,16,128]{3,2,1,0:T(8,128)} %observed.3) | copy-start | bytes 3145732
  21.1 10.4 %collective-permute-start.6 = (f32[64,256]{1,0:T(8,128)S(1)}, f32[64,256]{1,0:T(8,128)S(1)}, u32[]{:S(2)}, u32[]{:S(2)}) collective-permute-start(f32[64,256]{1,0:T(8,128)S(1)} %get-tuple-element.42), channel_id=1, source_target_pairs={{0,1},{1,0},{2,3},{3,2},{4,5},{5,4},{6,7},{7,6},{8,9},{9,8},{10,11... | collective-permute-start | bytes 196616 | tf_op jit(solution)/shard_map/ppermute | solution.py:27
  21.4 10.1 %collective-permute-start.7 = (f32[64,256]{1,0:T(8,128)S(1)}, f32[64,256]{1,0:T(8,128)S(1)}, u32[]{:S(2)}, u32[]{:S(2)}) collective-permute-start(f32[64,256]{1,0:T(8,128)S(1)} %get-tuple-element.43), channel_id=1, source_target_pairs={{1,2},{2,1},{5,6},{6,5},{9,10},{10,9},{13,14},{14,13},{17,18},{18,... | collective-permute-start | bytes 196616 | tf_op jit(solution)/shard_map/ppermute | solution.py:27
  25.4 2.8 %copy-start.5 = (f32[8,3,17]{2,0,1:T(8,128)S(1)}, f32[8,3,17]{2,0,1:T(8,128)}, u32[]{:S(2)}) copy-start(f32[8,3,17]{2,0,1:T(8,128)} %param.7) | copy-start | bytes 4900
  26.2 5.3 %collective-permute-start.4 = (f32[16,1024]{1,0:T(8,128)S(1)}, f32[16,1024]{1,0:T(8,128)S(1)}, u32[]{:S(2)}, u32[]{:S(2)}) collective-permute-start(f32[16,1024]{1,0:T(8,128)S(1)} %get-tuple-element.40), channel_id=1, source_target_pairs={{0,1},{1,0},{2,3},{3,2},{4,5},{5,4},{6,7},{7,6},{8,9},{9,8},{10,11... | collective-permute-start | bytes 196616 | tf_op jit(solution)/shard_map/ppermute | solution.py:27
  26.3 5.2 %collective-permute-start.5 = (f32[16,1024]{1,0:T(8,128)S(1)}, f32[16,1024]{1,0:T(8,128)S(1)}, u32[]{:S(2)}, u32[]{:S(2)}) collective-permute-start(f32[16,1024]{1,0:T(8,128)S(1)} %get-tuple-element.41), channel_id=1, source_target_pairs={{1,2},{2,1},{5,6},{6,5},{9,10},{10,9},{13,14},{14,13},{17,18},{18,... | collective-permute-start | bytes 196616 | tf_op jit(solution)/shard_map/ppermute | solution.py:27
  39.7 25.4 %all-to-all-start = ((f32[128,4,128]{2,1,0:T(4,128)}), f32[128,4,128]{2,1,0:T(4,128)S(1)}, u32[]{:S(2)}, u32[]{:S(2)}) async-start(f32[128,4,128]{2,1,0:T(4,128)} %get-tuple-element.58), calls=%async_computation | async-start | bytes 524288 | tf_op jit(solution)/shard_map/all_to_all | solution.py:479
  47.4 4.7 %collective-permute-start.8 = (f32[256,128]{1,0:T(8,128)S(1)}, f32[256,128]{1,0:T(8,128)S(1)}, u32[]{:S(2)}, u32[]{:S(2)}) collective-permute-start(f32[256,128]{1,0:T(8,128)S(1)} %get-tuple-element.53), channel_id=1, source_target_pairs={{0,32},{32,0},{64,96},{96,64},{1,33},{33,1},{65,97},{97,65},{2,34}... | collective-permute-start | bytes 393224 | tf_op jit(solution)/shard_map/ppermute | solution.py:27
  47.9 8.8 %collective-permute-start.9 = (f32[256,128]{1,0:T(8,128)S(1)}, f32[256,128]{1,0:T(8,128)S(1)}, u32[]{:S(2)}, u32[]{:S(2)}) collective-permute-start(f32[256,128]{1,0:T(8,128)S(1)} %get-tuple-element.54), channel_id=1, source_target_pairs={{32,64},{64,32},{33,65},{65,33},{34,66},{66,34},{35,67},{67,35},{3... | collective-permute-start | bytes 393224 | tf_op jit(solution)/shard_map/ppermute | solution.py:27
  57.3 4.3 %collective-permute-start.10 = (f32[128,128]{1,0:T(8,128)S(1)}, f32[128,128]{1,0:T(8,128)S(1)}, u32[]{:S(2)}, u32[]{:S(2)}) collective-permute-start(f32[128,128]{1,0:T(8,128)S(1)} %get-tuple-element.56), channel_id=1, source_target_pairs={{0,4},{4,0},{8,12},{12,8},{16,20},{20,16},{24,28},{28,24},{1,5},{5... | collective-permute-start | bytes 196616 | tf_op jit(solution)/shard_map/ppermute | solution.py:27
  58.0 7.1 %collective-permute-start.11 = (f32[128,128]{1,0:T(8,128)S(1)}, f32[128,128]{1,0:T(8,128)S(1)}, u32[]{:S(2)}, u32[]{:S(2)}) collective-permute-start(f32[128,128]{1,0:T(8,128)S(1)} %get-tuple-element.57), channel_id=1, source_target_pairs={{4,8},{8,4},{12,16},{16,12},{20,24},{24,20},{5,9},{9,5},{13,17},{1... | collective-permute-start | bytes 196616 | tf_op jit(solution)/shard_map/ppermute | solution.py:27

commit v5 on v4

--- a/solution.py
+++ b/solution.py
@@ -46,6 +46,10 @@
     return jax.ShapeDtypeStruct(dims, dtype)
 
 
+def is_odd(axis):
+    return lax.axis_index(axis) % 2 == 1
+
+
 def spread_cover(cover):
     lane = iota((8, LANES), 1) // CY
     row = jnp.zeros((8, LANES), F32)
@@ -54,7 +58,7 @@
     return row
 
 
-def y_pack(flag, cover_hbm, est_hbm, op1, op2, cover, est, sems):
+def y_pack(cover_hbm, est_hbm, op1, op2, w_own, cover, est, sems):
     copies = (
         pltpu.make_async_copy(est_hbm, est, sems.at[0]),
         pltpu.make_async_copy(cover_hbm, cover, sems.at[1]),
@@ -63,7 +67,7 @@
         copy.start()
     for copy in copies:
         copy.wait()
-    odd = flag[1] == 1
+    odd = is_odd("by")
     for i in range(CX):
         low, high = est[i, :R], est[i, CY - R :]
         op1[i * R : (i + 1) * R, :] = jnp.where(odd, low, high)
@@ -71,10 +75,13 @@
     row = spread_cover(cover)
     op1[CX * R :, :] = row
     op2[CX * R :, :] = row
-
-
-def x_pack(flag, cover, est, y1, y2, field, ws, op1, op2):
-    odd_x, odd_y = flag[0] == 1, flag[1] == 1
+    for v in range(V):
+        w_own[v : v + 1, :] = jnp.full((1, LANES), cover[v].astype(F32), F32)
+    w_own[V:, :] = row
+
+
+def x_pack(w_own, est, y1, y2, field, ws, op1, op2):
+    odd_x, odd_y = is_odd("bx"), is_odd("by")
     one, two = y1[...], y2[...]
     below, above = jnp.where(odd_y, one, two), jnp.where(odd_y, two, one)
     cells = CX * R
@@ -83,7 +90,7 @@
     field[:, R + CY :] = above[:cells].reshape(CX, R, LANES)
     ws[...] = jnp.zeros_like(ws)
     ws[:1] = below[cells : cells + 1]
-    ws[1:2] = spread_cover(cover)[:1]
+    ws[1:2] = w_own[V : V + 1, :]
     ws[2:3] = above[cells : cells + 1]
     for a in range(R):
         low, high = field[a], field[CX - R + a]
@@ -93,8 +100,8 @@
     op2[R * EY :, :] = ws[...]
 
 
-def z_pack(flag, fy, wy, x1, x2, field, ws, op1, op2):
-    odd_x, odd_z = flag[0] == 1, flag[2] == 1
+def z_pack(fy, wy, x1, x2, field, ws, op1, op2):
+    odd_x, odd_z = is_odd("bx"), is_odd("bz")
     one, two = x1[...], x2[...]
     below, above = jnp.where(odd_x, one, two), jnp.where(odd_x, two, one)
     cells = R * EY
@@ -111,8 +118,8 @@
     op2[...] = jnp.where(odd_z, high, low)
 
 
-def image_pack(flag, observed, op1, op2):
-    odd = flag[2] == 1
+def image_pack(observed, op1, op2):
+    odd = is_odd("bz")
     for v in range(V):
         turned = jnp.transpose(observed[v].reshape(CX * CY, LANES))
         low, high = turned[:R], turned[CZ - R :]
@@ -147,7 +154,7 @@
     return 1.0 / jnp.full((8, LANES), total, F32)[:1]
 
 
-def bands(taps, by, byt, wz1, wz2, tz1, tz2, tz3, tx):
+def bands(taps, by, byt, wz1, wz2, tz1, tz2, tz3, tx, tap_rows):
     for v in range(V):
         rows = slice(v * CY, (v + 1) * CY)
         scale = inverse_sum(taps, v, 0) * inverse_sum(taps, v, 1)
@@ -174,6 +181,9 @@
             row = jnp.where(owner == v, taps[v, 0, k], row)
         tx[k : k + 1, :] = row[:1]
     tx[K:, :] = jnp.zeros((24 - K, LANES), F32)
+    for v in range(V):
+        for k in range(K):
+            tap_rows[v, k : k + 1, :] = jnp.full((1, LANES), taps[v, 0, k], F32)
 
     wz1[...] = jnp.zeros_like(wz1)
     wz2[...] = jnp.zeros_like(wz2)
@@ -233,11 +243,11 @@
 
 
 def main_kernel(
-    flag, taps, cover, field, w9, z1, z2, i1, i2, observed, by, byt, wz1, wz2, tz1, tz2, tz3, tx,
+    field, w9, z1, z2, i1, i2, observed, w_own, by, byt, wz1, wz2, tz1, tz2, tz3, tx, tap_rows,
     mid, op1, op2, sums,
     et, image_e, gs, hs, hp, xs, xe, pe, ys, wy, part,
 ):
-    odd_x, odd_z = flag[0] == 1, flag[2] == 1
+    odd_x, odd_z = is_odd("bx"), is_odd("bz")
     one, two = z1[...], z2[...]
     below, above = jnp.where(odd_z, one, two), jnp.where(odd_z, two, one)
     e = jnp.concatenate([below, above], axis=0)
@@ -310,8 +320,8 @@
     seen = jnp.zeros((8, LANES), F32)
     packed = pe[...].reshape(EX * CY, 2 * LANES)
     for v in range(V):
-        t = [taps[v, 0, k] for k in range(K)]
-        own = cover[v].astype(F32)
+        t = [tap_rows[v, k : k + 1, :] for k in range(K)]
+        own = w_own[v : v + 1, :]
         for b in range(0, CY, 8):
             rows = slice(b, b + 8)
             for a in range(CX):
@@ -374,8 +384,8 @@
         sums[p] = both
 
 
-def x_add(flag, part, r1, r2, mid, op1, op2):
-    odd_x, odd_y = flag[0] == 1, flag[1] == 1
+def x_add(part, r1, r2, mid, op1, op2):
+    odd_x, odd_y = is_odd("bx"), is_odd("by")
     for a in range(CX):
         rows = slice((a % R) * EY, (a % R + 1) * EY)
         one, two = r1[rows, :], r2[rows, :]
@@ -386,13 +396,13 @@
         op2[a * R : (a + 1) * R, :] = jnp.where(odd_y, high, low)
 
 
-def y_add(flag, cover, part, r1, r2, est, sums, out):
-    odd = flag[1] == 1
+def y_add(w9, part, r1, r2, est, sums, out):
+    odd = is_odd("by")
     gathered = jnp.sum(sums[...], axis=0)[:1]
     lane = iota((1, LANES), 1)
     target = jnp.sum(jnp.where(lane == 0, gathered, 0.0), axis=1, keepdims=True)
     total = jnp.sum(jnp.where(lane == 64, gathered, 0.0), axis=1, keepdims=True)
-    count = jnp.sum(spread_cover(cover)[:1], axis=1, keepdims=True) * (1.0 / CY)
+    count = jnp.sum(w9[4:5, :], axis=1, keepdims=True) * (1.0 / CY)
     by = jnp.broadcast_to(target / total / count, (8, LANES))
     for a in range(CX):
         one, two = r1[a * R : (a + 1) * R, :], r2[a * R : (a + 1) * R, :]
@@ -401,27 +411,25 @@
 
 
 def on_device(estimate, observed, coverage, psf_taps):
-    flag = jnp.stack([lax.axis_index(axis) % 2 for axis in ALL]).astype(jnp.int32)
     cover = coverage.reshape(V)
     peers = lax.axis_size(ALL)
 
     op = shape(R * CX + 8, LANES)
-    y1, y2 = kernel_call(
+    y1, y2, w_own = kernel_call(
         y_pack,
-        (op, op),
+        (op, op, shape(V + 8, LANES)),
         scratch=(
             pltpu.SMEM((V,), jnp.int32),
             pltpu.VMEM((CX, CY, CZ), F32),
             pltpu.SemaphoreType.DMA((2,)),
         ),
-        n_in=3,
-        in_smem=1,
+        n_in=2,
         in_hbm=2,
         mib=60,
-    )(flag, cover, estimate)
+    )(cover, estimate)
     y1, y2 = swap(y1, y2, "by")
     op = shape(V * R, CX * CY)
-    i1, i2 = kernel_call(image_pack, (op, op), n_in=2, in_smem=1, flops=10**7)(flag, observed)
+    i1, i2 = kernel_call(image_pack, (op, op), n_in=1, flops=10**7)(observed)
     i1, i2 = swap(i1, i2, "bz")
     square = shape(V, 2 * LANES, LANES, dtype=BF16)
     wide = shape(V, 2 * LANES, 2 * LANES, dtype=BF16)
@@ -436,6 +444,7 @@
             square,
             square,
             shape(24, LANES),
+            shape(V, 24, LANES),
         ),
         n_in=1,
         in_smem=1,
@@ -443,13 +452,13 @@
     )(psf_taps)
     op = shape(EY * R + 8, LANES)
     fy, wy, x1, x2 = kernel_call(
-        x_pack, (shape(CX, EY, LANES), shape(8, LANES), op, op), n_in=5, in_smem=2
-    )(flag, cover, estimate, y1, y2)
+        x_pack, (shape(CX, EY, LANES), shape(8, LANES), op, op), n_in=4
+    )(w_own, estimate, y1, y2)
     x1, x2 = swap(x1, x2, "bx")
     op = shape(2 * R, ROWS)
     field, w9, z1, z2 = kernel_call(
-        z_pack, (shape(EX, EY, LANES), shape(16, LANES), op, op), n_in=5, in_smem=1
-    )(flag, fy, wy, x1, x2)
+        z_pack, (shape(EX, EY, LANES), shape(16, LANES), op, op), n_in=4
+    )(fy, wy, x1, x2)
     z1, z2 = swap(z1, z2, "bz")
 
     op = shape(EY * R, LANES)
@@ -469,21 +478,20 @@
             pltpu.VMEM((3, EY, 3 * LANES), F32),
             pltpu.VMEM((EX, EY, LANES), F32),
         ),
-        n_in=18,
-        in_smem=3,
+        n_in=17,
         mib=30,
         flops=2 * 10**9,
-    )(flag, psf_taps, cover, field, w9, z1, z2, i1, i2, observed, *tables)
+    )(field, w9, z1, z2, i1, i2, observed, w_own, *tables)
 
     x1, x2 = swap(x1, x2, "bx")
     sums = lax.all_to_all(sums, ALL, 0, 0)
     op = shape(R * CX, LANES)
-    part, y1, y2 = kernel_call(x_add, (shape(CX, CY, LANES), op, op), n_in=4, in_smem=1)(
-        flag, part, x1, x2
+    part, y1, y2 = kernel_call(x_add, (shape(CX, CY, LANES), op, op), n_in=3)(
+        part, x1, x2
     )
     y1, y2 = swap(y1, y2, "by")
-    return kernel_call(y_add, shape(CX, CY, LANES), n_in=7, in_smem=2)(
-        flag, cover, part, y1, y2, estimate, sums
+    return kernel_call(y_add, shape(CX, CY, LANES), n_in=6)(
+        w9, part, y1, y2, estimate, sums
     )
 
 

time: 67.3 us -> 64.8 us (0.963)
  Pallas kernels: 17.9 us -> 14 us
  local copies, waits for them, and re-layouts: 1.25 us -> 2.62 us
    pallas_call x5, Pallas kernels: 5.73 us -> 2.98 us  [the longest x1 1.68 us: on_device(): kernel_call(y_pack, (op, op, shape(V + 8, LANES)), scratch=(pltpu.SMEM((V...]
    unnamed x13, local copies, waits for them, and re-layouts: 1.25 us -> 2.62 us
  transfers between devices with their start and end apart: 13 -> 13, of which waited for: 3 -> 3; matrix products, arithmetic and copies ran while one was open for 0% -> 0% of each run, Pallas kernels for 8% -> 6%
where the time goes in v5:
time: 64.8 us; the launch traced here: 63.9 us
  starting transfers between devices  34.8 us (54%)
  Pallas kernels  14 us (22%)
  waiting for transfers between devices  12.3 us (19%)
  local copies, waits for them, and re-layouts  2.62 us (4%)
    ppermute x6, starting transfers between devices, swap(): lax.ppermute(two, axis, pairs(count, 1))  21.5 us
    ppermute x6, waiting for transfers between devices, swap(): lax.ppermute(two, axis, pairs(count, 1))  12.2 us
    all_to_all x1, starting transfers between devices, on_device(): sums = lax.all_to_all(sums, ALL, 0, 0)  8.21 us
    pallas_call x1, Pallas kernels, on_device(): kernel_call(main_kernel, (shape(CX, EY, LANES), op, op, shape(peers, 4, L...  7.54 us
    ppermute x6, starting transfers between devices, swap(): lax.ppermute(one, axis, pairs(count, 0))  5.06 us
    pallas_call x1, Pallas kernels, on_device(): kernel_call(bands, (shape(V * CY, LANES, dtype=BF16), shape(2 * EY, LANES...  3.26 us
    unnamed x13, local copies, waits for them, and re-layouts  2.62 us
    pallas_call x1, Pallas kernels, on_device(): kernel_call(y_pack, (op, op, shape(V + 8, LANES)), scratch=(pltpu.SMEM((V...  1.68 us
  transfers between devices with their start and end apart: 13, of which 3 were waited for; matrix products, arithmetic and copies ran while one was open for 0% of the time, Pallas kernels for 6%

profile of v5, /device:TPU:41, one launch (start us, length us, event | category | flops | bytes accessed | tf_op | source)
XLA Modules:
  0.0 63.9 jit_solution(44558847180071270)
XLA Ops:
  0.0 0.0 copy-start
  0.0 1.7 %shard_map.46 = (f32[136,128]{1,0:T(8,128)}, f32[136,128]{1,0:T(8,128)}, f32[16,128]{1,0:T(8,128)}) custom-call(s32[8]{0:T(128)} %bitcast.1, f32[16,16,128]{2,1,0:T(8,128)} %est.3), custom_call_target="tpu_custom_call" | custom-call | bytes 1024 | tf_op jit(solution)/shard_map/pallas_call | solution.py:418
  1.7 1.3 %collective-permute-start = (f32[136,128]{1,0:T(8,128)}, f32[136,128]{1,0:T(8,128)S(1)}, u32[]{:S(2)}, u32[]{:S(2)}) collective-permute-start(f32[136,128]{1,0:T(8,128)} %get-tuple-element.35), channel_id=1, source_target_pairs={{0,4},{4,0},{8,12},{12,8},{16,20},{20,16},{24,28},{28,24},{1,5},{5... | collective-permute-start | bytes 208904 | tf_op jit(solution)/shard_map/ppermute | solution.py:27
  3.0 3.3 %collective-permute-start.1 = (f32[136,128]{1,0:T(8,128)}, f32[136,128]{1,0:T(8,128)S(1)}, u32[]{:S(2)}, u32[]{:S(2)}) collective-permute-start(f32[136,128]{1,0:T(8,128)} %get-tuple-element.36), channel_id=1, source_target_pairs={{4,8},{8,4},{12,16},{16,12},{20,24},{24,20},{5,9},{9,5},{13,17},{1... | collective-permute-start | bytes 208904 | tf_op jit(solution)/shard_map/ppermute | solution.py:27
  6.2 0.0 collective-permute-done.y1
  6.3 4.1 %collective-permute-done.1.y2 = f32[136,128]{1,0:T(8,128)S(1)} collective-permute-done((f32[136,128]{1,0:T(8,128)}, f32[136,128]{1,0:T(8,128)S(1)}, u32[]{:S(2)}, u32[]{:S(2)}) %collective-permute-start.1) | collective-permute-done | bytes 69664 | tf_op jit(solution)/shard_map/ppermute | solution.py:27
  10.3 0.0 copy-done
  10.3 0.0 copy-start.3
  10.3 0.7 %copy-done.3 = f32[16,128]{1,0:T(8,128)S(1)} copy-done((f32[16,128]{1,0:T(8,128)S(1)}, f32[16,128]{1,0:T(8,128)}, u32[]{:S(2)}) %copy-start.3) | copy-done | bytes 8216
  11.1 2.2 %collective-permute-start.2 = (f32[264,128]{1,0:T(8,128)S(1)}, f32[264,128]{1,0:T(8,128)S(1)}, u32[]{:S(2)}, u32[]{:S(2)}) collective-permute-start(f32[264,128]{1,0:T(8,128)S(1)} %get-tuple-element.39), channel_id=1, source_target_pairs={{0,32},{32,0},{64,96},{96,64},{1,33},{33,1},{65,97},{97,65},{2,34}... | collective-permute-start | bytes 405512 | tf_op jit(solution)/shard_map/ppermute | solution.py:27
  13.3 4.6 %collective-permute-start.3 = (f32[264,128]{1,0:T(8,128)S(1)}, f32[264,128]{1,0:T(8,128)S(1)}, u32[]{:S(2)}, u32[]{:S(2)}) collective-permute-start(f32[264,128]{1,0:T(8,128)S(1)} %get-tuple-element.40), channel_id=1, source_target_pairs={{32,64},{64,32},{33,65},{65,33},{34,66},{66,34},{35,67},{67,35},{3... | collective-permute-start | bytes 405512 | tf_op jit(solution)/shard_map/ppermute | solution.py:27
  17.9 0.0 copy-start.1
  17.9 1.2 %copy-done.1 = f32[8,16,16,128]{3,2,1,0:T(8,128)S(1)} copy-done((f32[8,16,16,128]{3,2,1,0:T(8,128)S(1)}, f32[8,16,16,128]{3,2,1,0:T(8,128)}, u32[]{:S(2)}) %copy-start.1) | copy-done | bytes 1048600
  19.1 0.0 copy-start.2
  19.1 0.3 shard_map.49
  19.5 0.2 collective-permute-start.6
  19.7 4.0 %collective-permute-start.7 = (f32[64,256]{1,0:T(8,128)S(1)}, f32[64,256]{1,0:T(8,128)S(1)}, u32[]{:S(2)}, u32[]{:S(2)}) collective-permute-start(f32[64,256]{1,0:T(8,128)S(1)} %get-tuple-element.46), channel_id=1, source_target_pairs={{1,2},{2,1},{5,6},{6,5},{9,10},{10,9},{13,14},{14,13},{17,18},{18,... | collective-permute-start | bytes 196616 | tf_op jit(solution)/shard_map/ppermute | solution.py:27
  23.7 0.0 collective-permute-done.2.x1
  23.8 0.0 collective-permute-done.3.x2
  23.8 0.0 copy-start.5
  23.8 0.2 shard_map.48
  24.0 0.1 collective-permute-start.4
  24.1 1.9 %collective-permute-start.5 = (f32[16,1024]{1,0:T(8,128)S(1)}, f32[16,1024]{1,0:T(8,128)S(1)}, u32[]{:S(2)}, u32[]{:S(2)}) collective-permute-start(f32[16,1024]{1,0:T(8,128)S(1)} %get-tuple-element.44), channel_id=1, source_target_pairs={{1,2},{2,1},{5,6},{6,5},{9,10},{10,9},{13,14},{14,13},{17,18},{18,... | collective-permute-start | bytes 196616 | tf_op jit(solution)/shard_map/ppermute | solution.py:27
  26.0 0.0 copy-done.5
  26.1 3.3 %shard_map.50 = (bf16[128,128]{1,0:T(8,128)(2,1)S(1)}, f32[64,128]{1,0:T(8,128)S(1)}, bf16[8,256,256]{2,1,0:T(8,128)(2,1)S(1)}, bf16[8,256,256]{2,1,0:T(8,128)(2...) custom-call(f32[8,3,17]{2,1,0:T(4,128)S(1)} %copy.5.taps), custom_call_target="tpu_custom_call" | custom-call | flops 200000000 | bytes 1024 | tf_op jit(solution)/shard_map/pallas_call | solution.py:436
  29.3 0.0 collective-permute-done.6.i1
  29.3 0.0 collective-permute-done.7.i2
  29.3 0.0 collective-permute-done.4.z1
  29.3 0.0 collective-permute-done.5.z2
  29.4 0.0 copy-start.4
  29.4 0.0 copy-done.2
  29.4 0.7 %copy-done.4 = f32[16,128]{1,0:T(8,128)S(1)} copy-done((f32[16,128]{1,0:T(8,128)S(1)}, f32[16,128]{1,0:T(8,128)}, u32[]{:S(2)}) %copy-start.4) | copy-done | bytes 8216
  30.1 7.5 %shard_map.51 = (f32[16,32,128]{2,1,0:T(8,128)S(1)}, f32[256,128]{1,0:T(8,128)S(1)}, f32[256,128]{1,0:T(8,128)S(1)}, f32[128,4,128]{2,1,0:T(4,128)}) custom-call(f32[32,32,128]{2,1,0:T(8,128)S(1)} %get-tuple-element.42.field, f32[16,128]{1,0:T(8,128)S(1)} %get-tuple-element.41.w9, f32[16,1024]{1,0:T(8,128)S(1)} %collective-permute-done.4.z1, ...), custom_call_target="tpu_custom_call" | custom-call | flops 2000000000 | bytes 1024 | tf_op jit(solution)/shard_map/pallas_call | solution.py:465
  37.6 8.2 %all-to-all-start = ((f32[128,4,128]{2,1,0:T(4,128)}), f32[128,4,128]{2,1,0:T(4,128)S(1)}, u32[]{:S(2)}, u32[]{:S(2)}) async-start(f32[128,4,128]{2,1,0:T(4,128)} %get-tuple-element.62), calls=%async_computation | async-start | bytes 524288 | tf_op jit(solution)/shard_map/all_to_all | solution.py:487
  45.8 0.5 collective-permute-start.8
  46.3 4.2 %collective-permute-start.9 = (f32[256,128]{1,0:T(8,128)S(1)}, f32[256,128]{1,0:T(8,128)S(1)}, u32[]{:S(2)}, u32[]{:S(2)}) collective-permute-start(f32[256,128]{1,0:T(8,128)S(1)} %get-tuple-element.58), channel_id=1, source_target_pairs={{32,64},{64,32},{33,65},{65,33},{34,66},{66,34},{35,67},{67,35},{3... | collective-permute-start | bytes 393224 | tf_op jit(solution)/shard_map/ppermute | solution.py:27
  50.5 0.0 collective-permute-done.8.r1
  50.5 4.6 %collective-permute-done.9.r2 = f32[256,128]{1,0:T(8,128)S(1)} collective-permute-done((f32[256,128]{1,0:T(8,128)S(1)}, f32[256,128]{1,0:T(8,128)S(1)}, u32[]{:S(2)}, u32[]{:S(2)}) %collective-permute-start.9) | collective-permute-done | bytes 131104 | tf_op jit(solution)/shard_map/ppermute | solution.py:27
  55.1 0.8 %collective-permute-start.10 = (f32[128,128]{1,0:T(8,128)S(1)}, f32[128,128]{1,0:T(8,128)S(1)}, u32[]{:S(2)}, u32[]{:S(2)}) collective-permute-start(f32[128,128]{1,0:T(8,128)S(1)} %get-tuple-element.60), channel_id=1, source_target_pairs={{0,4},{4,0},{8,12},{12,8},{16,20},{20,16},{24,28},{28,24},{1,5},{5... | collective-permute-start | bytes 196616 | tf_op jit(solution)/shard_map/ppermute | solution.py:27
  55.9 3.5 %collective-permute-start.11 = (f32[128,128]{1,0:T(8,128)S(1)}, f32[128,128]{1,0:T(8,128)S(1)}, u32[]{:S(2)}, u32[]{:S(2)}) collective-permute-start(f32[128,128]{1,0:T(8,128)S(1)} %get-tuple-element.61), channel_id=1, source_target_pairs={{4,8},{8,4},{12,16},{16,12},{20,24},{24,20},{5,9},{9,5},{13,17},{1... | collective-permute-start | bytes 196616 | tf_op jit(solution)/shard_map/ppermute | solution.py:27
  59.4 0.0 collective-permute-done.10.r1
  59.4 3.6 %collective-permute-done.11.r2 = f32[128,128]{1,0:T(8,128)S(1)} collective-permute-done((f32[128,128]{1,0:T(8,128)S(1)}, f32[128,128]{1,0:T(8,128)S(1)}, u32[]{:S(2)}, u32[]{:S(2)}) %collective-permute-start.11) | collective-permute-done | bytes 65568 | tf_op jit(solution)/shard_map/ppermute | solution.py:27
  63.0 0.0 all-to-all-done.sums
  63.0 0.9 %shard_map.53 = f32[16,16,128]{2,1,0:T(8,128)} custom-call(f32[16,128]{1,0:T(8,128)S(1)} %get-tuple-element.41.w9, f32[16,16,128]{2,1,0:T(8,128)S(1)} %get-tuple-element.59.part, f32[128,128]{1,0:T(8,128)S(1)} %collective-permute-done.10.r1, f32[128,128]{1,0:T(8,128)S(1)} %collective-permute-done.11.r2, f32[16,16,128]{2,1,0:T(8,128)S(1)} %copy-done, ...), custom_call_target="tpu_custom_call" | custom-call | bytes 1024 | tf_op jit(solution)/shard_map/pallas_call | solution.py:493
  (3 shorter events, 0.1 us)
Async XLA Ops:
  0.0 10.3 %copy-start = (f32[16,16,128]{2,1,0:T(8,128)S(1)}, f32[16,16,128]{2,1,0:T(8,128)}, u32[]{:S(2)}) copy-start(f32[16,16,128]{2,1,0:T(8,128)} %est.3) | copy-start | bytes 393220
  1.7 4.6 %collective-permute-start = (f32[136,128]{1,0:T(8,128)}, f32[136,128]{1,0:T(8,128)S(1)}, u32[]{:S(2)}, u32[]{:S(2)}) collective-permute-start(f32[136,128]{1,0:T(8,128)} %get-tuple-element.35), channel_id=1, source_target_pairs={{0,4},{4,0},{8,12},{12,8},{16,20},{20,16},{24,28},{28,24},{1,5},{5... | collective-permute-start | bytes 208904 | tf_op jit(solution)/shard_map/ppermute | solution.py:27
  3.0 7.4 %collective-permute-start.1 = (f32[136,128]{1,0:T(8,128)}, f32[136,128]{1,0:T(8,128)S(1)}, u32[]{:S(2)}, u32[]{:S(2)}) collective-permute-start(f32[136,128]{1,0:T(8,128)} %get-tuple-element.36), channel_id=1, source_target_pairs={{4,8},{8,4},{12,16},{16,12},{20,24},{24,20},{5,9},{9,5},{13,17},{1... | collective-permute-start | bytes 208904 | tf_op jit(solution)/shard_map/ppermute | solution.py:27
  10.3 0.7 %copy-start.3 = (f32[16,128]{1,0:T(8,128)S(1)}, f32[16,128]{1,0:T(8,128)}, u32[]{:S(2)}) copy-start(f32[16,128]{1,0:T(8,128)} %get-tuple-element.34.w_own) | copy-start | bytes 24580
  11.1 12.7 %collective-permute-start.2 = (f32[264,128]{1,0:T(8,128)S(1)}, f32[264,128]{1,0:T(8,128)S(1)}, u32[]{:S(2)}, u32[]{:S(2)}) collective-permute-start(f32[264,128]{1,0:T(8,128)S(1)} %get-tuple-element.39), channel_id=1, source_target_pairs={{0,32},{32,0},{64,96},{96,64},{1,33},{33,1},{65,97},{97,65},{2,34}... | collective-permute-start | bytes 405512 | tf_op jit(solution)/shard_map/ppermute | solution.py:27
  13.3 10.5 %collective-permute-start.3 = (f32[264,128]{1,0:T(8,128)S(1)}, f32[264,128]{1,0:T(8,128)S(1)}, u32[]{:S(2)}, u32[]{:S(2)}) collective-permute-start(f32[264,128]{1,0:T(8,128)S(1)} %get-tuple-element.40), channel_id=1, source_target_pairs={{32,64},{64,32},{33,65},{65,33},{34,66},{66,34},{35,67},{67,35},{3... | collective-permute-start | bytes 405512 | tf_op jit(solution)/shard_map/ppermute | solution.py:27
  17.9 1.2 %copy-start.1 = (f32[8,16,16,128]{3,2,1,0:T(8,128)S(1)}, f32[8,16,16,128]{3,2,1,0:T(8,128)}, u32[]{:S(2)}) copy-start(f32[8,16,16,128]{3,2,1,0:T(8,128)} %observed.3) | copy-start | bytes 3145732
  19.1 10.2 %copy-start.2 = (f32[8,16,16,128]{3,2,1,0:T(8,128)S(1)}, f32[8,16,16,128]{3,2,1,0:T(8,128)}, u32[]{:S(2)}) copy-start(f32[8,16,16,128]{3,2,1,0:T(8,128)} %observed.3) | copy-start | bytes 3145732
  19.5 9.9 %collective-permute-start.6 = (f32[64,256]{1,0:T(8,128)S(1)}, f32[64,256]{1,0:T(8,128)S(1)}, u32[]{:S(2)}, u32[]{:S(2)}) collective-permute-start(f32[64,256]{1,0:T(8,128)S(1)} %get-tuple-element.45), channel_id=1, source_target_pairs={{0,1},{1,0},{2,3},{3,2},{4,5},{5,4},{6,7},{7,6},{8,9},{9,8},{10,11... | collective-permute-start | bytes 196616 | tf_op jit(solution)/shard_map/ppermute | solution.py:27
  19.7 9.6 %collective-permute-start.7 = (f32[64,256]{1,0:T(8,128)S(1)}, f32[64,256]{1,0:T(8,128)S(1)}, u32[]{:S(2)}, u32[]{:S(2)}) collective-permute-start(f32[64,256]{1,0:T(8,128)S(1)} %get-tuple-element.46), channel_id=1, source_target_pairs={{1,2},{2,1},{5,6},{6,5},{9,10},{10,9},{13,14},{14,13},{17,18},{18,... | collective-permute-start | bytes 196616 | tf_op jit(solution)/shard_map/ppermute | solution.py:27
  23.8 2.3 %copy-start.5 = (f32[8,3,17]{2,0,1:T(8,128)S(1)}, f32[8,3,17]{2,0,1:T(8,128)}, u32[]{:S(2)}) copy-start(f32[8,3,17]{2,0,1:T(8,128)} %param.7) | copy-start | bytes 4900
  24.0 5.3 %collective-permute-start.4 = (f32[16,1024]{1,0:T(8,128)S(1)}, f32[16,1024]{1,0:T(8,128)S(1)}, u32[]{:S(2)}, u32[]{:S(2)}) collective-permute-start(f32[16,1024]{1,0:T(8,128)S(1)} %get-tuple-element.43), channel_id=1, source_target_pairs={{0,1},{1,0},{2,3},{3,2},{4,5},{5,4},{6,7},{7,6},{8,9},{9,8},{10,11... | collective-permute-start | bytes 196616 | tf_op jit(solution)/shard_map/ppermute | solution.py:27
  24.1 5.2 %collective-permute-start.5 = (f32[16,1024]{1,0:T(8,128)S(1)}, f32[16,1024]{1,0:T(8,128)S(1)}, u32[]{:S(2)}, u32[]{:S(2)}) collective-permute-start(f32[16,1024]{1,0:T(8,128)S(1)} %get-tuple-element.44), channel_id=1, source_target_pairs={{1,2},{2,1},{5,6},{6,5},{9,10},{10,9},{13,14},{14,13},{17,18},{18,... | collective-permute-start | bytes 196616 | tf_op jit(solution)/shard_map/ppermute | solution.py:27
  29.4 0.7 %copy-start.4 = (f32[16,128]{1,0:T(8,128)S(1)}, f32[16,128]{1,0:T(8,128)}, u32[]{:S(2)}) copy-start(f32[16,128]{1,0:T(8,128)} %get-tuple-element.34.w_own) | copy-start | bytes 24580
  37.6 25.4 %all-to-all-start = ((f32[128,4,128]{2,1,0:T(4,128)}), f32[128,4,128]{2,1,0:T(4,128)S(1)}, u32[]{:S(2)}, u32[]{:S(2)}) async-start(f32[128,4,128]{2,1,0:T(4,128)} %get-tuple-element.62), calls=%async_computation | async-start | bytes 524288 | tf_op jit(solution)/shard_map/all_to_all | solution.py:487
  45.8 4.7 %collective-permute-start.8 = (f32[256,128]{1,0:T(8,128)S(1)}, f32[256,128]{1,0:T(8,128)S(1)}, u32[]{:S(2)}, u32[]{:S(2)}) collective-permute-start(f32[256,128]{1,0:T(8,128)S(1)} %get-tuple-element.57), channel_id=1, source_target_pairs={{0,32},{32,0},{64,96},{96,64},{1,33},{33,1},{65,97},{97,65},{2,34}... | collective-permute-start | bytes 393224 | tf_op jit(solution)/shard_map/ppermute | solution.py:27
  46.3 8.8 %collective-permute-start.9 = (f32[256,128]{1,0:T(8,128)S(1)}, f32[256,128]{1,0:T(8,128)S(1)}, u32[]{:S(2)}, u32[]{:S(2)}) collective-permute-start(f32[256,128]{1,0:T(8,128)S(1)} %get-tuple-element.58), channel_id=1, source_target_pairs={{32,64},{64,32},{33,65},{65,33},{34,66},{66,34},{35,67},{67,35},{3... | collective-permute-start | bytes 393224 | tf_op jit(solution)/shard_map/ppermute | solution.py:27
  55.1 4.3 %collective-permute-start.10 = (f32[128,128]{1,0:T(8,128)S(1)}, f32[128,128]{1,0:T(8,128)S(1)}, u32[]{:S(2)}, u32[]{:S(2)}) collective-permute-start(f32[128,128]{1,0:T(8,128)S(1)} %get-tuple-element.60), channel_id=1, source_target_pairs={{0,4},{4,0},{8,12},{12,8},{16,20},{20,16},{24,28},{28,24},{1,5},{5... | collective-permute-start | bytes 196616 | tf_op jit(solution)/shard_map/ppermute | solution.py:27
  55.9 7.1 %collective-permute-start.11 = (f32[128,128]{1,0:T(8,128)S(1)}, f32[128,128]{1,0:T(8,128)S(1)}, u32[]{:S(2)}, u32[]{:S(2)}) collective-permute-start(f32[128,128]{1,0:T(8,128)S(1)} %get-tuple-element.61), channel_id=1, source_target_pairs={{4,8},{8,4},{12,16},{16,12},{20,24},{24,20},{5,9},{9,5},{13,17},{1... | collective-permute-start | bytes 196616 | tf_op jit(solution)/shard_map/ppermute | solution.py:27

commit v6 on v5

--- a/solution.py
+++ b/solution.py
@@ -154,7 +154,7 @@
     return 1.0 / jnp.full((8, LANES), total, F32)[:1]
 
 
-def bands(taps, by, byt, wz1, wz2, tz1, tz2, tz3, tx, tap_rows):
+def bands(taps, by, byt, wz1, wz2):
     for v in range(V):
         rows = slice(v * CY, (v + 1) * CY)
         scale = inverse_sum(taps, v, 0) * inverse_sum(taps, v, 1)
@@ -174,43 +174,25 @@
     byt[:EY, :] = high.astype(F32)
     byt[EY:, :] = low.astype(F32)
 
-    owner = iota((8, LANES), 1) // (2 * R)
-    for k in range(K):
-        row = jnp.zeros((8, LANES), F32)
-        for v in range(V):
-            row = jnp.where(owner == v, taps[v, 0, k], row)
-        tx[k : k + 1, :] = row[:1]
-    tx[K:, :] = jnp.zeros((24 - K, LANES), F32)
-    for v in range(V):
-        for k in range(K):
-            tap_rows[v, k : k + 1, :] = jnp.full((1, LANES), taps[v, 0, k], F32)
-
-    wz1[...] = jnp.zeros_like(wz1)
-    wz2[...] = jnp.zeros_like(wz2)
-    tz2[...] = jnp.zeros_like(tz2)
-    tz3[...] = jnp.zeros_like(tz3)
+    wz1[:, :, LANES:] = jnp.zeros((V, 2 * LANES, LANES), BF16)
+    wz2[:, :LANES, LANES:] = jnp.zeros((V, LANES, LANES), BF16)
+    wz2[:, LANES + 12 * R :, :] = jnp.zeros((V, LANES - 12 * R, 2 * LANES), BF16)
     row, col = iota((LANES, LANES), 0), iota((LANES, LANES), 1)
-    short_row, short_col = row[: 2 * R], col[: 2 * R]
+    short_row = row[: 2 * R]
     end = row[: 4 * R]
     z_end = jnp.where(end < 2 * R, end - 2 * R, end - 2 * R + CZ)
     near_row = jnp.where(short_row < R, short_row, short_row - 2 * R + CZ)
-    slot_row = jnp.where(short_row < R, short_row - R, short_row - R + CZ)
 
     def z_of(v, carry):
         scale = inverse_sum(taps, v, 2)
-        place = short_col[:1] - 2 * R * v
+        place = col[:1] - 2 * R * v
         z = jnp.where(place < R, place - R, place - R + CZ)
         slot_col = jnp.where((place >= 0) & (place < 2 * R), z, 4 * CZ)
 
-        middle = pick(taps, v, 2, row - col + R, scale)
-        high, low = split(middle)
+        high, low = split(pick(taps, v, 2, row - col + R, scale))
         wz1[v, :LANES, :LANES] = high
         wz1[v, LANES:, :LANES] = high
         wz2[v, :LANES, :LANES] = low
-        high, low = split(jnp.transpose(middle))
-        tz1[v, :LANES, :] = high
-        tz1[v, LANES:, :] = high
-        tz2[v, :LANES, :] = low
 
         near = pick(taps, v, 2, near_row - slot_col + R, scale)
         zeros = jnp.zeros((R, LANES), F32)
@@ -228,7 +210,32 @@
             wz2[v, LANES : LANES + 4 * R, half] = high
             wz2[v, LANES + 4 * R : LANES + 8 * R, half] = high
             wz2[v, LANES + 8 * R : LANES + 12 * R, half] = low
-
+        return carry
+
+    lax.fori_loop(0, V, z_of, 0)
+
+
+def bands_back(taps, tz1, tz2, tz3, tx, tap_rows):
+    owner = iota((8, LANES), 1) // (2 * R)
+    for k in range(K):
+        mixed = jnp.zeros((8, LANES), F32)
+        for v in range(V):
+            mixed = jnp.where(owner == v, taps[v, 0, k], mixed)
+            tap_rows[v, k : k + 1, :] = jnp.full((1, LANES), taps[v, 0, k], F32)
+        tx[k : k + 1, :] = mixed[:1]
+    tx[K:, :] = jnp.zeros((24 - K, LANES), F32)
+    tz2[:, LANES:, :] = jnp.zeros((V, LANES, LANES), BF16)
+    tz3[...] = jnp.zeros_like(tz3)
+    row, col = iota((LANES, LANES), 0), iota((LANES, LANES), 1)
+    short_row, short_col = row[: 2 * R], col[: 2 * R]
+    slot_row = jnp.where(short_row < R, short_row - R, short_row - R + CZ)
+
+    def z_of(v, carry):
+        scale = inverse_sum(taps, v, 2)
+        high, low = split(pick(taps, v, 2, col - row + R, scale))
+        tz1[v, :LANES, :] = high
+        tz1[v, LANES:, :] = high
+        tz2[v, :LANES, :] = low
         high, low = split(pick(taps, v, 2, short_col - slot_row + R, scale))
         first = pl.multiple_of(v * 2 * R, 2 * R)
         tz2[v, pl.ds(LANES + first, 2 * R), :] = high
@@ -425,7 +432,7 @@
         ),
         n_in=2,
         in_hbm=2,
-        mib=60,
+        mib=40,
     )(cover, estimate)
     y1, y2 = swap(y1, y2, "by")
     op = shape(V * R, CX * CY)
@@ -435,20 +442,17 @@
     wide = shape(V, 2 * LANES, 2 * LANES, dtype=BF16)
     tables = kernel_call(
         bands,
-        (
-            shape(V * CY, LANES, dtype=BF16),
-            shape(2 * EY, LANES),
-            wide,
-            wide,
-            square,
-            square,
-            square,
-            shape(24, LANES),
-            shape(V, 24, LANES),
-        ),
+        (shape(V * CY, LANES, dtype=BF16), shape(2 * EY, LANES), wide, wide),
         n_in=1,
         in_smem=1,
-        flops=2 * 10**8,
+        flops=10**8,
+    )(psf_taps)
+    turned = kernel_call(
+        bands_back,
+        (square, square, square, shape(24, LANES), shape(V, 24, LANES)),
+        n_in=1,
+        in_smem=1,
+        flops=10**8,
     )(psf_taps)
     op = shape(EY * R + 8, LANES)
     fy, wy, x1, x2 = kernel_call(
@@ -481,7 +485,7 @@
         n_in=17,
         mib=30,
         flops=2 * 10**9,
-    )(field, w9, z1, z2, i1, i2, observed, w_own, *tables)
+    )(field, w9, z1, z2, i1, i2, observed, w_own, *tables, *turned)
 
     x1, x2 = swap(x1, x2, "bx")
     sums = lax.all_to_all(sums, ALL, 0, 0)

time: 64.8 us -> 64 us (0.988)
  starting transfers between devices: 34.8 us -> 33.9 us
    pallas_call x0 -> x1, Pallas kernels: none -> 1.75 us  [on_device(): kernel_call(bands_back, (square, square, square, shape(24, LANES), shape(...]
    pallas_call x1, Pallas kernels: 1.68 us -> 0.72 us  [on_device(): kernel_call(y_pack, (op, op, shape(V + 8, LANES)), scratch=(pltpu.SMEM((V...]
    all_to_all x1, starting transfers between devices: 8.21 us -> 7.32 us  [on_device(): sums = lax.all_to_all(sums, ALL, 0, 0)]
  transfers between devices with their start and end apart: 13 -> 13, of which waited for: 3 -> 3; matrix products, arithmetic and copies ran while one was open for 0% -> 0% of each run, Pallas kernels for 6% -> 8%
where the time goes in v6:
time: 64 us; the launch traced here: 63.2 us
  starting transfers between devices  33.9 us (53%)
  Pallas kernels  14.3 us (22%)
  waiting for transfers between devices  12.1 us (19%)
  local copies, waits for them, and re-layouts  2.8 us (4%)
    ppermute x6, starting transfers between devices, swap(): lax.ppermute(two, axis, pairs(count, 1))  21.5 us
    ppermute x6, waiting for transfers between devices, swap(): lax.ppermute(two, axis, pairs(count, 1))  12 us
    pallas_call x1, Pallas kernels, on_device(): kernel_call(main_kernel, (shape(CX, EY, LANES), op, op, shape(peers, 4, L...  7.63 us
    all_to_all x1, starting transfers between devices, on_device(): sums = lax.all_to_all(sums, ALL, 0, 0)  7.32 us
    ppermute x6, starting transfers between devices, swap(): lax.ppermute(one, axis, pairs(count, 0))  5.06 us
    unnamed x13, local copies, waits for them, and re-layouts  2.8 us
    pallas_call x1, Pallas kernels, on_device(): kernel_call(bands, (shape(V * CY, LANES, dtype=BF16), shape(2 * EY, LANES...  2.64 us
    pallas_call x1, Pallas kernels, on_device(): kernel_call(bands_back, (square, square, square, shape(24, LANES), shape(...  1.75 us
  transfers between devices with their start and end apart: 13, of which 3 were waited for; matrix products, arithmetic and copies ran while one was open for 0% of the time, Pallas kernels for 8%

profile of v6, /device:TPU:41, one launch (start us, length us, event | category | flops | bytes accessed | tf_op | source)
XLA Modules:
  0.0 63.2 jit_solution(10561668359381652543)
XLA Ops:
  0.0 0.0 copy-start.4
  0.0 0.7 %copy-done.4 = s32[8,1,1,1]{0,3,2,1:T(1,128)S(1)} copy-done((s32[8,1,1,1]{0,3,2,1:T(1,128)S(1)}, s32[8,1,1,1]{0,3,2,1:T(1,128)}, u32[]{:S(2)}) %copy-start.4) | copy-done | bytes 56
  0.7 0.0 copy-start
  0.7 0.9 %copy-done = f32[16,16,128]{2,1,0:T(8,128)S(1)} copy-done((f32[16,16,128]{2,1,0:T(8,128)S(1)}, f32[16,16,128]{2,1,0:T(8,128)}, u32[]{:S(2)}) %copy-start) | copy-done | bytes 131096
  1.6 0.7 %shard_map.46 = (f32[136,128]{1,0:T(8,128)S(1)}, f32[136,128]{1,0:T(8,128)S(1)}, f32[16,128]{1,0:T(8,128)S(1)}) custom-call(s32[8]{0:T(128)S(1)} %bitcast.1, f32[16,16,128]{2,1,0:T(8,128)S(1)} %copy-done), custom_call_target="tpu_custom_call" | custom-call | bytes 1024 | tf_op jit(solution)/shard_map/pallas_call | solution.py:425
  2.3 1.3 %collective-permute-start = (f32[136,128]{1,0:T(8,128)S(1)}, f32[136,128]{1,0:T(8,128)S(1)}, u32[]{:S(2)}, u32[]{:S(2)}) collective-permute-start(f32[136,128]{1,0:T(8,128)S(1)} %get-tuple-element.35), channel_id=1, source_target_pairs={{0,4},{4,0},{8,12},{12,8},{16,20},{20,16},{24,28},{28,24},{1,5},{5... | collective-permute-start | bytes 208904 | tf_op jit(solution)/shard_map/ppermute | solution.py:27
  3.6 3.3 %collective-permute-start.1 = (f32[136,128]{1,0:T(8,128)S(1)}, f32[136,128]{1,0:T(8,128)S(1)}, u32[]{:S(2)}, u32[]{:S(2)}) collective-permute-start(f32[136,128]{1,0:T(8,128)S(1)} %get-tuple-element.36), channel_id=1, source_target_pairs={{4,8},{8,4},{12,16},{16,12},{20,24},{24,20},{5,9},{9,5},{13,17},{1... | collective-permute-start | bytes 208904 | tf_op jit(solution)/shard_map/ppermute | solution.py:27
  6.8 0.0 collective-permute-done.y1
  6.9 3.9 %collective-permute-done.1.y2 = f32[136,128]{1,0:T(8,128)S(1)} collective-permute-done((f32[136,128]{1,0:T(8,128)S(1)}, f32[136,128]{1,0:T(8,128)S(1)}, u32[]{:S(2)}, u32[]{:S(2)}) %collective-permute-start.1) | collective-permute-done | bytes 69664 | tf_op jit(solution)/shard_map/ppermute | solution.py:27
  10.8 2.2 %collective-permute-start.2 = (f32[264,128]{1,0:T(8,128)S(1)}, f32[264,128]{1,0:T(8,128)S(1)}, u32[]{:S(2)}, u32[]{:S(2)}) collective-permute-start(f32[264,128]{1,0:T(8,128)S(1)} %get-tuple-element.39), channel_id=1, source_target_pairs={{0,32},{32,0},{64,96},{96,64},{1,33},{33,1},{65,97},{97,65},{2,34}... | collective-permute-start | bytes 405512 | tf_op jit(solution)/shard_map/ppermute | solution.py:27
  13.0 4.6 %collective-permute-start.3 = (f32[264,128]{1,0:T(8,128)S(1)}, f32[264,128]{1,0:T(8,128)S(1)}, u32[]{:S(2)}, u32[]{:S(2)}) collective-permute-start(f32[264,128]{1,0:T(8,128)S(1)} %get-tuple-element.40), channel_id=1, source_target_pairs={{32,64},{64,32},{33,65},{65,33},{34,66},{66,34},{35,67},{67,35},{3... | collective-permute-start | bytes 405512 | tf_op jit(solution)/shard_map/ppermute | solution.py:27
  17.6 0.0 copy-start.2
  17.6 1.2 %copy-done.2 = f32[8,16,16,128]{3,2,1,0:T(8,128)S(1)} copy-done((f32[8,16,16,128]{3,2,1,0:T(8,128)S(1)}, f32[8,16,16,128]{3,2,1,0:T(8,128)}, u32[]{:S(2)}) %copy-start.2) | copy-done | bytes 1048600
  18.8 0.0 copy-start.3
  18.8 0.3 shard_map.49
  19.1 0.2 collective-permute-start.6
  19.4 4.0 %collective-permute-start.7 = (f32[64,256]{1,0:T(8,128)S(1)}, f32[64,256]{1,0:T(8,128)S(1)}, u32[]{:S(2)}, u32[]{:S(2)}) collective-permute-start(f32[64,256]{1,0:T(8,128)S(1)} %get-tuple-element.46), channel_id=1, source_target_pairs={{1,2},{2,1},{5,6},{6,5},{9,10},{10,9},{13,14},{14,13},{17,18},{18,... | collective-permute-start | bytes 196616 | tf_op jit(solution)/shard_map/ppermute | solution.py:27
  23.4 0.0 collective-permute-done.2.x1
  23.4 0.0 collective-permute-done.3.x2
  23.4 0.0 copy-start.5
  23.5 0.2 shard_map.48
  23.7 0.1 collective-permute-start.4
  23.8 1.9 %collective-permute-start.5 = (f32[16,1024]{1,0:T(8,128)S(1)}, f32[16,1024]{1,0:T(8,128)S(1)}, u32[]{:S(2)}, u32[]{:S(2)}) collective-permute-start(f32[16,1024]{1,0:T(8,128)S(1)} %get-tuple-element.44), channel_id=1, source_target_pairs={{1,2},{2,1},{5,6},{6,5},{9,10},{10,9},{13,14},{14,13},{17,18},{18,... | collective-permute-start | bytes 196616 | tf_op jit(solution)/shard_map/ppermute | solution.py:27
  25.7 0.0 copy-done.5
  25.7 1.8 %shard_map.51 = (bf16[8,256,128]{2,1,0:T(8,128)(2,1)S(1)}, bf16[8,256,128]{2,1,0:T(8,128)(2,1)S(1)}, bf16[8,256,128]{2,1,0:T(8,128)(2,1)S(1)}, f32[24,128]{1,0:T(8,128)S(1)}, f32[8,24,128]{2,1,0:T(8,128)S(1)}) custom-call(f32[8,3,17]{2,1,0:T(4,128)S(1)} %copy.5.taps), custom_call_target="tpu_custom_call" | custom-call | flops 100000000 | bytes 1024 | tf_op jit(solution)/shard_map/pallas_call | solution.py:450
  27.5 2.6 %shard_map.50 = (bf16[128,128]{1,0:T(8,128)(2,1)S(1)}, f32[64,128]{1,0:T(8,128)S(1)}, bf16[8,256,256]{2,1,0:T(8,128)(2,1)S(1)}, bf16[8,256,256]{2,1,0:T(8,128)(2,1)S(1)}) custom-call(f32[8,3,17]{2,1,0:T(4,128)S(1)} %copy.5.taps), custom_call_target="tpu_custom_call" | custom-call | flops 100000000 | bytes 1024 | tf_op jit(solution)/shard_map/pallas_call | solution.py:443
  30.1 0.0 collective-permute-done.6.i1
  30.1 0.0 collective-permute-done.7.i2
  30.1 0.0 collective-permute-done.4.z1
  30.2 0.0 collective-permute-done.5.z2
  30.2 0.0 copy-done.3
  30.2 7.6 %shard_map.52 = (f32[16,32,128]{2,1,0:T(8,128)S(1)}, f32[256,128]{1,0:T(8,128)S(1)}, f32[256,128]{1,0:T(8,128)S(1)}, f32[128,4,128]{2,1,0:T(4,128)}) custom-call(f32[32,32,128]{2,1,0:T(8,128)S(1)} %get-tuple-element.42.field, f32[16,128]{1,0:T(8,128)S(1)} %get-tuple-element.41.w9, f32[16,1024]{1,0:T(8,128)S(1)} %collective-permute-done.4.z1, ...), custom_call_target="tpu_custom_call" | custom-call | flops 2000000000 | bytes 1024 | tf_op jit(solution)/shard_map/pallas_call | solution.py:469
  37.8 7.3 %all-to-all-start = ((f32[128,4,128]{2,1,0:T(4,128)}), f32[128,4,128]{2,1,0:T(4,128)S(1)}, u32[]{:S(2)}, u32[]{:S(2)}) async-start(f32[128,4,128]{2,1,0:T(4,128)} %get-tuple-element.62), calls=%async_computation | async-start | bytes 524288 | tf_op jit(solution)/shard_map/all_to_all | solution.py:491
  45.1 0.5 collective-permute-start.8
  45.6 4.2 %collective-permute-start.9 = (f32[256,128]{1,0:T(8,128)S(1)}, f32[256,128]{1,0:T(8,128)S(1)}, u32[]{:S(2)}, u32[]{:S(2)}) collective-permute-start(f32[256,128]{1,0:T(8,128)S(1)} %get-tuple-element.58), channel_id=1, source_target_pairs={{32,64},{64,32},{33,65},{65,33},{34,66},{66,34},{35,67},{67,35},{3... | collective-permute-start | bytes 393224 | tf_op jit(solution)/shard_map/ppermute | solution.py:27
  49.8 0.0 collective-permute-done.8.r1
  49.8 4.6 %collective-permute-done.9.r2 = f32[256,128]{1,0:T(8,128)S(1)} collective-permute-done((f32[256,128]{1,0:T(8,128)S(1)}, f32[256,128]{1,0:T(8,128)S(1)}, u32[]{:S(2)}, u32[]{:S(2)}) %collective-permute-start.9) | collective-permute-done | bytes 131104 | tf_op jit(solution)/shard_map/ppermute | solution.py:27
  54.4 0.0 copy-start.1
  54.5 0.8 %collective-permute-start.10 = (f32[128,128]{1,0:T(8,128)S(1)}, f32[128,128]{1,0:T(8,128)S(1)}, u32[]{:S(2)}, u32[]{:S(2)}) collective-permute-start(f32[128,128]{1,0:T(8,128)S(1)} %get-tuple-element.60), channel_id=1, source_target_pairs={{0,4},{4,0},{8,12},{12,8},{16,20},{20,16},{24,28},{28,24},{1,5},{5... | collective-permute-start | bytes 196616 | tf_op jit(solution)/shard_map/ppermute | solution.py:27
  55.2 3.5 %collective-permute-start.11 = (f32[128,128]{1,0:T(8,128)S(1)}, f32[128,128]{1,0:T(8,128)S(1)}, u32[]{:S(2)}, u32[]{:S(2)}) collective-permute-start(f32[128,128]{1,0:T(8,128)S(1)} %get-tuple-element.61), channel_id=1, source_target_pairs={{4,8},{8,4},{12,16},{16,12},{20,24},{24,20},{5,9},{9,5},{13,17},{1... | collective-permute-start | bytes 196616 | tf_op jit(solution)/shard_map/ppermute | solution.py:27
  58.8 0.0 collective-permute-done.10.r1
  58.8 3.6 %collective-permute-done.11.r2 = f32[128,128]{1,0:T(8,128)S(1)} collective-permute-done((f32[128,128]{1,0:T(8,128)S(1)}, f32[128,128]{1,0:T(8,128)S(1)}, u32[]{:S(2)}, u32[]{:S(2)}) %collective-permute-start.11) | collective-permute-done | bytes 65568 | tf_op jit(solution)/shard_map/ppermute | solution.py:27
  62.4 0.0 all-to-all-done.sums
  62.4 0.0 copy-done.1
  62.4 0.9 %shard_map.54 = f32[16,16,128]{2,1,0:T(8,128)} custom-call(f32[16,128]{1,0:T(8,128)S(1)} %get-tuple-element.41.w9, f32[16,16,128]{2,1,0:T(8,128)S(1)} %get-tuple-element.59.part, f32[128,128]{1,0:T(8,128)S(1)} %collective-permute-done.10.r1, f32[128,128]{1,0:T(8,128)S(1)} %collective-permute-done.11.r2, f32[16,16,128]{2,1,0:T(8,128)S(1)} %copy-done.1, ...), custom_call_target="tpu_custom_call" | custom-call | bytes 1024 | tf_op jit(solution)/shard_map/pallas_call | solution.py:497
  (3 shorter events, 0.1 us)
Async XLA Ops:
  0.0 0.7 %copy-start.4 = (s32[8,1,1,1]{0,3,2,1:T(1,128)S(1)}, s32[8,1,1,1]{0,3,2,1:T(1,128)}, u32[]{:S(2)}) copy-start(s32[8,1,1,1]{0,3,2,1:T(1,128)} %param.6) | copy-start | bytes 100
  0.7 0.9 %copy-start = (f32[16,16,128]{2,1,0:T(8,128)S(1)}, f32[16,16,128]{2,1,0:T(8,128)}, u32[]{:S(2)}) copy-start(f32[16,16,128]{2,1,0:T(8,128)} %est.3) | copy-start | bytes 393220
  2.3 4.6 %collective-permute-start = (f32[136,128]{1,0:T(8,128)S(1)}, f32[136,128]{1,0:T(8,128)S(1)}, u32[]{:S(2)}, u32[]{:S(2)}) collective-permute-start(f32[136,128]{1,0:T(8,128)S(1)} %get-tuple-element.35), channel_id=1, source_target_pairs={{0,4},{4,0},{8,12},{12,8},{16,20},{20,16},{24,28},{28,24},{1,5},{5... | collective-permute-start | bytes 208904 | tf_op jit(solution)/shard_map/ppermute | solution.py:27
  3.6 7.2 %collective-permute-start.1 = (f32[136,128]{1,0:T(8,128)S(1)}, f32[136,128]{1,0:T(8,128)S(1)}, u32[]{:S(2)}, u32[]{:S(2)}) collective-permute-start(f32[136,128]{1,0:T(8,128)S(1)} %get-tuple-element.36), channel_id=1, source_target_pairs={{4,8},{8,4},{12,16},{16,12},{20,24},{24,20},{5,9},{9,5},{13,17},{1... | collective-permute-start | bytes 208904 | tf_op jit(solution)/shard_map/ppermute | solution.py:27
  10.8 12.6 %collective-permute-start.2 = (f32[264,128]{1,0:T(8,128)S(1)}, f32[264,128]{1,0:T(8,128)S(1)}, u32[]{:S(2)}, u32[]{:S(2)}) collective-permute-start(f32[264,128]{1,0:T(8,128)S(1)} %get-tuple-element.39), channel_id=1, source_target_pairs={{0,32},{32,0},{64,96},{96,64},{1,33},{33,1},{65,97},{97,65},{2,34}... | collective-permute-start | bytes 405512 | tf_op jit(solution)/shard_map/ppermute | solution.py:27
  13.0 10.5 %collective-permute-start.3 = (f32[264,128]{1,0:T(8,128)S(1)}, f32[264,128]{1,0:T(8,128)S(1)}, u32[]{:S(2)}, u32[]{:S(2)}) collective-permute-start(f32[264,128]{1,0:T(8,128)S(1)} %get-tuple-element.40), channel_id=1, source_target_pairs={{32,64},{64,32},{33,65},{65,33},{34,66},{66,34},{35,67},{67,35},{3... | collective-permute-start | bytes 405512 | tf_op jit(solution)/shard_map/ppermute | solution.py:27
  17.6 1.2 %copy-start.2 = (f32[8,16,16,128]{3,2,1,0:T(8,128)S(1)}, f32[8,16,16,128]{3,2,1,0:T(8,128)}, u32[]{:S(2)}) copy-start(f32[8,16,16,128]{3,2,1,0:T(8,128)} %observed.3) | copy-start | bytes 3145732
  18.8 11.4 %copy-start.3 = (f32[8,16,16,128]{3,2,1,0:T(8,128)S(1)}, f32[8,16,16,128]{3,2,1,0:T(8,128)}, u32[]{:S(2)}) copy-start(f32[8,16,16,128]{3,2,1,0:T(8,128)} %observed.3) | copy-start | bytes 3145732
  19.1 11.0 %collective-permute-start.6 = (f32[64,256]{1,0:T(8,128)S(1)}, f32[64,256]{1,0:T(8,128)S(1)}, u32[]{:S(2)}, u32[]{:S(2)}) collective-permute-start(f32[64,256]{1,0:T(8,128)S(1)} %get-tuple-element.45), channel_id=1, source_target_pairs={{0,1},{1,0},{2,3},{3,2},{4,5},{5,4},{6,7},{7,6},{8,9},{9,8},{10,11... | collective-permute-start | bytes 196616 | tf_op jit(solution)/shard_map/ppermute | solution.py:27
  19.4 10.8 %collective-permute-start.7 = (f32[64,256]{1,0:T(8,128)S(1)}, f32[64,256]{1,0:T(8,128)S(1)}, u32[]{:S(2)}, u32[]{:S(2)}) collective-permute-start(f32[64,256]{1,0:T(8,128)S(1)} %get-tuple-element.46), channel_id=1, source_target_pairs={{1,2},{2,1},{5,6},{6,5},{9,10},{10,9},{13,14},{14,13},{17,18},{18,... | collective-permute-start | bytes 196616 | tf_op jit(solution)/shard_map/ppermute | solution.py:27
  23.4 2.3 %copy-start.5 = (f32[8,3,17]{2,0,1:T(8,128)S(1)}, f32[8,3,17]{2,0,1:T(8,128)}, u32[]{:S(2)}) copy-start(f32[8,3,17]{2,0,1:T(8,128)} %param.7) | copy-start | bytes 4900
  23.7 6.5 %collective-permute-start.4 = (f32[16,1024]{1,0:T(8,128)S(1)}, f32[16,1024]{1,0:T(8,128)S(1)}, u32[]{:S(2)}, u32[]{:S(2)}) collective-permute-start(f32[16,1024]{1,0:T(8,128)S(1)} %get-tuple-element.43), channel_id=1, source_target_pairs={{0,1},{1,0},{2,3},{3,2},{4,5},{5,4},{6,7},{7,6},{8,9},{9,8},{10,11... | collective-permute-start | bytes 196616 | tf_op jit(solution)/shard_map/ppermute | solution.py:27
  23.8 6.4 %collective-permute-start.5 = (f32[16,1024]{1,0:T(8,128)S(1)}, f32[16,1024]{1,0:T(8,128)S(1)}, u32[]{:S(2)}, u32[]{:S(2)}) collective-permute-start(f32[16,1024]{1,0:T(8,128)S(1)} %get-tuple-element.44), channel_id=1, source_target_pairs={{1,2},{2,1},{5,6},{6,5},{9,10},{10,9},{13,14},{14,13},{17,18},{18,... | collective-permute-start | bytes 196616 | tf_op jit(solution)/shard_map/ppermute | solution.py:27
  37.8 24.6 %all-to-all-start = ((f32[128,4,128]{2,1,0:T(4,128)}), f32[128,4,128]{2,1,0:T(4,128)S(1)}, u32[]{:S(2)}, u32[]{:S(2)}) async-start(f32[128,4,128]{2,1,0:T(4,128)} %get-tuple-element.62), calls=%async_computation | async-start | bytes 524288 | tf_op jit(solution)/shard_map/all_to_all | solution.py:491
  45.1 4.7 %collective-permute-start.8 = (f32[256,128]{1,0:T(8,128)S(1)}, f32[256,128]{1,0:T(8,128)S(1)}, u32[]{:S(2)}, u32[]{:S(2)}) collective-permute-start(f32[256,128]{1,0:T(8,128)S(1)} %get-tuple-element.57), channel_id=1, source_target_pairs={{0,32},{32,0},{64,96},{96,64},{1,33},{33,1},{65,97},{97,65},{2,34}... | collective-permute-start | bytes 393224 | tf_op jit(solution)/shard_map/ppermute | solution.py:27
  45.6 8.8 %collective-permute-start.9 = (f32[256,128]{1,0:T(8,128)S(1)}, f32[256,128]{1,0:T(8,128)S(1)}, u32[]{:S(2)}, u32[]{:S(2)}) collective-permute-start(f32[256,128]{1,0:T(8,128)S(1)} %get-tuple-element.58), channel_id=1, source_target_pairs={{32,64},{64,32},{33,65},{65,33},{34,66},{66,34},{35,67},{67,35},{3... | collective-permute-start | bytes 393224 | tf_op jit(solution)/shard_map/ppermute | solution.py:27
  54.4 7.9 %copy-start.1 = (f32[16,16,128]{2,1,0:T(8,128)S(1)}, f32[16,16,128]{2,1,0:T(8,128)}, u32[]{:S(2)}) copy-start(f32[16,16,128]{2,1,0:T(8,128)} %est.3) | copy-start | bytes 393220
  54.5 4.3 %collective-permute-start.10 = (f32[128,128]{1,0:T(8,128)S(1)}, f32[128,128]{1,0:T(8,128)S(1)}, u32[]{:S(2)}, u32[]{:S(2)}) collective-permute-start(f32[128,128]{1,0:T(8,128)S(1)} %get-tuple-element.60), channel_id=1, source_target_pairs={{0,4},{4,0},{8,12},{12,8},{16,20},{20,16},{24,28},{28,24},{1,5},{5... | collective-permute-start | bytes 196616 | tf_op jit(solution)/shard_map/ppermute | solution.py:27
  55.2 7.1 %collective-permute-start.11 = (f32[128,128]{1,0:T(8,128)S(1)}, f32[128,128]{1,0:T(8,128)S(1)}, u32[]{:S(2)}, u32[]{:S(2)}) collective-permute-start(f32[128,128]{1,0:T(8,128)S(1)} %get-tuple-element.61), channel_id=1, source_target_pairs={{4,8},{8,4},{12,16},{16,12},{20,24},{24,20},{5,9},{9,5},{13,17},{1... | collective-permute-start | bytes 196616 | tf_op jit(solution)/shard_map/ppermute | solution.py:27

commit v7 on v6

--- a/solution.py
+++ b/solution.py
@@ -24,7 +24,9 @@
 
 def swap(one, two, axis):
     count = lax.axis_size(axis)
-    return lax.ppermute(one, axis, pairs(count, 0)), lax.ppermute(two, axis, pairs(count, 1))
+    one = lax.ppermute(one, axis, pairs(count, 0))
+    two = lax.ppermute(two, axis, pairs(count, 1))
+    return one, two
 
 
 def kernel_call(body, out_shape, scratch=(), in_smem=0, flops=0, n_in=0, in_hbm=0, mib=8):
@@ -432,7 +434,7 @@
         ),
         n_in=2,
         in_hbm=2,
-        mib=40,
+        mib=60,
     )(cover, estimate)
     y1, y2 = swap(y1, y2, "by")
     op = shape(V * R, CX * CY)

time: 64 us -> 65 us (1.016)
  Pallas kernels: 14.3 us -> 15.1 us
    pallas_call x1, Pallas kernels: 0.72 us -> 1.68 us  [on_device(): kernel_call(y_pack, (op, op, shape(V + 8, LANES)), scratch=(pltpu.SMEM((V...]
where the time goes in v7:
time: 65 us; the launch traced here: 64.2 us
  starting transfers between devices  33.9 us (52%)
  Pallas kernels  15.1 us (23%)
  waiting for transfers between devices  12.3 us (19%)
  local copies, waits for them, and re-layouts  2.62 us (4%)
    ppermute x6, starting transfers between devices, swap(): two = lax.ppermute(two, axis, pairs(count, 1))  21.5 us
    ppermute x6, waiting for transfers between devices, swap(): two = lax.ppermute(two, axis, pairs(count, 1))  12.2 us
    pallas_call x1, Pallas kernels, on_device(): kernel_call(main_kernel, (shape(CX, EY, LANES), op, op, shape(peers, 4, L...  7.53 us
    all_to_all x1, starting transfers between devices, on_device(): sums = lax.all_to_all(sums, ALL, 0, 0)  7.32 us
    ppermute x6, starting transfers between devices, swap(): one = lax.ppermute(one, axis, pairs(count, 0))  5.06 us
    pallas_call x1, Pallas kernels, on_device(): kernel_call(bands, (shape(V * CY, LANES, dtype=BF16), shape(2 * EY, LANES...  2.64 us
    unnamed x13, local copies, waits for them, and re-layouts  2.62 us
    pallas_call x1, Pallas kernels, on_device(): kernel_call(bands_back, (square, square, square, shape(24, LANES), shape(...  1.75 us
  transfers between devices with their start and end apart: 13, of which 3 were waited for; matrix products, arithmetic and copies ran while one was open for 0% of the time, Pallas kernels for 8%

profile of v7, /device:TPU:41, one launch (start us, length us, event | category | flops | bytes accessed | tf_op | source)
XLA Modules:
  0.0 64.2 jit_solution(17308597860471997469)
XLA Ops:
  0.0 0.0 copy-start
  0.0 1.7 %shard_map.46 = (f32[136,128]{1,0:T(8,128)}, f32[136,128]{1,0:T(8,128)}, f32[16,128]{1,0:T(8,128)}) custom-call(s32[8]{0:T(128)} %bitcast.1, f32[16,16,128]{2,1,0:T(8,128)} %est.3), custom_call_target="tpu_custom_call" | custom-call | bytes 1024 | tf_op jit(solution)/shard_map/pallas_call | solution.py:427
  1.7 1.3 %collective-permute-start = (f32[136,128]{1,0:T(8,128)}, f32[136,128]{1,0:T(8,128)S(1)}, u32[]{:S(2)}, u32[]{:S(2)}) collective-permute-start(f32[136,128]{1,0:T(8,128)} %get-tuple-element.35), channel_id=1, source_target_pairs={{0,4},{4,0},{8,12},{12,8},{16,20},{20,16},{24,28},{28,24},{1,5},{5... | collective-permute-start | bytes 208904 | tf_op jit(solution)/shard_map/ppermute | solution.py:27
  3.0 3.3 %collective-permute-start.1 = (f32[136,128]{1,0:T(8,128)}, f32[136,128]{1,0:T(8,128)S(1)}, u32[]{:S(2)}, u32[]{:S(2)}) collective-permute-start(f32[136,128]{1,0:T(8,128)} %get-tuple-element.36), channel_id=1, source_target_pairs={{4,8},{8,4},{12,16},{16,12},{20,24},{24,20},{5,9},{9,5},{13,17},{1... | collective-permute-start | bytes 208904 | tf_op jit(solution)/shard_map/ppermute | solution.py:28
  6.2 0.0 collective-permute-done.y1
  6.3 4.1 %collective-permute-done.1.y2 = f32[136,128]{1,0:T(8,128)S(1)} collective-permute-done((f32[136,128]{1,0:T(8,128)}, f32[136,128]{1,0:T(8,128)S(1)}, u32[]{:S(2)}, u32[]{:S(2)}) %collective-permute-start.1) | collective-permute-done | bytes 69664 | tf_op jit(solution)/shard_map/ppermute | solution.py:28
  10.3 0.0 copy-done
  10.3 0.0 copy-start.3
  10.3 0.7 %copy-done.3 = f32[16,128]{1,0:T(8,128)S(1)} copy-done((f32[16,128]{1,0:T(8,128)S(1)}, f32[16,128]{1,0:T(8,128)}, u32[]{:S(2)}) %copy-start.3) | copy-done | bytes 8216
  11.1 2.2 %collective-permute-start.2 = (f32[264,128]{1,0:T(8,128)S(1)}, f32[264,128]{1,0:T(8,128)S(1)}, u32[]{:S(2)}, u32[]{:S(2)}) collective-permute-start(f32[264,128]{1,0:T(8,128)S(1)} %get-tuple-element.39), channel_id=1, source_target_pairs={{0,32},{32,0},{64,96},{96,64},{1,33},{33,1},{65,97},{97,65},{2,34}... | collective-permute-start | bytes 405512 | tf_op jit(solution)/shard_map/ppermute | solution.py:27
  13.3 4.6 %collective-permute-start.3 = (f32[264,128]{1,0:T(8,128)S(1)}, f32[264,128]{1,0:T(8,128)S(1)}, u32[]{:S(2)}, u32[]{:S(2)}) collective-permute-start(f32[264,128]{1,0:T(8,128)S(1)} %get-tuple-element.40), channel_id=1, source_target_pairs={{32,64},{64,32},{33,65},{65,33},{34,66},{66,34},{35,67},{67,35},{3... | collective-permute-start | bytes 405512 | tf_op jit(solution)/shard_map/ppermute | solution.py:28
  17.9 0.0 copy-start.1
  17.9 1.2 %copy-done.1 = f32[8,16,16,128]{3,2,1,0:T(8,128)S(1)} copy-done((f32[8,16,16,128]{3,2,1,0:T(8,128)S(1)}, f32[8,16,16,128]{3,2,1,0:T(8,128)}, u32[]{:S(2)}) %copy-start.1) | copy-done | bytes 1048600
  19.1 0.0 copy-start.2
  19.1 0.3 shard_map.49
  19.5 0.2 collective-permute-start.6
  19.7 4.0 %collective-permute-start.7 = (f32[64,256]{1,0:T(8,128)S(1)}, f32[64,256]{1,0:T(8,128)S(1)}, u32[]{:S(2)}, u32[]{:S(2)}) collective-permute-start(f32[64,256]{1,0:T(8,128)S(1)} %get-tuple-element.46), channel_id=1, source_target_pairs={{1,2},{2,1},{5,6},{6,5},{9,10},{10,9},{13,14},{14,13},{17,18},{18,... | collective-permute-start | bytes 196616 | tf_op jit(solution)/shard_map/ppermute | solution.py:28
  23.7 0.0 collective-permute-done.2.x1
  23.8 0.0 collective-permute-done.3.x2
  23.8 0.0 copy-start.5
  23.8 0.2 shard_map.48
  24.0 0.1 collective-permute-start.4
  24.1 1.9 %collective-permute-start.5 = (f32[16,1024]{1,0:T(8,128)S(1)}, f32[16,1024]{1,0:T(8,128)S(1)}, u32[]{:S(2)}, u32[]{:S(2)}) collective-permute-start(f32[16,1024]{1,0:T(8,128)S(1)} %get-tuple-element.44), channel_id=1, source_target_pairs={{1,2},{2,1},{5,6},{6,5},{9,10},{10,9},{13,14},{14,13},{17,18},{18,... | collective-permute-start | bytes 196616 | tf_op jit(solution)/shard_map/ppermute | solution.py:28
  26.0 0.0 copy-done.5
  26.1 1.8 %shard_map.51 = (bf16[8,256,128]{2,1,0:T(8,128)(2,1)S(1)}, bf16[8,256,128]{2,1,0:T(8,128)(2,1)S(1)}, bf16[8,256,128]{2,1,0:T(8,128)(2,1)S(1)}, f32[24,128]{1,0:T(8,128)S(1)}, f32[8,24,128]{2,1,0:T(8,128)S(1)}) custom-call(f32[8,3,17]{2,1,0:T(4,128)S(1)} %copy.5.taps), custom_call_target="tpu_custom_call" | custom-call | flops 100000000 | bytes 1024 | tf_op jit(solution)/shard_map/pallas_call | solution.py:452
  27.8 2.6 %shard_map.50 = (bf16[128,128]{1,0:T(8,128)(2,1)S(1)}, f32[64,128]{1,0:T(8,128)S(1)}, bf16[8,256,256]{2,1,0:T(8,128)(2,1)S(1)}, bf16[8,256,256]{2,1,0:T(8,128)(2,1)S(1)}) custom-call(f32[8,3,17]{2,1,0:T(4,128)S(1)} %copy.5.taps), custom_call_target="tpu_custom_call" | custom-call | flops 100000000 | bytes 1024 | tf_op jit(solution)/shard_map/pallas_call | solution.py:445
  30.5 0.0 collective-permute-done.6.i1
  30.5 0.0 collective-permute-done.7.i2
  30.5 0.0 collective-permute-done.4.z1
  30.5 0.0 collective-permute-done.5.z2
  30.5 0.0 copy-start.4
  30.5 0.0 copy-done.2
  30.5 0.7 %copy-done.4 = f32[16,128]{1,0:T(8,128)S(1)} copy-done((f32[16,128]{1,0:T(8,128)S(1)}, f32[16,128]{1,0:T(8,128)}, u32[]{:S(2)}) %copy-start.4) | copy-done | bytes 8216
  31.2 7.5 %shard_map.52 = (f32[16,32,128]{2,1,0:T(8,128)S(1)}, f32[256,128]{1,0:T(8,128)S(1)}, f32[256,128]{1,0:T(8,128)S(1)}, f32[128,4,128]{2,1,0:T(4,128)}) custom-call(f32[32,32,128]{2,1,0:T(8,128)S(1)} %get-tuple-element.42.field, f32[16,128]{1,0:T(8,128)S(1)} %get-tuple-element.41.w9, f32[16,1024]{1,0:T(8,128)S(1)} %collective-permute-done.4.z1, ...), custom_call_target="tpu_custom_call" | custom-call | flops 2000000000 | bytes 1024 | tf_op jit(solution)/shard_map/pallas_call | solution.py:471
  38.7 7.3 %all-to-all-start = ((f32[128,4,128]{2,1,0:T(4,128)}), f32[128,4,128]{2,1,0:T(4,128)S(1)}, u32[]{:S(2)}, u32[]{:S(2)}) async-start(f32[128,4,128]{2,1,0:T(4,128)} %get-tuple-element.62), calls=%async_computation | async-start | bytes 524288 | tf_op jit(solution)/shard_map/all_to_all | solution.py:493
  46.0 0.5 collective-permute-start.8
  46.5 4.2 %collective-permute-start.9 = (f32[256,128]{1,0:T(8,128)S(1)}, f32[256,128]{1,0:T(8,128)S(1)}, u32[]{:S(2)}, u32[]{:S(2)}) collective-permute-start(f32[256,128]{1,0:T(8,128)S(1)} %get-tuple-element.58), channel_id=1, source_target_pairs={{32,64},{64,32},{33,65},{65,33},{34,66},{66,34},{35,67},{67,35},{3... | collective-permute-start | bytes 393224 | tf_op jit(solution)/shard_map/ppermute | solution.py:28
  50.8 0.0 collective-permute-done.8.r1
  50.8 4.6 %collective-permute-done.9.r2 = f32[256,128]{1,0:T(8,128)S(1)} collective-permute-done((f32[256,128]{1,0:T(8,128)S(1)}, f32[256,128]{1,0:T(8,128)S(1)}, u32[]{:S(2)}, u32[]{:S(2)}) %collective-permute-start.9) | collective-permute-done | bytes 131104 | tf_op jit(solution)/shard_map/ppermute | solution.py:28
  55.4 0.8 %collective-permute-start.10 = (f32[128,128]{1,0:T(8,128)S(1)}, f32[128,128]{1,0:T(8,128)S(1)}, u32[]{:S(2)}, u32[]{:S(2)}) collective-permute-start(f32[128,128]{1,0:T(8,128)S(1)} %get-tuple-element.60), channel_id=1, source_target_pairs={{0,4},{4,0},{8,12},{12,8},{16,20},{20,16},{24,28},{28,24},{1,5},{5... | collective-permute-start | bytes 196616 | tf_op jit(solution)/shard_map/ppermute | solution.py:27
  56.2 3.5 %collective-permute-start.11 = (f32[128,128]{1,0:T(8,128)S(1)}, f32[128,128]{1,0:T(8,128)S(1)}, u32[]{:S(2)}, u32[]{:S(2)}) collective-permute-start(f32[128,128]{1,0:T(8,128)S(1)} %get-tuple-element.61), channel_id=1, source_target_pairs={{4,8},{8,4},{12,16},{16,12},{20,24},{24,20},{5,9},{9,5},{13,17},{1... | collective-permute-start | bytes 196616 | tf_op jit(solution)/shard_map/ppermute | solution.py:28
  59.7 0.0 collective-permute-done.10.r1
  59.7 3.6 %collective-permute-done.11.r2 = f32[128,128]{1,0:T(8,128)S(1)} collective-permute-done((f32[128,128]{1,0:T(8,128)S(1)}, f32[128,128]{1,0:T(8,128)S(1)}, u32[]{:S(2)}, u32[]{:S(2)}) %collective-permute-start.11) | collective-permute-done | bytes 65568 | tf_op jit(solution)/shard_map/ppermute | solution.py:28
  63.3 0.0 all-to-all-done.sums
  63.3 0.9 %shard_map.54 = f32[16,16,128]{2,1,0:T(8,128)} custom-call(f32[16,128]{1,0:T(8,128)S(1)} %get-tuple-element.41.w9, f32[16,16,128]{2,1,0:T(8,128)S(1)} %get-tuple-element.59.part, f32[128,128]{1,0:T(8,128)S(1)} %collective-permute-done.10.r1, f32[128,128]{1,0:T(8,128)S(1)} %collective-permute-done.11.r2, f32[16,16,128]{2,1,0:T(8,128)S(1)} %copy-done, ...), custom_call_target="tpu_custom_call" | custom-call | bytes 1024 | tf_op jit(solution)/shard_map/pallas_call | solution.py:499
  (3 shorter events, 0.1 us)
Async XLA Ops:
  0.0 10.3 %copy-start = (f32[16,16,128]{2,1,0:T(8,128)S(1)}, f32[16,16,128]{2,1,0:T(8,128)}, u32[]{:S(2)}) copy-start(f32[16,16,128]{2,1,0:T(8,128)} %est.3) | copy-start | bytes 393220
  1.7 4.6 %collective-permute-start = (f32[136,128]{1,0:T(8,128)}, f32[136,128]{1,0:T(8,128)S(1)}, u32[]{:S(2)}, u32[]{:S(2)}) collective-permute-start(f32[136,128]{1,0:T(8,128)} %get-tuple-element.35), channel_id=1, source_target_pairs={{0,4},{4,0},{8,12},{12,8},{16,20},{20,16},{24,28},{28,24},{1,5},{5... | collective-permute-start | bytes 208904 | tf_op jit(solution)/shard_map/ppermute | solution.py:27
  3.0 7.4 %collective-permute-start.1 = (f32[136,128]{1,0:T(8,128)}, f32[136,128]{1,0:T(8,128)S(1)}, u32[]{:S(2)}, u32[]{:S(2)}) collective-permute-start(f32[136,128]{1,0:T(8,128)} %get-tuple-element.36), channel_id=1, source_target_pairs={{4,8},{8,4},{12,16},{16,12},{20,24},{24,20},{5,9},{9,5},{13,17},{1... | collective-permute-start | bytes 208904 | tf_op jit(solution)/shard_map/ppermute | solution.py:28
  10.3 0.7 %copy-start.3 = (f32[16,128]{1,0:T(8,128)S(1)}, f32[16,128]{1,0:T(8,128)}, u32[]{:S(2)}) copy-start(f32[16,128]{1,0:T(8,128)} %get-tuple-element.34.w_own) | copy-start | bytes 24580
  11.1 12.7 %collective-permute-start.2 = (f32[264,128]{1,0:T(8,128)S(1)}, f32[264,128]{1,0:T(8,128)S(1)}, u32[]{:S(2)}, u32[]{:S(2)}) collective-permute-start(f32[264,128]{1,0:T(8,128)S(1)} %get-tuple-element.39), channel_id=1, source_target_pairs={{0,32},{32,0},{64,96},{96,64},{1,33},{33,1},{65,97},{97,65},{2,34}... | collective-permute-start | bytes 405512 | tf_op jit(solution)/shard_map/ppermute | solution.py:27
  13.3 10.5 %collective-permute-start.3 = (f32[264,128]{1,0:T(8,128)S(1)}, f32[264,128]{1,0:T(8,128)S(1)}, u32[]{:S(2)}, u32[]{:S(2)}) collective-permute-start(f32[264,128]{1,0:T(8,128)S(1)} %get-tuple-element.40), channel_id=1, source_target_pairs={{32,64},{64,32},{33,65},{65,33},{34,66},{66,34},{35,67},{67,35},{3... | collective-permute-start | bytes 405512 | tf_op jit(solution)/shard_map/ppermute | solution.py:28
  17.9 1.2 %copy-start.1 = (f32[8,16,16,128]{3,2,1,0:T(8,128)S(1)}, f32[8,16,16,128]{3,2,1,0:T(8,128)}, u32[]{:S(2)}) copy-start(f32[8,16,16,128]{3,2,1,0:T(8,128)} %observed.3) | copy-start | bytes 3145732
  19.1 11.4 %copy-start.2 = (f32[8,16,16,128]{3,2,1,0:T(8,128)S(1)}, f32[8,16,16,128]{3,2,1,0:T(8,128)}, u32[]{:S(2)}) copy-start(f32[8,16,16,128]{3,2,1,0:T(8,128)} %observed.3) | copy-start | bytes 3145732
  19.5 11.0 %collective-permute-start.6 = (f32[64,256]{1,0:T(8,128)S(1)}, f32[64,256]{1,0:T(8,128)S(1)}, u32[]{:S(2)}, u32[]{:S(2)}) collective-permute-start(f32[64,256]{1,0:T(8,128)S(1)} %get-tuple-element.45), channel_id=1, source_target_pairs={{0,1},{1,0},{2,3},{3,2},{4,5},{5,4},{6,7},{7,6},{8,9},{9,8},{10,11... | collective-permute-start | bytes 196616 | tf_op jit(solution)/shard_map/ppermute | solution.py:27
  19.7 10.8 %collective-permute-start.7 = (f32[64,256]{1,0:T(8,128)S(1)}, f32[64,256]{1,0:T(8,128)S(1)}, u32[]{:S(2)}, u32[]{:S(2)}) collective-permute-start(f32[64,256]{1,0:T(8,128)S(1)} %get-tuple-element.46), channel_id=1, source_target_pairs={{1,2},{2,1},{5,6},{6,5},{9,10},{10,9},{13,14},{14,13},{17,18},{18,... | collective-permute-start | bytes 196616 | tf_op jit(solution)/shard_map/ppermute | solution.py:28
  23.8 2.3 %copy-start.5 = (f32[8,3,17]{2,0,1:T(8,128)S(1)}, f32[8,3,17]{2,0,1:T(8,128)}, u32[]{:S(2)}) copy-start(f32[8,3,17]{2,0,1:T(8,128)} %param.7) | copy-start | bytes 4900
  24.0 6.5 %collective-permute-start.4 = (f32[16,1024]{1,0:T(8,128)S(1)}, f32[16,1024]{1,0:T(8,128)S(1)}, u32[]{:S(2)}, u32[]{:S(2)}) collective-permute-start(f32[16,1024]{1,0:T(8,128)S(1)} %get-tuple-element.43), channel_id=1, source_target_pairs={{0,1},{1,0},{2,3},{3,2},{4,5},{5,4},{6,7},{7,6},{8,9},{9,8},{10,11... | collective-permute-start | bytes 196616 | tf_op jit(solution)/shard_map/ppermute | solution.py:27
  24.1 6.4 %collective-permute-start.5 = (f32[16,1024]{1,0:T(8,128)S(1)}, f32[16,1024]{1,0:T(8,128)S(1)}, u32[]{:S(2)}, u32[]{:S(2)}) collective-permute-start(f32[16,1024]{1,0:T(8,128)S(1)} %get-tuple-element.44), channel_id=1, source_target_pairs={{1,2},{2,1},{5,6},{6,5},{9,10},{10,9},{13,14},{14,13},{17,18},{18,... | collective-permute-start | bytes 196616 | tf_op jit(solution)/shard_map/ppermute | solution.py:28
  30.5 0.7 %copy-start.4 = (f32[16,128]{1,0:T(8,128)S(1)}, f32[16,128]{1,0:T(8,128)}, u32[]{:S(2)}) copy-start(f32[16,128]{1,0:T(8,128)} %get-tuple-element.34.w_own) | copy-start | bytes 24580
  38.7 24.5 %all-to-all-start = ((f32[128,4,128]{2,1,0:T(4,128)}), f32[128,4,128]{2,1,0:T(4,128)S(1)}, u32[]{:S(2)}, u32[]{:S(2)}) async-start(f32[128,4,128]{2,1,0:T(4,128)} %get-tuple-element.62), calls=%async_computation | async-start | bytes 524288 | tf_op jit(solution)/shard_map/all_to_all | solution.py:493
  46.0 4.7 %collective-permute-start.8 = (f32[256,128]{1,0:T(8,128)S(1)}, f32[256,128]{1,0:T(8,128)S(1)}, u32[]{:S(2)}, u32[]{:S(2)}) collective-permute-start(f32[256,128]{1,0:T(8,128)S(1)} %get-tuple-element.57), channel_id=1, source_target_pairs={{0,32},{32,0},{64,96},{96,64},{1,33},{33,1},{65,97},{97,65},{2,34}... | collective-permute-start | bytes 393224 | tf_op jit(solution)/shard_map/ppermute | solution.py:27
  46.5 8.8 %collective-permute-start.9 = (f32[256,128]{1,0:T(8,128)S(1)}, f32[256,128]{1,0:T(8,128)S(1)}, u32[]{:S(2)}, u32[]{:S(2)}) collective-permute-start(f32[256,128]{1,0:T(8,128)S(1)} %get-tuple-element.58), channel_id=1, source_target_pairs={{32,64},{64,32},{33,65},{65,33},{34,66},{66,34},{35,67},{67,35},{3... | collective-permute-start | bytes 393224 | tf_op jit(solution)/shard_map/ppermute | solution.py:28
  55.4 4.3 %collective-permute-start.10 = (f32[128,128]{1,0:T(8,128)S(1)}, f32[128,128]{1,0:T(8,128)S(1)}, u32[]{:S(2)}, u32[]{:S(2)}) collective-permute-start(f32[128,128]{1,0:T(8,128)S(1)} %get-tuple-element.60), channel_id=1, source_target_pairs={{0,4},{4,0},{8,12},{12,8},{16,20},{20,16},{24,28},{28,24},{1,5},{5... | collective-permute-start | bytes 196616 | tf_op jit(solution)/shard_map/ppermute | solution.py:27
  56.2 7.1 %collective-permute-start.11 = (f32[128,128]{1,0:T(8,128)S(1)}, f32[128,128]{1,0:T(8,128)S(1)}, u32[]{:S(2)}, u32[]{:S(2)}) collective-permute-start(f32[128,128]{1,0:T(8,128)S(1)} %get-tuple-element.61), channel_id=1, source_target_pairs={{4,8},{8,4},{12,16},{16,12},{20,24},{24,20},{5,9},{9,5},{13,17},{1... | collective-permute-start | bytes 196616 | tf_op jit(solution)/shard_map/ppermute | solution.py:28
